TPU v7x, 32 devices: a whole 2x2x4 slice. The times are simulated.
32 devices in a mesh: dp: 8 (over z, core), fsdp: 4 (over y, x).
Axes of the slice: x: 2, y: 2, z: 4, core: 2. Of those that a mesh axis runs over, the one named last changes fastest.
Arguments:
- tokens: bfloat16 [32, 512, 1024], P(('dp', 'fsdp')), may hold values from -6 to 6
- images: bfloat16 [64, 588, 1024], P(('dp', 'fsdp')), may hold values from -6 to 6
- segment_ids: int32 [32, 512], P(('dp', 'fsdp')), may hold values from 0 to 3, never falling along the last dimension, each value on 1 to 256 neighbouring positions
- image_map: int32 [32, 4], P(('dp', 'fsdp')), may hold values from 0 to 1
- out_grad: bfloat16 [32, 512, 1024], P(('dp', 'fsdp')), may hold values from -6 to 6
- norm_self: bfloat16 [1024], P(('dp', 'fsdp')), may hold values from 0.5 to 1.5
- attn_query: bfloat16 [1024, 1024], P(('dp', 'fsdp')), may hold values from -0.1875 to 0.1875
- attn_key: bfloat16 [1024, 1024], P(('dp', 'fsdp')), may hold values from -0.1875 to 0.1875
- attn_value: bfloat16 [1024, 1024], P(('dp', 'fsdp')), may hold values from -0.1875 to 0.1875
- attn_out: bfloat16 [1024, 1024], P(('dp', 'fsdp')), may hold values from -0.75 to 0.75
- norm_cross: bfloat16 [1024], P(('dp', 'fsdp')), may hold values from 0.5 to 1.5
- cross_query: bfloat16 [1024, 1024], P(('dp', 'fsdp')), may hold values from -0.1875 to 0.1875
- cross_key: bfloat16 [1024, 1024], P(('dp', 'fsdp')), may hold values from -0.1875 to 0.1875
- cross_value: bfloat16 [1024, 1024], P(('dp', 'fsdp')), may hold values from -0.1875 to 0.1875
- cross_out: bfloat16 [1024, 1024], P(('dp', 'fsdp')), may hold values from -0.75 to 0.75
- norm_ffn: bfloat16 [1024], P(('dp', 'fsdp')), may hold values from 0.5 to 1.5
- ffn_up: bfloat16 [1024, 4096], P(('dp', 'fsdp')), may hold values from -0.1875 to 0.1875
- ffn_down: bfloat16 [4096, 1024], P(('dp', 'fsdp')), may hold values from -0.09375 to 0.09375
Outputs:
- output: bfloat16 [32, 512, 1024], P(('dp', 'fsdp'))
- grad_tokens: bfloat16 [32, 512, 1024], P(('dp', 'fsdp'))
- grad_images: bfloat16 [64, 588, 1024], P(('dp', 'fsdp'))
- grad_norm_self: float32 [1024], P(('dp', 'fsdp'))
- grad_attn_query: float32 [1024, 1024], P(('dp', 'fsdp'))
- grad_attn_key: float32 [1024, 1024], P(('dp', 'fsdp'))
- grad_attn_value: float32 [1024, 1024], P(('dp', 'fsdp'))
- grad_attn_out: float32 [1024, 1024], P(('dp', 'fsdp'))
- grad_norm_cross: float32 [1024], P(('dp', 'fsdp'))
- grad_cross_query: float32 [1024, 1024], P(('dp', 'fsdp'))
- grad_cross_key: float32 [1024, 1024], P(('dp', 'fsdp'))
- grad_cross_value: float32 [1024, 1024], P(('dp', 'fsdp'))
- grad_cross_out: float32 [1024, 1024], P(('dp', 'fsdp'))
- grad_norm_ffn: float32 [1024], P(('dp', 'fsdp'))
- grad_ffn_up: float32 [1024, 4096], P(('dp', 'fsdp'))
- grad_ffn_down: float32 [4096, 1024], P(('dp', 'fsdp'))
Inputs may be any that keep to these rules, and one draw needn't show every extreme that they name: `segment_ids`: Non-decreasing along each row; each of a row's 4 pages holds 1 to 256 tokens, one exactly 256. `image_map`: A local index among the row's own images.
All inputs are finite; a program needn't handle non-finite values.
Results may differ from a plain program's by a relative error of at most 0.02.
Values may be sent and summed in bfloat16 or wider, within the bound.
A program may use at most 256 MiB of HBM per device.

v0:
```python
import functools

import jax
import jax.numpy as jnp
from jax import lax
from jax.experimental import pallas as pl
from jax.experimental.pallas import tpu as pltpu
from jax.sharding import PartitionSpec as P


AXES = ("dp", "fsdp")
LOG2E = 1.4426950408889634
EPSILON = 1e-05
MASKED = -1e30
TILE = 128
PAGE_MAX = 256
VMEM = 62 * 1024 * 1024

bf16 = jnp.bfloat16
f32 = jnp.float32


def product(left, right):
    return jnp.dot(left, right, preferred_element_type=f32)


def product_t(left, right):
    return lax.dot_general(left, right, (((1,), (1,)), ((), ())), preferred_element_type=f32)


def product_rows(left, right):
    return lax.dot_general(left, right, (((0,), (0,)), ((), ())), preferred_element_type=f32)


def normed(values, gain):
    centred = values - jnp.mean(values, axis=-1, keepdims=True)
    variance = jnp.mean(centred * centred, axis=-1, keepdims=True)
    inverse = lax.rsqrt(variance + EPSILON)
    unit = centred * inverse
    return unit * gain, unit, inverse


def norm_back(unit, inverse, gain, gradient):
    scaled = gradient * gain
    mean_scaled = jnp.mean(scaled, axis=-1, keepdims=True)
    mean_along = jnp.mean(scaled * unit, axis=-1, keepdims=True)
    return inverse * (scaled - mean_scaled - unit * mean_along), jnp.sum(gradient * unit, axis=0)


def params(count):
    return pltpu.CompilerParams(
        dimension_semantics=("arbitrary",) * count, vmem_limit_bytes=VMEM
    )


def cost(microseconds):
    return pl.CostEstimate(flops=int(microseconds * 1e9), bytes_accessed=0, transcendentals=0)


def two_heads(block):
    lane = lax.broadcasted_iota(jnp.int32, block.shape, 1)
    zero = jnp.zeros_like(block)
    half = block.shape[1] // 2
    return jnp.concatenate(
        [jnp.where(lane < half, block, zero), jnp.where(lane >= half, block, zero)], axis=0
    )


def join_heads(both):
    rows = both.shape[1] // 2
    feature = lax.broadcasted_iota(jnp.int32, (both.shape[0], rows), 0)
    return jnp.where(feature < both.shape[0] // 2, both[:, :rows], both[:, rows:]).T


def twice(row):
    return jnp.concatenate([row, row], axis=1)


def key_range(tile):
    return max(0, tile * TILE - PAGE_MAX), (tile + 1) * TILE


def fill_bias(page_column, page_row, bias, tiles):
    for tile in range(tiles):
        low, high = key_range(tile)
        keys = low + lax.broadcasted_iota(jnp.int32, (high - low, TILE), 0)
        queries = tile * TILE + lax.broadcasted_iota(jnp.int32, (high - low, TILE), 1)
        same = page_column[low:high, :] == page_row[:, tile * TILE : (tile + 1) * TILE]
        bias[tile, : high - low, :] = jnp.where((keys <= queries) & same, 0.0, MASKED)


def self_forward_kernel(page_column, page_row, q, k, v, out, totals, bias):
    tiles = q.shape[0] // TILE
    scale = LOG2E * (q.shape[1] // 2) ** (-0.5)

    @pl.when(pl.program_id(0) == 0)
    def _():
        fill_bias(page_column, page_row, bias, tiles)

    for tile in range(tiles):
        low, high = key_range(tile)
        here = slice(tile * TILE, (tile + 1) * TILE)
        scores = product_t(k[low:high, :], two_heads(q[here, :])) * scale + twice(
            bias[tile, : high - low, :]
        )
        highest = jnp.max(scores, axis=0, keepdims=True)
        weights = jnp.exp2(scores - highest)
        total = jnp.sum(weights, axis=0, keepdims=True)
        mixed = product_rows(v[low:high, :], weights.astype(bf16)) * (1.0 / total)
        out[here, :] = join_heads(mixed).astype(bf16)
        level = highest + jnp.log2(total)
        totals[0, 0:1, here] = level[:, :TILE]
        totals[0, 1:2, here] = level[:, TILE:]


def self_forward(pages, qkv):
    rows, width = qkv.shape[0], qkv.shape[1] // 3
    pairs = width // 128
    return pl.pallas_call(
        self_forward_kernel,
        grid=(pairs,),
        in_specs=[
            pl.BlockSpec((rows, 1), lambda j: (0, 0)),
            pl.BlockSpec((1, rows), lambda j: (0, 0)),
            pl.BlockSpec((rows, 128), lambda j: (0, j)),
            pl.BlockSpec((rows, 128), lambda j: (0, pairs + j)),
            pl.BlockSpec((rows, 128), lambda j: (0, 2 * pairs + j)),
        ],
        out_specs=[
            pl.BlockSpec((rows, 128), lambda j: (0, j)),
            pl.BlockSpec((1, 2, rows), lambda j: (j, 0, 0)),
        ],
        out_shape=[
            jax.ShapeDtypeStruct((rows, width), bf16),
            jax.ShapeDtypeStruct((pairs, 2, rows), f32),
        ],
        scratch_shapes=[pltpu.VMEM((rows // TILE, PAGE_MAX + TILE, TILE), f32)],
        compiler_params=params(1),
        name="self_forward",
        cost_estimate=cost(14),
    )(pages[:, None], pages[None, :], qkv, qkv, qkv)


def self_backward_kernel(page_column, page_row, q, k, v, g, totals, out, bias, dk, dv):
    tiles = q.shape[0] // TILE
    half_scale = (q.shape[1] // 2) ** (-0.5)
    scale = LOG2E * half_scale

    @pl.when(pl.program_id(0) == 0)
    def _():
        fill_bias(page_column, page_row, bias, tiles)

    dk[...] = jnp.zeros_like(dk)
    dv[...] = jnp.zeros_like(dv)
    for tile in range(tiles):
        low, high = key_range(tile)
        here = slice(tile * TILE, (tile + 1) * TILE)
        queries, grads = two_heads(q[here, :]), two_heads(g[here, :])
        keys, values = k[low:high, :], v[low:high, :]
        level = jnp.concatenate([totals[0, 0:1, here], totals[0, 1:2, here]], axis=1)
        weights = jnp.exp2(
            product_t(keys, queries) * scale + twice(bias[tile, : high - low, :]) - level
        )
        along = weights * product_t(values, grads)
        change = (along - weights * jnp.sum(along, axis=0, keepdims=True)).astype(bf16)
        dv[low:high, :] += product(weights.astype(bf16), grads)
        dk[low:high, :] += product(change, queries)
        out[0, here, :] = (join_heads(product_rows(keys, change)) * half_scale).astype(bf16)
    out[1] = (dk[...] * half_scale).astype(bf16)
    out[2] = dv[...].astype(bf16)


def self_backward(pages, qkv, grads, totals):
    rows, width = qkv.shape[0], qkv.shape[1] // 3
    pairs = width // 128
    return pl.pallas_call(
        self_backward_kernel,
        grid=(pairs,),
        in_specs=[
            pl.BlockSpec((rows, 1), lambda j: (0, 0)),
            pl.BlockSpec((1, rows), lambda j: (0, 0)),
            pl.BlockSpec((rows, 128), lambda j: (0, j)),
            pl.BlockSpec((rows, 128), lambda j: (0, pairs + j)),
            pl.BlockSpec((rows, 128), lambda j: (0, 2 * pairs + j)),
            pl.BlockSpec((rows, 128), lambda j: (0, j)),
            pl.BlockSpec((1, 2, rows), lambda j: (j, 0, 0)),
        ],
        out_specs=pl.BlockSpec((3, rows, 128), lambda j: (0, 0, j)),
        out_shape=jax.ShapeDtypeStruct((3, rows, width), bf16),
        scratch_shapes=[
            pltpu.VMEM((rows // TILE, PAGE_MAX + TILE, TILE), f32),
            pltpu.VMEM((rows, 128), f32),
            pltpu.VMEM((rows, 128), f32),
        ],
        compiler_params=params(1),
        name="self_backward",
        cost_estimate=cost(15),
    )(pages[:, None], pages[None, :], qkv, qkv, qkv, grads, totals)


def cross_steps(count, tiles):
    first = (count + TILE - 1) // TILE
    skip = count // TILE
    return first, skip, first + tiles - skip


def cross_step(step, first, skip):
    image = jnp.where(step < first, 0, 1)
    tile = jnp.where(step < first, step, step - first + skip)
    return image, pl.multiple_of(tile * TILE, TILE)


def cross_forward_kernel(count_ref, q, k, v, out, totals):
    scale = LOG2E * (q.shape[1] // 2) ** (-0.5)
    count = count_ref[0]
    first, skip, steps = cross_steps(count, q.shape[0] // TILE)

    def one(step, carry):
        image, start = cross_step(step, first, skip)
        here = pl.ds(start, TILE)
        scores = product_t(k[image], two_heads(q[here, :])) * scale
        highest = jnp.max(scores, axis=0, keepdims=True)
        weights = jnp.exp2(scores - highest)
        total = jnp.sum(weights, axis=0, keepdims=True)
        mixed = product_rows(v[image], weights.astype(bf16)) * (1.0 / total)
        row = start + lax.broadcasted_iota(jnp.int32, (TILE, 128), 0)
        mine = (row >= count) == (image == 1)
        out[here, :] = jnp.where(mine, join_heads(mixed), out[here, :].astype(f32)).astype(bf16)
        level = highest + jnp.log2(total)
        lane = start + lax.broadcasted_iota(jnp.int32, (1, TILE), 1)
        mine = (lane >= count) == (image == 1)
        totals[0, 0:1, here] = jnp.where(mine, level[:, :TILE], totals[0, 0:1, here])
        totals[0, 1:2, here] = jnp.where(mine, level[:, TILE:], totals[0, 1:2, here])
        return carry

    lax.fori_loop(0, steps, one, 0)


def cross_forward(count, query, kv):
    rows, width = query.shape
    pairs = width // 128
    images, length = kv.shape[:2]
    return pl.pallas_call(
        cross_forward_kernel,
        grid_spec=pltpu.PrefetchScalarGridSpec(
            num_scalar_prefetch=1,
            grid=(pairs,),
            in_specs=[
                pl.BlockSpec((rows, 128), lambda j, c: (0, j)),
                pl.BlockSpec((images, length, 128), lambda j, c: (0, 0, j)),
                pl.BlockSpec((images, length, 128), lambda j, c: (0, 0, pairs + j)),
            ],
            out_specs=[
                pl.BlockSpec((rows, 128), lambda j, c: (0, j)),
                pl.BlockSpec((1, 2, rows), lambda j, c: (j, 0, 0)),
            ],
        ),
        out_shape=[
            jax.ShapeDtypeStruct((rows, width), bf16),
            jax.ShapeDtypeStruct((pairs, 2, rows), f32),
        ],
        compiler_params=params(1),
        name="cross_forward",
        cost_estimate=cost(24),
    )(count, query, kv, kv)


def cross_backward_kernel(count_ref, q, k, v, g, totals, dq_out, dkv_out, dq, dk, dv):
    half_scale = (q.shape[1] // 2) ** (-0.5)
    scale = LOG2E * half_scale
    count = count_ref[0]
    first, skip, steps = cross_steps(count, q.shape[0] // TILE)
    dq[...] = jnp.zeros_like(dq)
    dk[...] = jnp.zeros_like(dk)
    dv[...] = jnp.zeros_like(dv)

    def one(step, carry):
        image, start = cross_step(step, first, skip)
        here = pl.ds(start, TILE)
        queries, grads = two_heads(q[here, :]), two_heads(g[here, :])
        lane = start + lax.broadcasted_iota(jnp.int32, (1, TILE), 1)
        mine = (lane >= count) == (image == 1)
        level = jnp.concatenate(
            [
                jnp.where(mine, totals[0, 0:1, here], -MASKED),
                jnp.where(mine, totals[0, 1:2, here], -MASKED),
            ],
            axis=1,
        )
        weights = jnp.exp2(product_t(k[image], queries) * scale - level)
        along = weights * product_t(v[image], grads)
        change = (along - weights * jnp.sum(along, axis=0, keepdims=True)).astype(bf16)
        dv[image] += product(weights.astype(bf16), grads)
        dk[image] += product(change, queries)
        dq[here, :] += join_heads(product_rows(k[image], change))
        return carry

    lax.fori_loop(0, steps, one, 0)
    dq_out[...] = (dq[...] * half_scale).astype(bf16)
    dkv_out[0] = (dk[...] * half_scale).astype(bf16)
    dkv_out[1] = dv[...].astype(bf16)


def cross_backward(count, query, kv, grads, totals):
    rows, width = query.shape
    pairs = width // 128
    images, length = kv.shape[:2]
    return pl.pallas_call(
        cross_backward_kernel,
        grid_spec=pltpu.PrefetchScalarGridSpec(
            num_scalar_prefetch=1,
            grid=(pairs,),
            in_specs=[
                pl.BlockSpec((rows, 128), lambda j, c: (0, j)),
                pl.BlockSpec((images, length, 128), lambda j, c: (0, 0, j)),
                pl.BlockSpec((images, length, 128), lambda j, c: (0, 0, pairs + j)),
                pl.BlockSpec((rows, 128), lambda j, c: (0, j)),
                pl.BlockSpec((1, 2, rows), lambda j, c: (j, 0, 0)),
            ],
            out_specs=[
                pl.BlockSpec((rows, 128), lambda j, c: (0, j)),
                pl.BlockSpec((2, images, length, 128), lambda j, c: (0, 0, 0, j)),
            ],
            scratch_shapes=[
                pltpu.VMEM((rows, 128), f32),
                pltpu.VMEM((images, length, 128), f32),
                pltpu.VMEM((images, length, 128), f32),
            ],
        ),
        out_shape=[
            jax.ShapeDtypeStruct((rows, width), bf16),
            jax.ShapeDtypeStruct((2, images, length, width), bf16),
        ],
        compiler_params=params(1),
        name="cross_backward",
        cost_estimate=cost(28),
    )(count, query, kv, kv, grads, totals)


def put_rows(me, devices, lanes, left, staged):
    flipped = left.astype(f32).T
    depth = flipped.shape[0] // devices
    for block in range(devices):
        relative = block ^ me
        other = (relative // lanes) % 2
        place = (relative // (2 * lanes)) * lanes + relative % lanes + (1 - other) * (devices // 2)
        start = pl.multiple_of(place * depth, depth)
        staged[pl.ds(start, depth), :] = flipped[block * depth : (block + 1) * depth, :]


def put_halves(total, send, keep):
    half = total.shape[0] // 2
    send[...] = total[:half, :].astype(bf16).reshape(send.shape)
    keep[...] = total[half:, :].astype(bf16).reshape(keep.shape)


def weight_grad_kernel(devices, lanes, me_ref, left, right, send, keep, staged, flipped):
    @pl.when((pl.program_id(0) == 0) & (pl.program_id(1) == 0))
    def _():
        for part in range(left.shape[0]):
            put_rows(me_ref[0], devices, lanes, left[part], staged)
            flipped[part] = staged[...].astype(bf16)

    total = product(flipped[0], right[0, 0])
    for part in range(1, left.shape[0]):
        total += product(flipped[part], right[0, part])
    put_halves(total, send, keep)


def weight_grad(me, devices, lanes, left, right):
    parts, rows, depth = left.shape
    kinds, columns = right.shape[0], right.shape[3]
    wide = 512
    steps = columns // wide
    block = (1, devices // 2, depth // devices, wide)
    spec = pl.BlockSpec(block, lambda i, j, m: (i, 0, 0, j))
    shape = jax.ShapeDtypeStruct((kinds, devices // 2, depth // devices, columns), bf16)
    return pl.pallas_call(
        functools.partial(weight_grad_kernel, devices, lanes),
        grid_spec=pltpu.PrefetchScalarGridSpec(
            num_scalar_prefetch=1,
            grid=(kinds, steps),
            in_specs=[
                pl.BlockSpec((parts, rows, depth), lambda i, j, m: (0, 0, 0)),
                pl.BlockSpec((1, parts, rows, wide), lambda i, j, m: (i, 0, 0, j)),
            ],
            out_specs=[spec, spec],
            scratch_shapes=[pltpu.VMEM((depth, rows), f32), pltpu.VMEM((parts, depth, rows), bf16)],
        ),
        out_shape=[shape, shape],
        compiler_params=params(2),
        name="weight_grad",
        cost_estimate=cost(3 * kinds * parts),
    )(me, left, right)


def norm_grad_kernel(d_ref, w_ref, unit, inverse, gain, g_ref, out, low, gain_out, total):
    step = pl.program_id(0)
    kinds, _, width = d_ref.shape
    part = product_t(d_ref[0], w_ref[:, :width])
    for kind in range(1, kinds):
        part += product_t(d_ref[kind], w_ref[:, kind * width : (kind + 1) * width])
    wide = part.shape[1]
    total[:, pl.ds(pl.multiple_of(step * wide, wide), wide)] = part

    @pl.when(step == pl.num_programs(0) - 1)
    def _():
        change, gain_grad = norm_back(unit[...], inverse[...], gain[...], total[...])
        result = g_ref[...] + change
        out[...] = result
        low[...] = result.astype(bf16)
        gain_out[...] = gain_grad[None, :]


def norm_grad(grads, weights, first, unit, inverse, gain, g):
    kinds, rows, width = grads.shape
    wide = 256

    def whole(shape):
        return pl.BlockSpec(shape, lambda j: (0,) * len(shape))

    return pl.pallas_call(
        norm_grad_kernel,
        grid=(width // wide,),
        in_specs=[
            whole((kinds, rows, width)),
            pl.BlockSpec((wide, kinds * width), lambda j: (j, first)),
            whole((rows, width)), whole((rows, 1)), whole((1, width)), whole((rows, width)),
        ],
        out_specs=[whole((rows, width)), whole((rows, width)), whole((1, width))],
        out_shape=[
            jax.ShapeDtypeStruct((rows, width), f32),
            jax.ShapeDtypeStruct((rows, width), bf16),
            jax.ShapeDtypeStruct((1, width), f32),
        ],
        scratch_shapes=[pltpu.VMEM((rows, width), f32)],
        compiler_params=params(1),
        name="norm_grad",
        cost_estimate=cost(4 * kinds),
    )(grads, weights, unit, inverse, gain, g)


def feed_kernel(
    devices, lanes, me_ref, x_ref, g_ref, gain_ref, up_ref, down_ref,
    out, gx, ggain, up_send, up_keep, down_send, down_keep,
    unit, inverse, hidden, staged, flipped, total, back,
):
    step = pl.program_id(0)
    me = me_ref[0]

    @pl.when(step == 0)
    def _():
        h, u, i = normed(x_ref[...], gain_ref[...])
        unit[...] = u
        inverse[...] = i
        hidden[...] = h.astype(bf16)
        put_rows(me, devices, lanes, h, staged)
        flipped[...] = staged[...].astype(bf16)
        total[...] = jnp.zeros_like(total)
        back[...] = jnp.zeros_like(back)

    g = g_ref[...]
    up = up_ref[...].reshape(-1, up_ref.shape[-1])
    down = down_ref[...].reshape(-1, down_ref.shape[-1])
    inner = product(hidden[...], up)
    share = 0.5 + 0.5 * lax.erf(inner * (0.5**0.5))
    slope = share + inner * (jnp.exp(-0.5 * inner * inner) * 0.3989422804014327)
    active = (inner * share).astype(bf16)
    total[...] += product(active, down)
    change = (product_t(g, down) * slope).astype(bf16)
    back[...] += product_t(change, up)
    put_halves(product(flipped[...], change), up_send, up_keep)
    grad_down = product_rows(active, g)
    depth = grad_down.shape[0] // lanes
    low = me % lanes

    def put(target):
        for block in range(lanes):
            target[0, block ^ low] = grad_down[block * depth : (block + 1) * depth, :].astype(bf16)

    @pl.when(step % 2 == 1)
    def _():
        put(down_send)

    @pl.when(step % 2 == 0)
    def _():
        put(down_keep)

    @pl.when(step == pl.num_programs(0) - 1)
    def _():
        out[...] = (x_ref[...] + total[...]).astype(bf16)
        gx_norm, gain_grad = norm_back(unit[...], inverse[...], gain_ref[...], back[...])
        gx[...] = g_ref[...].astype(f32) + gx_norm
        ggain[...] = gain_grad[None, :]


def feed(me, devices, lanes, x, g, gain, weights):
    rows, width = x.shape
    pieces, depth = weights.shape[2:4]
    hidden = pieces * width
    groups = devices // lanes
    tile = hidden // groups
    across = width // tile

    def group(s, m):
        return s ^ (m[0] // lanes)

    def whole(shape):
        return pl.BlockSpec(shape, lambda s, m: (0,) * len(shape))

    up_block = pl.BlockSpec((devices // 2, width // devices, tile), lambda s, m: (0, 0, group(s, m)))
    down_block = pl.BlockSpec((1, lanes, tile // lanes, width), lambda s, m: (s // 2, 0, 0, 0))
    up_shape = jax.ShapeDtypeStruct((devices // 2, width // devices, hidden), bf16)
    down_shape = jax.ShapeDtypeStruct((groups // 2, lanes, tile // lanes, width), bf16)
    return pl.pallas_call(
        functools.partial(feed_kernel, devices, lanes),
        grid_spec=pltpu.PrefetchScalarGridSpec(
            num_scalar_prefetch=1,
            grid=(groups,),
            in_specs=[
                whole((rows, width)),
                whole((rows, width)),
                whole((1, width)),
                pl.BlockSpec(
                    (devices, None, None, depth, tile),
                    lambda s, m: (0, 0, group(s, m) // across, 0, group(s, m) % across),
                ),
                pl.BlockSpec(
                    (lanes, None, pieces, depth, width), lambda s, m: (group(s, m), 1, 0, 0, 0)
                ),
            ],
            out_specs=[
                whole((rows, width)), whole((rows, width)), whole((1, width)),
                up_block, up_block, down_block, down_block,
            ],
            scratch_shapes=[
                pltpu.VMEM((rows, width), f32),
                pltpu.VMEM((rows, 1), f32),
                pltpu.VMEM((rows, width), bf16),
                pltpu.VMEM((width, rows), f32),
                pltpu.VMEM((width, rows), bf16),
                pltpu.VMEM((rows, width), f32),
                pltpu.VMEM((rows, width), f32),
            ],
        ),
        out_shape=[
            jax.ShapeDtypeStruct((rows, width), bf16),
            jax.ShapeDtypeStruct((rows, width), f32),
            jax.ShapeDtypeStruct((1, width), f32),
            up_shape, up_shape, down_shape, down_shape,
        ],
        compiler_params=params(1),
        name="feed",
        cost_estimate=cost(45),
    )(me, x, g, gain, weights, weights)


def gather_kernel(devices, lanes, tracks, x_ref, out, own_sem, send_sem, recv_sem):
    me = lax.axis_index("dp") * lanes + lax.axis_index("fsdp")
    count = devices // 2

    def device(bit):
        other = me ^ bit
        return (other // lanes, lax.rem(other, lanes))

    barrier = pltpu.get_barrier_semaphore()
    every = [1 << b for b in range(devices.bit_length() - 1)]
    for bit in every:
        pl.semaphore_signal(
            barrier, inc=1, device_id=device(bit), device_id_type=pl.DeviceIdType.MESH
        )
    pl.semaphore_wait(barrier, len(every))
    own = pltpu.make_async_copy(x_ref, out.at[me], own_sem)
    own.start()
    sends = []

    def block(track, number, to_core):
        low, high, bits = tracks[track]
        owner = me ^ sum(b for p, b in enumerate(bits) if (number >> p) & 1)
        return out.at[owner ^ lanes if to_core else owner, :, low:high]

    def arrived(track, number):
        to_core = number >= count
        here = block(track, number - count if to_core else number, to_core)
        pltpu.make_async_remote_copy(
            src_ref=here,
            dst_ref=here,
            send_sem=send_sem.at[0],
            recv_sem=recv_sem.at[track, number],
            device_id=device(lanes),
            device_id_type=pl.DeviceIdType.MESH,
        ).wait_recv()
        return here

    for number in sorted(range(count), key=lambda k: (bin(k).count("1"), k)):
        for track, (low, high, bits) in enumerate(tracks):
            there = block(track, number, False)
            here = arrived(track, number) if number else x_ref.at[:, low:high]
            for place, bit in enumerate(bits + (lanes,)):
                if number >> place == 0 or bit == lanes:
                    copy = pltpu.make_async_remote_copy(
                        src_ref=here,
                        dst_ref=there,
                        send_sem=send_sem.at[len(sends)],
                        recv_sem=recv_sem.at[track, number + (1 << place)],
                        device_id=device(bit),
                        device_id_type=pl.DeviceIdType.MESH,
                    )
                    copy.start()
                    sends.append(copy)
    for number in range(count, devices):
        for track in range(len(tracks)):
            arrived(track, number)
    for copy in sends:
        copy.wait_send()
    own.wait()


def gather(number, devices, lanes, values):
    depth, columns = values.shape
    middle = (columns // 256) * 128
    high = tuple(2 * lanes << b for b in range((devices // (2 * lanes)).bit_length() - 1))
    links = [high + tuple(1 << b for b in way) for way in orders(lanes)]
    tracks = ((0, middle, links[0]), (middle, columns, links[1]))
    return pl.pallas_call(
        functools.partial(gather_kernel, devices, lanes, tracks),
        in_specs=[pl.BlockSpec(memory_space=pltpu.VMEM)],
        out_specs=pl.BlockSpec(memory_space=pltpu.HBM),
        out_shape=jax.ShapeDtypeStruct((devices, depth, columns), values.dtype),
        scratch_shapes=[
            pltpu.SemaphoreType.DMA,
            pltpu.SemaphoreType.DMA((len(tracks) * (devices - 1),)),
            pltpu.SemaphoreType.DMA((len(tracks), devices)),
        ],
        compiler_params=pltpu.CompilerParams(collective_id=number, has_side_effects=True),
        name="gather",
        cost_estimate=cost(40),
    )(values).reshape(-1, columns)


def swap(values, devices, bit):
    return lax.ppermute(values, AXES, [(i, i ^ bit) for i in range(devices)])


def cross_core(halves, devices, lanes):
    send, keep = (half.reshape(-1, devices // 2, *half.shape[-2:]) for half in halves)
    arrived = swap(send, devices, lanes)
    return [(keep[kind], arrived[kind]) for kind in range(keep.shape[0])]


def halved(pairs, devices, left, bit):
    inner = 1 << left.index(bit)

    def total(pair, pick):
        keep, arrived = pair
        shape = (keep.shape[0] // (2 * inner), 2, inner, *keep.shape[1:])
        a, b = keep.reshape(shape)[:, pick], arrived.reshape(shape)[:, pick]
        return (a.astype(f32) + b.astype(f32)).astype(bf16).reshape(-1, *keep.shape[1:])

    out, keep = (jnp.concatenate([total(pair, pick) for pair in pairs], axis=-1) for pick in (1, 0))
    return keep, swap(out, devices, 1 << bit)


def owner_sums(pairs, devices, lanes, order, late=()):
    left = list(range(lanes.bit_length() - 1))
    for stage, bit in enumerate(order):
        pairs = [halved(pairs, devices, left, bit)]
        if stage == 0 and late:
            pairs.append(halved(late, devices, left, bit))
        left.remove(bit)
    ((keep, arrived),) = pairs
    result = keep[0].astype(f32) + arrived[0].astype(f32)
    for high in range(1, devices // (2 * lanes)):
        out = (keep[high].astype(f32) + arrived[high].astype(f32)).astype(bf16)
        result += swap(out, devices, high * 2 * lanes).astype(f32)
    return result


def after(values, first):
    return lax.optimization_barrier((values, first))[0]


def orders(lanes):
    low = list(range(lanes.bit_length() - 1))
    return low, low[::-1]


def gain_halves(values, devices, lanes, me):
    kinds, depth = values.shape
    blocks = jnp.pad(values.T, ((0, 0), (0, 128 - kinds))).astype(bf16)
    blocks = blocks.reshape(devices, depth // devices, 128)[jnp.arange(devices) ^ me]
    blocks = blocks.reshape(-1, 2, lanes, depth // devices, 128)
    return blocks[:, 1], blocks[:, 0]


def shards(devices, lanes, tokens, images, segment_ids, image_map, out_grad, norm_self, attn_query,
           attn_key, attn_value, attn_out, norm_cross, cross_query, cross_key, cross_value, cross_out,
           norm_ffn, ffn_up, ffn_down):
    me = lax.axis_index("dp") * lanes + lax.axis_index("fsdp")
    me_ref = me.astype(jnp.int32)[None]
    depth, width = attn_query.shape
    gains = jnp.stack([norm_self, norm_cross, norm_ffn], axis=1)
    gains = jnp.pad(gains, ((0, 0), (0, 128 - 3)))
    first_set = jnp.concatenate([attn_query, attn_key, attn_value, cross_key, cross_value, gains], axis=1)
    second_set = jnp.concatenate([attn_out, cross_query, cross_out], axis=1)
    pieces = ffn_up.shape[1] // width
    feed_set = jnp.stack(
        [ffn_up.reshape(depth, pieces, width).transpose(1, 0, 2), ffn_down.reshape(pieces, depth, width)]
    )
    first_set = gather(0, devices, lanes, first_set)
    feed_set = lax.all_gather(after(feed_set, first_set), AXES, axis=0)
    w_qkv = first_set[:, : 3 * width]
    w_kv = first_set[:, 3 * width : 5 * width]
    gains = first_set[:, 5 * width : 5 * width + 3].T.astype(f32)

    pages = segment_ids[0]
    length = pages.shape[0]
    page_index = jnp.arange(image_map.shape[1])
    second = jnp.sum(jnp.where(pages[:, None] == page_index[None, :], image_map[0][None, :], 0), axis=1)
    place_now = jnp.arange(length)
    earlier = place_now[None, :] < place_now[:, None]
    ones_before = jnp.sum(jnp.where(earlier, second[None, :], 0), axis=1)
    count = length - jnp.sum(second)
    place = jnp.where(second == 1, count + ones_before, place_now - ones_before)
    moved = place_now[:, None] == place[None, :]
    order = moved.astype(bf16)
    count = count.astype(jnp.int32)[None]
    pages = jnp.sum(jnp.where(moved, pages[None, :], 0), axis=1)
    inputs = product(order, tokens[0])
    grad_out = product(order, out_grad[0]).astype(bf16)

    hidden_one, unit_one, inverse_one = normed(inputs, gains[0:1])
    hidden_one = hidden_one.astype(bf16)
    qkv = product(hidden_one, w_qkv).astype(bf16)
    mixed_one, log_one = self_forward(pages, qkv)
    kv = lax.dot_general(images, w_kv, (((2,), (0,)), ((), ())), preferred_element_type=f32).astype(bf16)
    second_set = gather(1, devices, lanes, after(second_set, (mixed_one, kv)))
    w_out = second_set[:, :width]
    w_cross_query = second_set[:, width : 2 * width]
    w_cross_out = second_set[:, 2 * width :]
    after_self = inputs + product(mixed_one, w_out)
    hidden_two, unit_two, inverse_two = normed(after_self, gains[1:2])
    hidden_two = hidden_two.astype(bf16)
    query_two = product(hidden_two, w_cross_query).astype(bf16)
    mixed_two, log_two = cross_forward(count, query_two, kv)
    after_cross = after_self + product(mixed_two, w_cross_out)

    (output, grad_after_cross, grad_gain_ffn, up_send, up_keep, down_send, down_keep) = feed(
        me_ref, devices, lanes, after_cross, grad_out, gains[2:3], feed_set
    )
    one_way, other_way = orders(lanes)

    def sums(way, *pairs, late=()):
        return owner_sums(sum(pairs, []), devices, lanes, way, late)

    def halves_of(left, right):
        return weight_grad(me_ref, devices, lanes, left, right)

    def paired(halves):
        return cross_core(halves, devices, lanes)

    grad_up = sums(one_way, paired((up_send, up_keep)))
    grad_down = sums(other_way, paired((down_send, down_keep)))

    branch_two = grad_after_cross.astype(bf16)
    grad_mixed_two = product_t(branch_two, w_cross_out).astype(bf16)
    halves = halves_of(mixed_two[None], branch_two[None, None])
    pair_out_two = paired(halves)
    grad_mixed_two = after(grad_mixed_two, halves[0])
    grad_query_two, grad_kv = cross_backward(count, query_two, kv, grad_mixed_two, log_two)
    halves = halves_of(images, grad_kv)
    pair_kv = paired(halves)
    halves = halves_of(hidden_two[None], after(grad_query_two, halves[0])[None, None])
    pair_query_two = paired(halves)
    grad_c = sums(one_way, pair_out_two, pair_query_two)
    grad_d = sums(other_way, pair_kv)
    grad_after_self, branch_one, grad_gain_cross = norm_grad(
        after(grad_query_two, halves[0])[None], second_set, 1, unit_two, inverse_two, gains[1:2], grad_after_cross
    )
    grad_mixed_one = product_t(branch_one, w_out).astype(bf16)
    grad_qkv = self_backward(pages, qkv, grad_mixed_one, log_one)
    halves = halves_of(mixed_one[None], after(branch_one, grad_qkv)[None, None])
    pair_out_one = paired(halves)
    halves = halves_of(hidden_one[None], after(grad_qkv, halves[0])[:, None])
    pair_qkv = paired(halves)
    _, grad_inputs, grad_gain_self = norm_grad(
        after(grad_qkv, halves[0]), first_set, 0, unit_one, inverse_one, gains[0:1], grad_after_self
    )
    gain_grads = jnp.concatenate([grad_gain_self, grad_gain_cross, grad_gain_ffn])
    pair_gains = paired(gain_halves(gain_grads, devices, lanes, me))
    grad_a = sums(one_way, pair_out_one, pair_qkv[:1])
    grad_b = sums(other_way, pair_qkv[1:], late=pair_gains)
    gain_sums = grad_b[:, 2 * width :]

    grad_kv = after(grad_kv, grad_inputs)
    back = (((2,), (1,)), ((), ()))
    grad_images = lax.dot_general(grad_kv[0], w_kv[:, :width], back, preferred_element_type=f32)
    grad_images += lax.dot_general(grad_kv[1], w_kv[:, width:], back, preferred_element_type=f32)
    output = product_rows(order, output).astype(bf16)
    grad_inputs = product_rows(order, grad_inputs).astype(bf16)
    return (
        output[None],
        grad_inputs[None],
        grad_images.astype(bf16),
        gain_sums[:, 0],
        grad_a[:, width:],
        grad_b[:, :width],
        grad_b[:, width : 2 * width],
        grad_a[:, :width],
        gain_sums[:, 1],
        grad_c[:, width:],
        grad_d[:, :width],
        grad_d[:, width:],
        grad_c[:, :width],
        gain_sums[:, 2],
        grad_up,
        grad_down,
    )


def solution(mesh):
    rows = P(AXES)
    devices, lanes = mesh.shape["dp"] * mesh.shape["fsdp"], mesh.shape["fsdp"]
    return jax.shard_map(
        functools.partial(shards, devices, lanes),
        mesh=mesh,
        in_specs=(rows,) * 18,
        out_specs=(rows,) * 16,
        check_vma=False,
    )
```

profile of v0, /device:TPU:0, one launch (start us, length us, event | category | flops | bytes accessed | tf_op | source)
XLA Modules:
  0.0 636.3 jit_solution(1364116220456897283)
XLA Ops:
  13.1 60.7 %gather.15 = bf16[32,32,5248]{2,1,0:T(8,128)(2,1)} custom-call(bf16[32,5248]{1,0:T(8,128)(2,1)} %copy-done.28), custom_call_target="tpu_custom_call" | custom-call | flops 40000000000 | tf_op jit(solution)/shard_map/gather/pallas_call | solution.py:625
  74.9 1.5 pad_maximum_fusion.9
  77.4 1.8 slice_convert_fusion
  83.0 2.1 copy.202.left
  86.9 1.3 fusion.84
  89.8 5.0 fusion.2.q.k.v
  94.8 6.9 %convert_bitcast_fusion.k.v = bf16[2,588,2048]{2,1,0:T(8,128)(2,1)} fusion(bf16[1024,5248]{1,0:T(8,128)(2,1)S(1)} %bitcast.502, bf16[2,588,1024]{2,0,1:T(2,128)(2,1)S(1)} %copy-done.11), kind=kOutput, calls=%fused_computation.4 | convolution fusion | flops 4934909952 | bytes 11419648 | tf_op jit(solution)/shard_map/dot_general | solution.py:736
  101.7 14.1 %self_forward.1 = (bf16[512,1024]{1,0:T(8,128)(2,1)}, f32[8,2,512]{2,1,0:T(2,128)}) custom-call(s32[512,1]{1,0:T(8,128)} %copy.201.page_column, s32[1,512]{1,0:T(1,128)} %bitcast.493, bf16[512,3072]{1,0:T(8,128)(2,1)} %fusion.2.q.k.v, bf16[512,3072]{1,0:T(8,128)(2,1)} %fusion.2.q.k.v, bf16[512,3072]{1,0:T(8,128)(2,1)} %fusion.2.q.k.v), custom_call_target="tpu_custom_call" | custom-call | flops 14000000000 | tf_op jit(solution)/shard_map/self_forward/pallas_call | solution.py:119
  115.8 53.1 %gather.16 = bf16[32,32,3072]{2,1,0:T(8,128)(2,1)} custom-call(bf16[32,3072]{1,0:T(8,128)(2,1)} %pad_maximum_fusion.10.x_ref), custom_call_target="tpu_custom_call" | custom-call | flops 40000000000 | tf_op jit(solution)/shard_map/gather/pallas_call | solution.py:625
  168.9 3.3 fusion.131
  176.2 2.9 convolution_convert_fusion.2.g_ref
  179.2 1.3 fusion.85
  180.5 4.6 fusion.38.q
  185.2 29.9 %cross_forward.1 = (bf16[512,1024]{1,0:T(8,128)(2,1)}, f32[8,2,512]{2,1,0:T(2,128)}) custom-call(s32[1]{0:T(128)} %bitcast.15.count_ref, bf16[512,1024]{1,0:T(8,128)(2,1)} %fusion.38.q, bf16[2,588,2048]{2,1,0:T(8,128)(2,1)} %convert_bitcast_fusion.k.v, bf16[2,588,2048]{2,1,0:T(8,128)(2,1)} %convert_bitcast_fusion.k.v), custom_call_target="tpu_custom_call" | custom-call | flops 24000000000 | tf_op jit(solution)/shard_map/cross_forward/pallas_call | solution.py:243
  215.0 5.1 fusion.29.x_ref
  220.2 38.7 %feed.1 = (bf16[512,1024]{1,0:T(8,128)(2,1)}, f32[512,1024]{1,0:T(8,128)}, f32[1,1024]{1,0:T(1,128)}, bf16[16,32,4096]{2,1,0:T(8,128)(2,1)}, bf16[16,32,4096]{2,...) custom-call(s32[1]{0:T(128)} %bitcast.2.me_ref, f32[512,1024]{1,0:T(8,128)} %fusion.29.x_ref, ...), custom_call_target="tpu_custom_call" | custom-call | flops 44999999488 | tf_op jit(solution)/shard_map/feed/pallas_call | solution.py:515
  258.8 2.9 convert_bitcast_fusion.1.right
  261.8 3.9 fusion.35.g
  265.6 4.4 weight_grad.5
  270.5 34.9 %cross_backward.1 = (bf16[512,1024]{1,0:T(8,128)(2,1)}, bf16[2,2,588,1024]{3,2,1,0:T(8,128)(2,1)}) custom-call(s32[1]{0:T(128)} %bitcast.15.count_ref, bf16[512,1024]{1,0:T(8,128)(2,1)} %fusion.38.q, bf16[2,588,2048]{2,1,0:T(8,128)(2,1)} %convert_bitcast_fusion.k.v, bf16[2,588,2048]{2,1,0:T(8,128)(2,1)} %convert_bitcast_fusion.k.v, ...), custom_call_target="tpu_custom_call" | custom-call | flops 28000000000 | tf_op jit(solution)/shard_map/cross_backward/pallas_call | solution.py:308
  305.3 12.0 %weight_grad.6 = (bf16[2,16,32,1024]{3,2,1,0:T(8,128)(2,1)}, bf16[2,16,32,1024]{3,2,1,0:T(8,128)(2,1)}) custom-call(s32[1]{0:T(128)} %bitcast.2.me_ref, bf16[2,588,1024]{2,1,0:T(8,128)(2,1)} %copy.202.left, bf16[2,2,588,1024]{3,2,1,0:T(8,128)(2,1)} %get-tuple-element.77.right), custom_call_target="tpu_custom_call" | custom-call | flops 12000000000 | tf_op jit(solution)/shard_map/weight_grad/pallas_call | solution.py:378
  317.4 4.5 weight_grad.7
  322.4 8.1 %norm_grad.2 = (f32[512,1024]{1,0:T(8,128)}, bf16[512,1024]{1,0:T(8,128)(2,1)}, f32[1,1024]{1,0:T(1,128)}) custom-call(bf16[1,512,1024]{2,1,0:T(8,128)(2,1)} %bitcast.519, bf16[1024,3072]{1,0:T(8,128)(2,1)} %bitcast.514, f32[512,1024]{1,0:T(8,128)} %copy-done.13, f32[512,1]{1,0:T(8,128)} %copy.206.inverse, f32[1,1024]{1,0:T(1,128)} %copy-done.27, ...), custom_call_target="tpu_custom_call" | custom-call | flops 4000000000 | tf_op jit(solution)/shard_map/norm_grad/pallas_call | solution.py:422
  330.5 4.2 fusion.32.g
  334.7 15.0 %self_backward.1.d_ref = bf16[3,512,1024]{2,1,0:T(8,128)(2,1)} custom-call(s32[512,1]{1,0:T(8,128)} %copy.201.page_column, s32[1,512]{1,0:T(1,128)} %bitcast.494, bf16[512,3072]{1,0:T(8,128)(2,1)} %fusion.2.q.k.v, bf16[512,3072]{1,0:T(8,128)(2,1)} %fusion.2.q.k.v, bf16[512,3072]{1,0:T(8,128)(2,1)} %fusion.2.q.k.v, bf16[512,1024]{1,0:T(8,128)(2,1)} %fusion.32.g, ...), custom_call_target="tpu_custom_call" | custom-call | flops 15000000512 | tf_op jit(solution)/shard_map/self_backward/pallas_call | solution.py:176
  349.7 4.5 weight_grad.8
  354.2 8.5 %weight_grad.9 = (bf16[3,16,32,1024]{3,2,1,0:T(8,128)(2,1)}, bf16[3,16,32,1024]{3,2,1,0:T(8,128)(2,1)}) custom-call(s32[1]{0:T(128)} %bitcast.2.me_ref, bf16[1,512,1024]{2,1,0:T(8,128)(2,1)} %get-tuple-element.191.left, bf16[3,1,512,1024]{3,2,1,0:T(8,128)(2,1)} %bitcast.516), custom_call_target="tpu_custom_call" | custom-call | flops 8999999488 | tf_op jit(solution)/shard_map/weight_grad/pallas_call | solution.py:378
  362.7 3.8 fusion.119
  366.5 11.1 %norm_grad.3 = (f32[512,1024]{1,0:T(8,128)}, bf16[512,1024]{1,0:T(8,128)(2,1)}, f32[1,1024]{1,0:T(1,128)}) custom-call(bf16[3,512,1024]{2,1,0:T(8,128)(2,1)} %self_backward.1.d_ref, bf16[1024,5248]{1,0:T(8,128)(2,1)} %bitcast.498, f32[512,1024]{1,0:T(8,128)} %copy-done.12, f32[512,1]{1,0:T(8,128)} %copy.208.inverse, f32[1,1024]{1,0:T(1,128)} %copy-done.26, ...), custom_call_target="tpu_custom_call" | custom-call | flops 12000000000 | tf_op jit(solution)/shard_map/norm_grad/pallas_call | solution.py:422
  381.1 5.2 fusion.6
  386.3 5.9 add_convert_fusion
  393.7 3.0 fusion.42
  397.9 1.6 add_convert_fusion.18
  401.5 1.7 fusion.41
  403.2 3.9 copy.233
  411.0 15.2 %collective-permute-done.16 = bf16[8,32,2048]{2,1,0:T(8,128)(2,1)S(1)} collective-permute-done((bf16[8,32,2048]{2,1,0:T(8,128)(2,1)S(1)}, bf16[8,32,2048]{2,1,0:T(8,128)(2,1)S(1)}, u32[]{:S(2)}, u32[]{:S(2)}) %collective-permute-start.16) | collective-permute-done | bytes 1048608 | tf_op jit(solution)/shard_map/ppermute | solution.py:642
  427.8 1.7 fusion.122
  431.0 10.5 %collective-permute-done.17 = bf16[4,32,2048]{2,1,0:T(8,128)(2,1)S(1)} collective-permute-done((bf16[4,32,2048]{2,1,0:T(8,128)(2,1)S(1)}, bf16[4,32,2048]{2,1,0:T(8,128)(2,1)S(1)}, u32[]{:S(2)}, u32[]{:S(2)}) %collective-permute-start.17) | collective-permute-done | bytes 524320 | tf_op jit(solution)/shard_map/ppermute | solution.py:642
  441.8 4.3 collective-permute-start.20
  446.5 2.0 collective-permute-done.18
  448.5 3.5 collective-permute-done.19
  452.8 9.6 %collective-permute-done.22 = bf16[8,32,2048]{2,1,0:T(8,128)(2,1)S(1)} collective-permute-done((bf16[8,32,2048]{2,1,0:T(8,128)(2,1)S(1)}, bf16[8,32,2048]{2,1,0:T(8,128)(2,1)S(1)}, u32[]{:S(2)}, u32[]{:S(2)}) %collective-permute-start.22) | collective-permute-done | bytes 1048608 | tf_op jit(solution)/shard_map/ppermute | solution.py:642
  465.9 9.2 %collective-permute-done.23 = bf16[4,32,2048]{2,1,0:T(8,128)(2,1)S(1)} collective-permute-done((bf16[4,32,2048]{2,1,0:T(8,128)(2,1)S(1)}, bf16[4,32,2048]{2,1,0:T(8,128)(2,1)S(1)}, u32[]{:S(2)}, u32[]{:S(2)}) %collective-permute-start.23) | collective-permute-done | bytes 524320 | tf_op jit(solution)/shard_map/ppermute | solution.py:642
  475.4 4.3 collective-permute-start.26
  479.8 2.5 collective-permute-done.24
  482.3 3.9 collective-permute-done.25
  488.2 2.4 fusion.86
  491.5 1.8 add_convert_fusion.4
  494.2 14.1 %collective-permute-done.9 = bf16[8,32,2048]{2,1,0:T(8,128)(2,1)S(1)} collective-permute-done((bf16[8,32,2048]{2,1,0:T(8,128)(2,1)S(1)}, bf16[8,32,2048]{2,1,0:T(8,128)(2,1)S(1)}, u32[]{:S(2)}, u32[]{:S(2)}) %collective-permute-start.9) | collective-permute-done | bytes 1048608 | tf_op jit(solution)/shard_map/ppermute | solution.py:642
  509.9 2.2 collective-permute-done.1
  513.4 49.0 %collective-permute-done.10 = bf16[4,32,2048]{2,1,0:T(8,128)(2,1)S(1)} collective-permute-done((bf16[4,32,2048]{2,1,0:T(8,128)(2,1)S(1)}, bf16[4,32,2048]{2,1,0:T(8,128)(2,1)S(1)}, u32[]{:S(2)}, u32[]{:S(2)}) %collective-permute-start.10) | collective-permute-done | bytes 524320 | tf_op jit(solution)/shard_map/ppermute | solution.py:642
  562.7 4.3 collective-permute-start.13
  568.2 7.0 %collective-permute-done.12 = bf16[32,2048]{1,0:T(8,128)(2,1)S(1)} collective-permute-done((bf16[32,2048]{1,0:T(8,128)(2,1)S(1)}, bf16[32,2048]{1,0:T(8,128)(2,1)S(1)}, u32[]{:S(2)}, u32[]{:S(2)}) %collective-permute-start.12) | collective-permute-done | bytes 131104 | tf_op jit(solution)/shard_map/ppermute | solution.py:642
  575.2 1.9 collective-permute-start.7
  579.6 1.8 collective-permute-start.29
  581.4 1.7 collective-permute-done.6
  585.1 8.1 %collective-permute-done.35 = bf16[4,128,1024]{2,1,0:T(8,128)(2,1)S(1)} collective-permute-done((bf16[4,128,1024]{2,1,0:T(8,128)(2,1)S(1)}, bf16[4,128,1024]{2,1,0:T(8,128)(2,1)S(1)}, u32[]{:S(2)}, u32[]{:S(2)}) %collective-permute-start.35) | collective-permute-done | bytes 1048608 | tf_op jit(solution)/shard_map/ppermute | solution.py:642
  593.5 2.1 collective-permute-start.36
  596.5 1.5 collective-permute-start.38
  599.4 1.8 collective-permute-start.31
  601.2 3.8 collective-permute-done.36
  605.0 2.2 collective-permute-start.32
  607.1 12.1 %collective-permute-done.37 = bf16[128,1024]{1,0:T(8,128)(2,1)S(1)} collective-permute-done((bf16[128,1024]{1,0:T(8,128)(2,1)S(1)}, bf16[128,1024]{1,0:T(8,128)(2,1)S(1)}, u32[]{:S(2)}, u32[]{:S(2)}) %collective-permute-start.37) | collective-permute-done | bytes 262176 | tf_op jit(solution)/shard_map/ppermute | solution.py:642
  620.3 7.7 %collective-permute-done.31 = bf16[32,4096]{1,0:T(8,128)(2,1)S(1)} collective-permute-done((bf16[32,4096]{1,0:T(8,128)(2,1)S(1)}, bf16[32,4096]{1,0:T(8,128)(2,1)S(1)}, u32[]{:S(2)}, u32[]{:S(2)}) %collective-permute-start.31) | collective-permute-done | bytes 262176 | tf_op jit(solution)/shard_map/ppermute | solution.py:642
  (222 shorter events, 56.5 us)
Async XLA Ops:
  7.2 77.9 %copy-start = (bf16[1,512,1024]{2,1,0:T(8,128)(2,1)S(1)}, bf16[1,512,1024]{2,1,0:T(8,128)(2,1)}, u32[]{:S(2)}) copy-start(bf16[1,512,1024]{2,1,0:T(8,128)(2,1)} %param.18) | copy-start | bytes 3145732
  7.2 213.0 %all-gather.3.cloned.1.call-start = ((), (), s32[]{:S(2)}) async-start(), calls=%async_computation | async-start | bytes 17301504 | tf_op jit(solution)/shard_map/all_gather | solution.py:711
  13.1 60.7 %copy-start.19 = (bf16[32,4096]{1,0:T(8,128)(2,1)S(1)}, bf16[32,4096]{1,0:T(8,128)(2,1)}, u32[]{:S(2)}) copy-start(bf16[32,4096]{1,0:T(8,128)(2,1)} %param.34) | copy-start | bytes 786436
  13.1 61.6 %copy-start.20 = (bf16[128,1024]{1,0:T(8,128)(2,1)S(1)}, bf16[128,1024]{1,0:T(8,128)(2,1)}, u32[]{:S(2)}) copy-start(bf16[128,1024]{1,0:T(8,128)(2,1)} %param.35) | copy-start | bytes 786436
  74.9 5.5 copy-start.30
  74.9 5.5 copy-start.34
  74.9 8.1 %copy-start.11 = (bf16[2,588,1024]{2,0,1:T(2,128)(2,1)S(1)}, bf16[2,588,1024]{2,0,1:T(2,128)(2,1)}, u32[]{:S(2)}) copy-start(bf16[2,588,1024]{2,0,1:T(2,128)(2,1)} %param.19) | copy-start | bytes 7225348
  81.9 94.3 %copy-start.24 = (s32[512]{0:T(512)}, s32[512]{0:T(512)S(1)}, u32[]{:S(2)}) copy-start(s32[512]{0:T(512)S(1)} %subtract_select_fusion) | copy-start | bytes 6148
  82.1 3.0 copy-start.29
  83.0 6.7 %copy-start.31 = (bf16[32,32,5248]{2,1,0:T(8,128)(2,1)S(1)}, bf16[32,32,5248]{2,1,0:T(8,128)(2,1)}, u32[]{:S(2)}) copy-start(bf16[32,32,5248]{2,1,0:T(8,128)(2,1)} %gather.15) | copy-start | bytes 32243716
  86.9 93.6 %copy-start.27 = (f32[1,1024]{1,0:T(1,128)}, f32[1,1024]{1,0:T(1,128)S(1)}, u32[]{:S(2)}) copy-start(f32[1,1024]{1,0:T(1,128)S(1)} %get-tuple-element.257.gain) | copy-start | bytes 12292
  89.0 5.7 copy-start.12
  115.8 53.2 %copy-start.3 = (f32[512,1024]{1,0:T(8,128)S(1)}, f32[512,1024]{1,0:T(8,128)}, u32[]{:S(2)}) copy-start(f32[512,1024]{1,0:T(8,128)} %copy-done.2) | copy-start | bytes 6291460
  173.9 5.3 copy-start.5
  180.5 4.6 copy-start.13
  270.1 129.4 %collective-permute-start.14 = (bf16[1,16,32,1024]{3,2,1,0:T(8,128)(2,1)}, bf16[1,16,32,1024]{3,2,1,0:T(8,128)(2,1)}, u32[]{:S(2)}, u32[]{:S(2)}) collective-permute-start(bf16[1,16,32,1024]{3,2,1,0:T(8,128)(2,1)} %get-tuple-element.59), channel_id=1, source_target_pairs={{0,4},{1,5},{2,6},{3,7},{4,0},{5,1},{6,2},{7,3},{8,12},{9,13},{10,... | collective-permute-start | bytes 3145736 | tf_op jit(solution)/shard_map/ppermute | solution.py:642
  317.3 110.5 %collective-permute-start.21 = (bf16[2,16,32,1024]{3,2,1,0:T(8,128)(2,1)}, bf16[2,16,32,1024]{3,2,1,0:T(8,128)(2,1)}, u32[]{:S(2)}, u32[]{:S(2)}) collective-permute-start(bf16[2,16,32,1024]{3,2,1,0:T(8,128)(2,1)} %get-tuple-element.64), channel_id=1, source_target_pairs={{0,4},{1,5},{2,6},{3,7},{4,0},{5,1},{6,2},{7,3},{8,12},{9,13},{10,... | collective-permute-start | bytes 6291464 | tf_op jit(solution)/shard_map/ppermute | solution.py:642
  321.9 75.0 %collective-permute-start.15 = (bf16[1,16,32,1024]{3,2,1,0:T(8,128)(2,1)}, bf16[1,16,32,1024]{3,2,1,0:T(8,128)(2,1)}, u32[]{:S(2)}, u32[]{:S(2)}) collective-permute-start(bf16[1,16,32,1024]{3,2,1,0:T(8,128)(2,1)} %get-tuple-element.66), channel_id=1, source_target_pairs={{0,4},{1,5},{2,6},{3,7},{4,0},{5,1},{6,2},{7,3},{8,12},{9,13},{10,... | collective-permute-start | bytes 3145736 | tf_op jit(solution)/shard_map/ppermute | solution.py:642
  354.2 54.3 %collective-permute-start.8 = (bf16[1,16,32,1024]{3,2,1,0:T(8,128)(2,1)}, bf16[1,16,32,1024]{3,2,1,0:T(8,128)(2,1)}, u32[]{:S(2)}, u32[]{:S(2)}) collective-permute-start(bf16[1,16,32,1024]{3,2,1,0:T(8,128)(2,1)} %get-tuple-element.71), channel_id=1, source_target_pairs={{0,4},{1,5},{2,6},{3,7},{4,0},{5,1},{6,2},{7,3},{8,12},{9,13},{10,... | collective-permute-start | bytes 3145736 | tf_op jit(solution)/shard_map/ppermute | solution.py:642
  366.5 11.8 %copy-start.33 = (f32[1,1024]{1,0:T(1,128)S(1)}, f32[1,1024]{1,0:T(1,128)}, u32[]{:S(2)}) copy-start(f32[1,1024]{1,0:T(1,128)} %get-tuple-element.80) | copy-start | bytes 12292
  366.5 11.8 %copy-start.32 = (f32[1,1024]{1,0:T(1,128)S(1)}, f32[1,1024]{1,0:T(1,128)}, u32[]{:S(2)}) copy-start(f32[1,1024]{1,0:T(1,128)} %get-tuple-element.81) | copy-start | bytes 12292
  379.4 6.9 %slice-start = ((s8[4849664]{0:T(1024)(128)(4,1)}), s8[655360]{0:T(1024)(128)(4,1)S(1)}, s32[]{:S(2)}) async-start(s8[4849664]{0:T(1024)(128)(4,1)} %bitcast.522), calls=%async_computation.1 | async-start | bytes 1310720
  380.5 16.2 %collective-permute-start.2 = (bf16[1,16,32,128]{3,2,1,0:T(8,128)(2,1)S(1)}, bf16[1,16,32,128]{3,2,1,0:T(8,128)(2,1)S(1)}, u32[]{:S(2)}, u32[]{:S(2)}) collective-permute-start(bf16[1,16,32,128]{3,2,1,0:T(8,128)(2,1)S(1)} %bitcast.481), channel_id=1, source_target_pairs={{0,4},{1,5},{2,6},{3,7},{4,0},{5,1},{6,2},{7,3},{8,12},{9,13},{10,... | collective-permute-start | bytes 393224 | tf_op jit(solution)/shard_map/ppermute | solution.py:642
  381.1 5.2 slice-start.1
  386.3 5.9 copy-start.15
  393.7 4.1 copy-start.18
  396.8 66.6 %collective-permute-start = (bf16[3,16,32,1024]{3,2,1,0:T(8,128)(2,1)}, bf16[3,16,32,1024]{3,2,1,0:T(8,128)(2,1)S(1)}, u32[]{:S(2)}, u32[]{:S(2)}) collective-permute-start(bf16[3,16,32,1024]{3,2,1,0:T(8,128)(2,1)} %get-tuple-element.73), channel_id=1, source_target_pairs={{0,4},{1,5},{2,6},{3,7},{4,0},{5,1},{6,2},{7,3},{8,12},{9,13},{10,... | collective-permute-start | bytes 9437192 | tf_op jit(solution)/shard_map/ppermute | solution.py:642
  396.9 10.3 %collective-permute-start.3 = (bf16[8,32,128]{2,1,0:T(8,128)(2,1)S(1)}, bf16[8,32,128]{2,1,0:T(8,128)(2,1)S(1)}, u32[]{:S(2)}, u32[]{:S(2)}) collective-permute-start(bf16[8,32,128]{2,1,0:T(8,128)(2,1)S(1)} %bitcast.484), channel_id=1, source_target_pairs={{0,2},{1,3},{2,0},{3,1},{4,6},{5,7},{6,4},{7,5},{8,10},{9,11},{10,... | collective-permute-start | bytes 196616 | tf_op jit(solution)/shard_map/ppermute | solution.py:642
  400.9 25.3 %collective-permute-start.16 = (bf16[8,32,2048]{2,1,0:T(8,128)(2,1)S(1)}, bf16[8,32,2048]{2,1,0:T(8,128)(2,1)S(1)}, u32[]{:S(2)}, u32[]{:S(2)}) collective-permute-start(bf16[8,32,2048]{2,1,0:T(8,128)(2,1)S(1)} %pad_maximum_fusion.2), channel_id=1, source_target_pairs={{0,1},{1,0},{2,3},{3,2},{4,5},{5,4},{6,7},{7,6},{8,9},{9,8},{10,11... | collective-permute-start | bytes 3145736 | tf_op jit(solution)/shard_map/ppermute | solution.py:642
  426.6 14.9 %collective-permute-start.17 = (bf16[4,32,2048]{2,1,0:T(8,128)(2,1)S(1)}, bf16[4,32,2048]{2,1,0:T(8,128)(2,1)S(1)}, u32[]{:S(2)}, u32[]{:S(2)}) collective-permute-start(bf16[4,32,2048]{2,1,0:T(8,128)(2,1)S(1)} %get-tuple-element.221), channel_id=1, source_target_pairs={{0,2},{1,3},{2,0},{3,1},{4,6},{5,7},{6,4},{7,5},{8,10},{9,11},{10,... | collective-permute-start | bytes 1572872 | tf_op jit(solution)/shard_map/ppermute | solution.py:642
  430.1 32.3 %collective-permute-start.22 = (bf16[8,32,2048]{2,1,0:T(8,128)(2,1)S(1)}, bf16[8,32,2048]{2,1,0:T(8,128)(2,1)S(1)}, u32[]{:S(2)}, u32[]{:S(2)}) collective-permute-start(bf16[8,32,2048]{2,1,0:T(8,128)(2,1)S(1)} %pad_maximum_fusion.3), channel_id=1, source_target_pairs={{0,2},{1,3},{2,0},{3,1},{4,6},{5,7},{6,4},{7,5},{8,10},{9,11},{10,... | collective-permute-start | bytes 3145736 | tf_op jit(solution)/shard_map/ppermute | solution.py:642
  441.5 7.0 %copy-start.35 = (bf16[4,4,128,1024]{3,2,1,0:T(8,128)(2,1)S(1)}, bf16[4,4,128,1024]{3,2,1,0:T(8,128)(2,1)}, u32[]{:S(2)}) copy-start(bf16[4,4,128,1024]{3,2,1,0:T(8,128)(2,1)} %get-tuple-element.89) | copy-start | bytes 12582916
  441.6 6.9 %collective-permute-start.18 = (bf16[32,2048]{1,0:T(8,128)(2,1)S(1)}, bf16[32,2048]{1,0:T(8,128)(2,1)S(1)}, u32[]{:S(2)}, u32[]{:S(2)}) collective-permute-start(bf16[32,2048]{1,0:T(8,128)(2,1)S(1)} %get-tuple-element.234), channel_id=1, source_target_pairs={{0,8},{1,9},{2,10},{3,11},{4,12},{5,13},{6,14},{7,15},{8,0},{9,1},... | collective-permute-start | bytes 393224 | tf_op jit(solution)/shard_map/ppermute | solution.py:642
  441.7 10.3 %collective-permute-start.19 = (bf16[32,2048]{1,0:T(8,128)(2,1)S(1)}, bf16[32,2048]{1,0:T(8,128)(2,1)S(1)}, u32[]{:S(2)}, u32[]{:S(2)}) collective-permute-start(bf16[32,2048]{1,0:T(8,128)(2,1)S(1)} %get-tuple-element.236), channel_id=1, source_target_pairs={{0,16},{1,17},{2,18},{3,19},{4,20},{5,21},{6,22},{7,23},{8,24},{9,... | collective-permute-start | bytes 393224 | tf_op jit(solution)/shard_map/ppermute | solution.py:642
  441.8 10.2 %collective-permute-start.20 = (bf16[32,2048]{1,0:T(8,128)(2,1)S(1)}, bf16[32,2048]{1,0:T(8,128)(2,1)S(1)}, u32[]{:S(2)}, u32[]{:S(2)}) collective-permute-start(bf16[32,2048]{1,0:T(8,128)(2,1)S(1)} %get-tuple-element.235), channel_id=1, source_target_pairs={{0,24},{1,25},{2,26},{3,27},{4,28},{5,29},{6,30},{7,31},{8,16},{9,... | collective-permute-start | bytes 393224 | tf_op jit(solution)/shard_map/ppermute | solution.py:642
  448.5 39.7 %collective-permute-start.33 = (bf16[1,16,128,1024]{3,2,1,0:T(8,128)(2,1)S(1)}, bf16[1,16,128,1024]{3,2,1,0:T(8,128)(2,1)S(1)}, u32[]{:S(2)}, u32[]{:S(2)}) collective-permute-start(bf16[1,16,128,1024]{3,2,1,0:T(8,128)(2,1)S(1)} %bitcast.509), channel_id=1, source_target_pairs={{0,4},{1,5},{2,6},{3,7},{4,0},{5,1},{6,2},{7,3},{8,12},{9,13},{10,... | collective-permute-start | bytes 12582920 | tf_op jit(solution)/shard_map/ppermute | solution.py:642
  452.0 39.5 %collective-permute-start.27 = (bf16[1,16,32,4096]{3,2,1,0:T(8,128)(2,1)}, bf16[1,16,32,4096]{3,2,1,0:T(8,128)(2,1)S(1)}, u32[]{:S(2)}, u32[]{:S(2)}) collective-permute-start(bf16[1,16,32,4096]{3,2,1,0:T(8,128)(2,1)} %bitcast.121), channel_id=1, source_target_pairs={{0,4},{1,5},{2,6},{3,7},{4,0},{5,1},{6,2},{7,3},{8,12},{9,13},{10,... | collective-permute-start | bytes 12582920 | tf_op jit(solution)/shard_map/ppermute | solution.py:642
  462.7 12.4 %collective-permute-start.23 = (bf16[4,32,2048]{2,1,0:T(8,128)(2,1)S(1)}, bf16[4,32,2048]{2,1,0:T(8,128)(2,1)S(1)}, u32[]{:S(2)}, u32[]{:S(2)}) collective-permute-start(bf16[4,32,2048]{2,1,0:T(8,128)(2,1)S(1)} %get-tuple-element.215), channel_id=1, source_target_pairs={{0,1},{1,0},{2,3},{3,2},{4,5},{5,4},{6,7},{7,6},{8,9},{9,8},{10,11... | collective-permute-start | bytes 1572872 | tf_op jit(solution)/shard_map/ppermute | solution.py:642
  475.1 13.0 %copy-start.7 = (bf16[4,4,128,1024]{3,2,1,0:T(8,128)(2,1)S(1)}, bf16[4,4,128,1024]{3,2,1,0:T(8,128)(2,1)}, u32[]{:S(2)}) copy-start(bf16[4,4,128,1024]{3,2,1,0:T(8,128)(2,1)} %get-tuple-element.88) | copy-start | bytes 12582916
  475.2 7.1 %collective-permute-start.24 = (bf16[32,2048]{1,0:T(8,128)(2,1)S(1)}, bf16[32,2048]{1,0:T(8,128)(2,1)S(1)}, u32[]{:S(2)}, u32[]{:S(2)}) collective-permute-start(bf16[32,2048]{1,0:T(8,128)(2,1)S(1)} %get-tuple-element.231), channel_id=1, source_target_pairs={{0,8},{1,9},{2,10},{3,11},{4,12},{5,13},{6,14},{7,15},{8,0},{9,1},... | collective-permute-start | bytes 393224 | tf_op jit(solution)/shard_map/ppermute | solution.py:642
  475.3 10.9 %collective-permute-start.25 = (bf16[32,2048]{1,0:T(8,128)(2,1)S(1)}, bf16[32,2048]{1,0:T(8,128)(2,1)S(1)}, u32[]{:S(2)}, u32[]{:S(2)}) collective-permute-start(bf16[32,2048]{1,0:T(8,128)(2,1)S(1)} %get-tuple-element.233), channel_id=1, source_target_pairs={{0,16},{1,17},{2,18},{3,19},{4,20},{5,21},{6,22},{7,23},{8,24},{9,... | collective-permute-start | bytes 393224 | tf_op jit(solution)/shard_map/ppermute | solution.py:642
  475.4 12.0 %collective-permute-start.26 = (bf16[32,2048]{1,0:T(8,128)(2,1)S(1)}, bf16[32,2048]{1,0:T(8,128)(2,1)S(1)}, u32[]{:S(2)}, u32[]{:S(2)}) collective-permute-start(bf16[32,2048]{1,0:T(8,128)(2,1)S(1)} %get-tuple-element.232), channel_id=1, source_target_pairs={{0,24},{1,25},{2,26},{3,27},{4,28},{5,29},{6,30},{7,31},{8,16},{9,... | collective-permute-start | bytes 393224 | tf_op jit(solution)/shard_map/ppermute | solution.py:642
  482.3 26.0 %collective-permute-start.9 = (bf16[8,32,2048]{2,1,0:T(8,128)(2,1)S(1)}, bf16[8,32,2048]{2,1,0:T(8,128)(2,1)S(1)}, u32[]{:S(2)}, u32[]{:S(2)}) collective-permute-start(bf16[8,32,2048]{2,1,0:T(8,128)(2,1)S(1)} %pad_maximum_fusion.1), channel_id=1, source_target_pairs={{0,1},{1,0},{2,3},{3,2},{4,5},{5,4},{6,7},{7,6},{8,9},{9,8},{10,11... | collective-permute-start | bytes 3145736 | tf_op jit(solution)/shard_map/ppermute | solution.py:642
  486.1 26.0 %collective-permute-start.1 = (bf16[8,32,2048]{2,1,0:T(8,128)(2,1)S(1)}, bf16[8,32,2048]{2,1,0:T(8,128)(2,1)S(1)}, u32[]{:S(2)}, u32[]{:S(2)}) collective-permute-start(bf16[8,32,2048]{2,1,0:T(8,128)(2,1)S(1)} %pad_maximum_fusion), channel_id=1, source_target_pairs={{0,2},{1,3},{2,0},{3,1},{4,6},{5,7},{6,4},{7,5},{8,10},{9,11},{10,... | collective-permute-start | bytes 3145736 | tf_op jit(solution)/shard_map/ppermute | solution.py:642
  488.1 3.4 copy-start.6
  490.6 87.3 %collective-permute-start.34 = (bf16[8,128,1024]{2,1,0:T(8,128)(2,1)S(1)}, bf16[8,128,1024]{2,1,0:T(8,128)(2,1)S(1)}, u32[]{:S(2)}, u32[]{:S(2)}) collective-permute-start(bf16[8,128,1024]{2,1,0:T(8,128)(2,1)S(1)} %bitcast.458), channel_id=1, source_target_pairs={{0,2},{1,3},{2,0},{3,1},{4,6},{5,7},{6,4},{7,5},{8,10},{9,11},{10,... | collective-permute-start | bytes 6291464 | tf_op jit(solution)/shard_map/ppermute | solution.py:642
  493.3 85.5 %collective-permute-start.28 = (bf16[8,32,4096]{2,1,0:T(8,128)(2,1)S(1)}, bf16[8,32,4096]{2,1,0:T(8,128)(2,1)S(1)}, u32[]{:S(2)}, u32[]{:S(2)}) collective-permute-start(bf16[8,32,4096]{2,1,0:T(8,128)(2,1)S(1)} %get-tuple-element.199), channel_id=1, source_target_pairs={{0,1},{1,0},{2,3},{3,2},{4,5},{5,4},{6,7},{7,6},{8,9},{9,8},{10,11... | collective-permute-start | bytes 6291464 | tf_op jit(solution)/shard_map/ppermute | solution.py:642
  508.7 53.7 %collective-permute-start.10 = (bf16[4,32,2048]{2,1,0:T(8,128)(2,1)S(1)}, bf16[4,32,2048]{2,1,0:T(8,128)(2,1)S(1)}, u32[]{:S(2)}, u32[]{:S(2)}) collective-permute-start(bf16[4,32,2048]{2,1,0:T(8,128)(2,1)S(1)} %get-tuple-element.225), channel_id=1, source_target_pairs={{0,2},{1,3},{2,0},{3,1},{4,6},{5,7},{6,4},{7,5},{8,10},{9,11},{10,... | collective-permute-start | bytes 1572872 | tf_op jit(solution)/shard_map/ppermute | solution.py:642
  512.4 50.3 %collective-permute-start.4 = (bf16[4,32,2176]{2,1,0:T(8,128)(2,1)S(1)}, bf16[4,32,2176]{2,1,0:T(8,128)(2,1)S(1)}, u32[]{:S(2)}, u32[]{:S(2)}) collective-permute-start(bf16[4,32,2176]{2,1,0:T(8,128)(2,1)S(1)} %pad_maximum_fusion.4), channel_id=1, source_target_pairs={{0,1},{1,0},{2,3},{3,2},{4,5},{5,4},{6,7},{7,6},{8,9},{9,8},{10,11... | collective-permute-start | bytes 1671176 | tf_op jit(solution)/shard_map/ppermute | solution.py:642
  562.5 5.4 collective-permute-start.11
  562.6 12.7 %collective-permute-start.12 = (bf16[32,2048]{1,0:T(8,128)(2,1)S(1)}, bf16[32,2048]{1,0:T(8,128)(2,1)S(1)}, u32[]{:S(2)}, u32[]{:S(2)}) collective-permute-start(bf16[32,2048]{1,0:T(8,128)(2,1)S(1)} %get-tuple-element.239), channel_id=1, source_target_pairs={{0,16},{1,17},{2,18},{3,19},{4,20},{5,21},{6,22},{7,23},{8,24},{9,... | collective-permute-start | bytes 393224 | tf_op jit(solution)/shard_map/ppermute | solution.py:642
  562.7 12.6 %collective-permute-start.13 = (bf16[32,2048]{1,0:T(8,128)(2,1)S(1)}, bf16[32,2048]{1,0:T(8,128)(2,1)S(1)}, u32[]{:S(2)}, u32[]{:S(2)}) collective-permute-start(bf16[32,2048]{1,0:T(8,128)(2,1)S(1)} %get-tuple-element.238), channel_id=1, source_target_pairs={{0,24},{1,25},{2,26},{3,27},{4,28},{5,29},{6,30},{7,31},{8,16},{9,... | collective-permute-start | bytes 393224 | tf_op jit(solution)/shard_map/ppermute | solution.py:642
  567.9 13.5 %collective-permute-start.5 = (bf16[32,2176]{1,0:T(8,128)(2,1)S(1)}, bf16[32,2176]{1,0:T(8,128)(2,1)S(1)}, u32[]{:S(2)}, u32[]{:S(2)}) collective-permute-start(bf16[32,2176]{1,0:T(8,128)(2,1)S(1)} %get-tuple-element.228), channel_id=1, source_target_pairs={{0,8},{1,9},{2,10},{3,11},{4,12},{5,13},{6,14},{7,15},{8,0},{9,1},... | collective-permute-start | bytes 417800 | tf_op jit(solution)/shard_map/ppermute | solution.py:642
  575.2 7.9 %collective-permute-start.6 = (bf16[32,2176]{1,0:T(8,128)(2,1)S(1)}, bf16[32,2176]{1,0:T(8,128)(2,1)S(1)}, u32[]{:S(2)}, u32[]{:S(2)}) collective-permute-start(bf16[32,2176]{1,0:T(8,128)(2,1)S(1)} %get-tuple-element.230), channel_id=1, source_target_pairs={{0,16},{1,17},{2,18},{3,19},{4,20},{5,21},{6,22},{7,23},{8,24},{9,... | collective-permute-start | bytes 417800 | tf_op jit(solution)/shard_map/ppermute | solution.py:642
  575.2 7.9 %collective-permute-start.7 = (bf16[32,2176]{1,0:T(8,128)(2,1)S(1)}, bf16[32,2176]{1,0:T(8,128)(2,1)S(1)}, u32[]{:S(2)}, u32[]{:S(2)}) collective-permute-start(bf16[32,2176]{1,0:T(8,128)(2,1)S(1)} %get-tuple-element.229), channel_id=1, source_target_pairs={{0,24},{1,25},{2,26},{3,27},{4,28},{5,29},{6,30},{7,31},{8,16},{9,... | collective-permute-start | bytes 417800 | tf_op jit(solution)/shard_map/ppermute | solution.py:642
  578.4 14.9 %collective-permute-start.35 = (bf16[4,128,1024]{2,1,0:T(8,128)(2,1)S(1)}, bf16[4,128,1024]{2,1,0:T(8,128)(2,1)S(1)}, u32[]{:S(2)}, u32[]{:S(2)}) collective-permute-start(bf16[4,128,1024]{2,1,0:T(8,128)(2,1)S(1)} %fusion.44), channel_id=1, source_target_pairs={{0,1},{1,0},{2,3},{3,2},{4,5},{5,4},{6,7},{7,6},{8,9},{9,8},{10,11... | collective-permute-start | bytes 3145736 | tf_op jit(solution)/shard_map/ppermute | solution.py:642
  579.6 18.5 %collective-permute-start.29 = (bf16[4,32,4096]{2,1,0:T(8,128)(2,1)S(1)}, bf16[4,32,4096]{2,1,0:T(8,128)(2,1)S(1)}, u32[]{:S(2)}, u32[]{:S(2)}) collective-permute-start(bf16[4,32,4096]{2,1,0:T(8,128)(2,1)S(1)} %get-tuple-element.201), channel_id=1, source_target_pairs={{0,2},{1,3},{2,0},{3,1},{4,6},{5,7},{6,4},{7,5},{8,10},{9,11},{10,... | collective-permute-start | bytes 3145736 | tf_op jit(solution)/shard_map/ppermute | solution.py:642
  593.5 11.4 %collective-permute-start.36 = (bf16[128,1024]{1,0:T(8,128)(2,1)S(1)}, bf16[128,1024]{1,0:T(8,128)(2,1)S(1)}, u32[]{:S(2)}, u32[]{:S(2)}) collective-permute-start(bf16[128,1024]{1,0:T(8,128)(2,1)S(1)} %get-tuple-element.208), channel_id=1, source_target_pairs={{0,8},{1,9},{2,10},{3,11},{4,12},{5,13},{6,14},{7,15},{8,0},{9,1},... | collective-permute-start | bytes 786440 | tf_op jit(solution)/shard_map/ppermute | solution.py:642
  595.6 23.6 %collective-permute-start.37 = (bf16[128,1024]{1,0:T(8,128)(2,1)S(1)}, bf16[128,1024]{1,0:T(8,128)(2,1)S(1)}, u32[]{:S(2)}, u32[]{:S(2)}) collective-permute-start(bf16[128,1024]{1,0:T(8,128)(2,1)S(1)} %get-tuple-element.210), channel_id=1, source_target_pairs={{0,16},{1,17},{2,18},{3,19},{4,20},{5,21},{6,22},{7,23},{8,24},{9,... | collective-permute-start | bytes 786440 | tf_op jit(solution)/shard_map/ppermute | solution.py:642
  596.5 22.7 %collective-permute-start.38 = (bf16[128,1024]{1,0:T(8,128)(2,1)S(1)}, bf16[128,1024]{1,0:T(8,128)(2,1)S(1)}, u32[]{:S(2)}, u32[]{:S(2)}) collective-permute-start(bf16[128,1024]{1,0:T(8,128)(2,1)S(1)} %get-tuple-element.209), channel_id=1, source_target_pairs={{0,24},{1,25},{2,26},{3,27},{4,28},{5,29},{6,30},{7,31},{8,16},{9,... | collective-permute-start | bytes 786440 | tf_op jit(solution)/shard_map/ppermute | solution.py:642
  598.1 30.9 %copy-start.1 = (bf16[1,512,1024]{2,1,0:T(8,128)(2,1)S(1)}, bf16[1,512,1024]{2,1,0:T(8,128)(2,1)}, u32[]{:S(2)}) copy-start(bf16[1,512,1024]{2,1,0:T(8,128)(2,1)} %param.18) | copy-start | bytes 3145732
  598.3 22.0 %collective-permute-start.30 = (bf16[32,4096]{1,0:T(8,128)(2,1)S(1)}, bf16[32,4096]{1,0:T(8,128)(2,1)S(1)}, u32[]{:S(2)}, u32[]{:S(2)}) collective-permute-start(bf16[32,4096]{1,0:T(8,128)(2,1)S(1)} %get-tuple-element.211), channel_id=1, source_target_pairs={{0,8},{1,9},{2,10},{3,11},{4,12},{5,13},{6,14},{7,15},{8,0},{9,1},... | collective-permute-start | bytes 786440 | tf_op jit(solution)/shard_map/ppermute | solution.py:642
  599.4 28.6 %collective-permute-start.31 = (bf16[32,4096]{1,0:T(8,128)(2,1)S(1)}, bf16[32,4096]{1,0:T(8,128)(2,1)S(1)}, u32[]{:S(2)}, u32[]{:S(2)}) collective-permute-start(bf16[32,4096]{1,0:T(8,128)(2,1)S(1)} %get-tuple-element.213), channel_id=1, source_target_pairs={{0,16},{1,17},{2,18},{3,19},{4,20},{5,21},{6,22},{7,23},{8,24},{9,... | collective-permute-start | bytes 786440 | tf_op jit(solution)/shard_map/ppermute | solution.py:642
  605.0 23.1 %collective-permute-start.32 = (bf16[32,4096]{1,0:T(8,128)(2,1)S(1)}, bf16[32,4096]{1,0:T(8,128)(2,1)S(1)}, u32[]{:S(2)}, u32[]{:S(2)}) collective-permute-start(bf16[32,4096]{1,0:T(8,128)(2,1)S(1)} %get-tuple-element.212), channel_id=1, source_target_pairs={{0,24},{1,25},{2,26},{3,27},{4,28},{5,29},{6,30},{7,31},{8,16},{9,... | collective-permute-start | bytes 786440 | tf_op jit(solution)/shard_map/ppermute | solution.py:642
  (15 other events, 29.1 us)
Sparse Core Ops, SparseCore 0:
  77.5 126.7 all-gather.2
where the time goes:
time: 642 us; the launch traced here: 636 us
  Pallas kernels  299 us (47%)
  waiting for transfers between devices  163 us (25%)
  matrix products  52.6 us (8%)
  starting transfers between devices  38.6 us (6%)
  local copies, waits for them, and re-layouts  33.9 us (5%)
  other arithmetic  32.9 us (5%)
  between operations  16 us (2%)
    ppermute x39, waiting for transfers between devices, swap(): return lax.ppermute(values, AXES, [(i, i ^ bit) for i in range(devices)])  163 us
    pallas_call x2, Pallas kernels, gather(): pl.pallas_call(functools.partial(gather_kernel, devices, lanes, tracks),...  114 us
    pallas_call x1, Pallas kernels, feed(): pl.pallas_call(functools.partial(feed_kernel, devices, lanes), grid_spec=...  38.7 us
    ppermute x39, starting transfers between devices, swap(): return lax.ppermute(values, AXES, [(i, i ^ bit) for i in range(devices)])  38.5 us
    pallas_call x1, Pallas kernels, cross_backward(): pl.pallas_call(cross_backward_kernel, grid_spec=pltpu.PrefetchScalarGridS...  34.9 us
    pallas_call x5, Pallas kernels, weight_grad(): pl.pallas_call(functools.partial(weight_grad_kernel, devices, lanes), gri...  33.8 us
    pallas_call x1, Pallas kernels, cross_forward(): pl.pallas_call(cross_forward_kernel, grid_spec=pltpu.PrefetchScalarGridSp...  29.9 us
    dot_general x6, matrix products, product(): return jnp.dot(left, right, preferred_element_type=f32)  21.7 us
  transfers between devices with their start and end apart: 40, of which 18 were waited for; matrix products, arithmetic and copies ran while one was open for 16% of the time, Pallas kernels for 31%

commit v1 on v0

--- a/solution.py
+++ b/solution.py
@@ -337,61 +337,144 @@
     )(count, query, kv, kv, grads, totals)
 
 
-def put_rows(me, devices, lanes, left, staged):
+def here(lanes):
+    return lax.axis_index("dp") * lanes + lax.axis_index("fsdp")
+
+
+def bit_of(number, bit):
+    return (number // (1 << bit)) % 2
+
+
+def stages(devices, lanes, way):
+    return list(way) + list(range(lanes.bit_length(), devices.bit_length() - 1))
+
+
+def place_of(relative, devices, lanes, way):
+    place = 0
+    for bit in stages(devices, lanes, way)[1:]:
+        place = place * 2 + bit_of(relative, bit)
+    return place
+
+
+def put_rows(me, devices, lanes, way, left, staged):
     flipped = left.astype(f32).T
     depth = flipped.shape[0] // devices
     for block in range(devices):
         relative = block ^ me
-        other = (relative // lanes) % 2
-        place = (relative // (2 * lanes)) * lanes + relative % lanes + (1 - other) * (devices // 2)
+        quarter = 2 * (1 - bit_of(relative, lanes.bit_length() - 1)) + (1 - bit_of(relative, way[0]))
+        place = quarter * (devices // 4) + place_of(relative, devices, lanes, way)
         start = pl.multiple_of(place * depth, depth)
         staged[pl.ds(start, depth), :] = flipped[block * depth : (block + 1) * depth, :]
 
 
-def put_halves(total, send, keep):
+def greet(partner):
+    barrier = pltpu.get_barrier_semaphore()
+    pl.semaphore_signal(barrier, inc=1, device_id=partner, device_id_type=pl.DeviceIdType.MESH)
+    pl.semaphore_wait(barrier, 1)
+
+
+def other_core(me, lanes):
+    other = me ^ lanes
+    return (other // lanes, lax.rem(other, lanes))
+
+
+def to_core(partner, source, target, send_sem, recv_sem):
+    return pltpu.make_async_remote_copy(
+        src_ref=source,
+        dst_ref=target,
+        send_sem=send_sem,
+        recv_sem=recv_sem,
+        device_id=partner,
+        device_id_type=pl.DeviceIdType.MESH,
+    )
+
+
+def put_halves(total, out, keep):
     half = total.shape[0] // 2
-    send[...] = total[:half, :].astype(bf16).reshape(send.shape)
+    out[...] = total[:half, :].astype(bf16).reshape(out.shape)
     keep[...] = total[half:, :].astype(bf16).reshape(keep.shape)
 
 
-def weight_grad_kernel(devices, lanes, me_ref, left, right, send, keep, staged, flipped):
-    @pl.when((pl.program_id(0) == 0) & (pl.program_id(1) == 0))
+def weight_grad_kernel(devices, lanes, way, given, *refs):
+    left, right = refs[:2]
+    out, keep, staged, flipped, sent, own, came, send_sem, recv_sem = refs[2 + given :]
+    step, steps = pl.program_id(0), pl.num_programs(0) - 1
+    me = here(lanes)
+    partner = other_core(me, lanes)
+    half = flipped.shape[1] // 2
+
+    @pl.when(step == 0)
     def _():
+        greet(partner)
         for part in range(left.shape[0]):
-            put_rows(me_ref[0], devices, lanes, left[part], staged)
+            put_rows(me, devices, lanes, way, left[part], staged)
             flipped[part] = staged[...].astype(bf16)
 
-    total = product(flipped[0], right[0, 0])
-    for part in range(1, left.shape[0]):
-        total += product(flipped[part], right[0, part])
-    put_halves(total, send, keep)
-
-
-def weight_grad(me, devices, lanes, left, right):
+    def copy(at):
+        return to_core(partner, sent.at[at % 2], came.at[at], send_sem.at[at], recv_sem.at[at])
+
+    @pl.when(step < steps)
+    def _():
+        def rows(low):
+            total = product(flipped[0, low : low + half, :], right[0, 0])
+            for part in range(1, left.shape[0]):
+                total += product(flipped[part, low : low + half, :], right[0, part])
+            return total
+
+        sent[step % 2] = rows(0).astype(bf16)
+        own[step % 2] = rows(half)
+        copy(step).start()
+
+    @pl.when(step > 0)
+    def _():
+        copy(step - 1).wait()
+        put_halves(own[(step - 1) % 2] + came[step - 1].astype(f32), out, keep)
+
+
+def weight_grad(number, devices, lanes, way, left, right, columns, first=0, into=(), only=None):
     parts, rows, depth = left.shape
-    kinds, columns = right.shape[0], right.shape[3]
+    low, high = only or (0, right.shape[0])
+    kinds, width = high - low, right.shape[3]
     wide = 512
-    steps = columns // wide
-    block = (1, devices // 2, depth // devices, wide)
-    spec = pl.BlockSpec(block, lambda i, j, m: (i, 0, 0, j))
-    shape = jax.ShapeDtypeStruct((kinds, devices // 2, depth // devices, columns), bf16)
+    across = width // wide
+    steps = kinds * across
+    block = (devices // 4, depth // devices, wide)
+    spec = pl.BlockSpec(block, lambda s: (0, 0, first // wide + jnp.maximum(s - 1, 0)))
+    shape = jax.ShapeDtypeStruct((devices // 4, depth // devices, columns), bf16)
+
+    def source(s):
+        s = jnp.minimum(s, steps - 1)
+        return (low + s // across, 0, 0, s % across)
+
     return pl.pallas_call(
-        functools.partial(weight_grad_kernel, devices, lanes),
-        grid_spec=pltpu.PrefetchScalarGridSpec(
-            num_scalar_prefetch=1,
-            grid=(kinds, steps),
-            in_specs=[
-                pl.BlockSpec((parts, rows, depth), lambda i, j, m: (0, 0, 0)),
-                pl.BlockSpec((1, parts, rows, wide), lambda i, j, m: (i, 0, 0, j)),
-            ],
-            out_specs=[spec, spec],
-            scratch_shapes=[pltpu.VMEM((depth, rows), f32), pltpu.VMEM((parts, depth, rows), bf16)],
+        functools.partial(weight_grad_kernel, devices, lanes, way, len(into)),
+        grid=(steps + 1,),
+        in_specs=[
+            pl.BlockSpec((parts, rows, depth), lambda s: (0, 0, 0)),
+            pl.BlockSpec((1, parts, rows, wide), source),
+        ]
+        + [pl.BlockSpec(memory_space=pltpu.HBM)] * len(into),
+        out_specs=[spec, spec],
+        scratch_shapes=[
+            pltpu.VMEM((depth, rows), f32),
+            pltpu.VMEM((parts, depth, rows), bf16),
+            pltpu.VMEM((2, depth // 2, wide), bf16),
+            pltpu.VMEM((2, depth // 2, wide), f32),
+            pltpu.VMEM((steps, depth // 2, wide), bf16),
+            pltpu.SemaphoreType.DMA((steps,)),
+            pltpu.SemaphoreType.DMA((steps,)),
+        ],
+        out_shape=[shape, shape],
+        input_output_aliases={2 + i: i for i in range(len(into))},
+        compiler_params=pltpu.CompilerParams(
+            dimension_semantics=("arbitrary",),
+            vmem_limit_bytes=VMEM,
+            collective_id=number,
+            has_side_effects=True,
         ),
-        out_shape=[shape, shape],
-        compiler_params=params(2),
         name="weight_grad",
         cost_estimate=cost(3 * kinds * parts),
-    )(me, left, right)
+    )(left, right, *into)
 
 
 def norm_grad_kernel(d_ref, w_ref, unit, inverse, gain, g_ref, out, low, gain_out, total):
@@ -441,60 +524,106 @@
 
 
 def feed_kernel(
-    devices, lanes, me_ref, x_ref, g_ref, gain_ref, up_ref, down_ref,
-    out, gx, ggain, up_send, up_keep, down_send, down_keep,
+    devices, lanes, ways, x_ref, g_ref, gain_ref, up_ref, down_ref,
+    out, gx, low_gx, ggain, up_out, up_keep, down_out, down_keep,
     unit, inverse, hidden, staged, flipped, total, back,
+    up_sent, up_own, up_came, down_sent, down_own, down_came,
+    up_send_sem, up_recv_sem, down_send_sem, down_recv_sem,
 ):
-    step = pl.program_id(0)
-    me = me_ref[0]
+    step, groups = pl.program_id(0), pl.num_programs(0) - 1
+    me = here(lanes)
+    partner = other_core(me, lanes)
+    core, low, high = (me // lanes) % 2, me % lanes, me // (2 * lanes)
 
     @pl.when(step == 0)
     def _():
+        greet(partner)
         h, u, i = normed(x_ref[...], gain_ref[...])
         unit[...] = u
         inverse[...] = i
         hidden[...] = h.astype(bf16)
-        put_rows(me, devices, lanes, h, staged)
+        put_rows(me, devices, lanes, ways[0], h, staged)
         flipped[...] = staged[...].astype(bf16)
         total[...] = jnp.zeros_like(total)
         back[...] = jnp.zeros_like(back)
 
-    g = g_ref[...]
-    up = up_ref[...].reshape(-1, up_ref.shape[-1])
-    down = down_ref[...].reshape(-1, down_ref.shape[-1])
-    inner = product(hidden[...], up)
-    share = 0.5 + 0.5 * lax.erf(inner * (0.5**0.5))
-    slope = share + inner * (jnp.exp(-0.5 * inner * inner) * 0.3989422804014327)
-    active = (inner * share).astype(bf16)
-    total[...] += product(active, down)
-    change = (product_t(g, down) * slope).astype(bf16)
-    back[...] += product_t(change, up)
-    put_halves(product(flipped[...], change), up_send, up_keep)
-    grad_down = product_rows(active, g)
-    depth = grad_down.shape[0] // lanes
-    low = me % lanes
-
-    def put(target):
-        for block in range(lanes):
-            target[0, block ^ low] = grad_down[block * depth : (block + 1) * depth, :].astype(bf16)
-
-    @pl.when(step % 2 == 1)
+    def up_copy(at):
+        return to_core(partner, up_sent.at[at % 2], up_came.at[at], up_send_sem.at[at], up_recv_sem.at[at])
+
+    def down_copy(at):
+        return to_core(partner, down_sent, down_came.at[at], down_send_sem.at[at], down_recv_sem.at[at])
+
+    @pl.when(step < groups)
     def _():
-        put(down_send)
-
-    @pl.when(step % 2 == 0)
-    def _():
-        put(down_keep)
-
-    @pl.when(step == pl.num_programs(0) - 1)
+        g = g_ref[...]
+        up = up_ref[...].reshape(-1, up_ref.shape[-1])
+        down = down_ref[...].reshape(-1, down_ref.shape[-1])
+        inner = product(hidden[...], up)
+        share = 0.5 + 0.5 * lax.erf(inner * (0.5**0.5))
+        slope = share + inner * (jnp.exp(-0.5 * inner * inner) * 0.3989422804014327)
+        active = (inner * share).astype(bf16)
+        change = (product_t(g, down) * slope).astype(bf16)
+        half = flipped.shape[0] // 2
+        up_sent[step % 2] = product(flipped[:half, :], change).astype(bf16)
+        grad_down = product_rows(active, g)
+
+        @pl.when(step % 2 != core)
+        def _():
+            down_sent[...] = grad_down.astype(bf16)
+
+        @pl.when(step % 2 == core)
+        def _():
+            down_own[...] = grad_down
+
+        up_own[step % 2] = product(flipped[half:, :], change)
+        total[...] += product(active, down)
+        back[...] += product_t(change, up)
+        up_copy(step).start()
+
+        @pl.when(step % 2 != core)
+        def _():
+            down_copy(step // 2).start()
+
+    @pl.when(step == groups)
     def _():
         out[...] = (x_ref[...] + total[...]).astype(bf16)
         gx_norm, gain_grad = norm_back(unit[...], inverse[...], gain_ref[...], back[...])
-        gx[...] = g_ref[...].astype(f32) + gx_norm
+        result = g_ref[...].astype(f32) + gx_norm
+        gx[...] = result
+        low_gx[...] = result.astype(bf16)
         ggain[...] = gain_grad[None, :]
 
-
-def feed(me, devices, lanes, x, g, gain, weights):
+    @pl.when(step > 0)
+    def _():
+        before = step - 1
+        up_copy(before).wait()
+        put_halves(up_own[before % 2] + up_came[before].astype(f32), up_out, up_keep)
+
+        @pl.when(before % 2 != core)
+        def _():
+            down_copy(before // 2).wait_send()
+
+        @pl.when(before % 2 == core)
+        def _():
+            down_copy(before // 2).wait_recv()
+            sums = down_own[...] + down_came[before // 2].astype(f32)
+            depth = sums.shape[0] // lanes
+            for block in range(lanes):
+                relative = (block ^ low) + 2 * lanes * ((before // 2) ^ high)
+                place = place_of(relative, devices, lanes, ways[1])
+                piece = sums[block * depth : (block + 1) * depth, :].astype(bf16)
+                goes = bit_of(relative, ways[1][0]) == 1
+
+                @pl.when(goes)
+                def _(place=place, piece=piece):
+                    down_out[place] = piece
+
+                @pl.when(jnp.logical_not(goes))
+                def _(place=place, piece=piece):
+                    down_keep[place] = piece
+
+
+def feed(number, devices, lanes, ways, x, g, gain, weights):
     rows, width = x.shape
     pieces, depth = weights.shape[2:4]
     hidden = pieces * width
@@ -502,57 +631,67 @@
     tile = hidden // groups
     across = width // tile
 
-    def group(s, m):
-        return s ^ (m[0] // lanes)
+    def group(s):
+        return jnp.minimum(s, groups - 1)
 
     def whole(shape):
-        return pl.BlockSpec(shape, lambda s, m: (0,) * len(shape))
-
-    up_block = pl.BlockSpec((devices // 2, width // devices, tile), lambda s, m: (0, 0, group(s, m)))
-    down_block = pl.BlockSpec((1, lanes, tile // lanes, width), lambda s, m: (s // 2, 0, 0, 0))
-    up_shape = jax.ShapeDtypeStruct((devices // 2, width // devices, hidden), bf16)
-    down_shape = jax.ShapeDtypeStruct((groups // 2, lanes, tile // lanes, width), bf16)
+        return pl.BlockSpec(shape, lambda s: (0,) * len(shape))
+
+    up_block = pl.BlockSpec((devices // 4, depth, tile), lambda s: (0, 0, jnp.maximum(s - 1, 0)))
+    up_shape = jax.ShapeDtypeStruct((devices // 4, depth, hidden), bf16)
+    down_shape = jax.ShapeDtypeStruct((devices // 4, hidden // devices, width), bf16)
     return pl.pallas_call(
-        functools.partial(feed_kernel, devices, lanes),
-        grid_spec=pltpu.PrefetchScalarGridSpec(
-            num_scalar_prefetch=1,
-            grid=(groups,),
-            in_specs=[
-                whole((rows, width)),
-                whole((rows, width)),
-                whole((1, width)),
-                pl.BlockSpec(
-                    (devices, None, None, depth, tile),
-                    lambda s, m: (0, 0, group(s, m) // across, 0, group(s, m) % across),
-                ),
-                pl.BlockSpec(
-                    (lanes, None, pieces, depth, width), lambda s, m: (group(s, m), 1, 0, 0, 0)
-                ),
-            ],
-            out_specs=[
-                whole((rows, width)), whole((rows, width)), whole((1, width)),
-                up_block, up_block, down_block, down_block,
-            ],
-            scratch_shapes=[
-                pltpu.VMEM((rows, width), f32),
-                pltpu.VMEM((rows, 1), f32),
-                pltpu.VMEM((rows, width), bf16),
-                pltpu.VMEM((width, rows), f32),
-                pltpu.VMEM((width, rows), bf16),
-                pltpu.VMEM((rows, width), f32),
-                pltpu.VMEM((rows, width), f32),
-            ],
-        ),
+        functools.partial(feed_kernel, devices, lanes, ways),
+        grid=(groups + 1,),
+        in_specs=[
+            whole((rows, width)),
+            whole((rows, width)),
+            whole((1, width)),
+            pl.BlockSpec(
+                (devices, None, None, depth, tile),
+                lambda s: (0, 0, group(s) // across, 0, group(s) % across),
+            ),
+            pl.BlockSpec((lanes, None, pieces, depth, width), lambda s: (group(s), 1, 0, 0, 0)),
+        ],
+        out_specs=[
+            whole((rows, width)), whole((rows, width)), whole((rows, width)), whole((1, width)),
+            up_block, up_block, whole(down_shape.shape), whole(down_shape.shape),
+        ],
+        scratch_shapes=[
+            pltpu.VMEM((rows, width), f32),
+            pltpu.VMEM((rows, 1), f32),
+            pltpu.VMEM((rows, width), bf16),
+            pltpu.VMEM((width, rows), f32),
+            pltpu.VMEM((width, rows), bf16),
+            pltpu.VMEM((rows, width), f32),
+            pltpu.VMEM((rows, width), f32),
+            pltpu.VMEM((2, width // 2, tile), bf16),
+            pltpu.VMEM((2, width // 2, tile), f32),
+            pltpu.VMEM((groups, width // 2, tile), bf16),
+            pltpu.VMEM((tile, width), bf16),
+            pltpu.VMEM((tile, width), f32),
+            pltpu.VMEM((groups // 2, tile, width), bf16),
+            pltpu.SemaphoreType.DMA((groups,)),
+            pltpu.SemaphoreType.DMA((groups,)),
+            pltpu.SemaphoreType.DMA((groups // 2,)),
+            pltpu.SemaphoreType.DMA((groups // 2,)),
+        ],
         out_shape=[
             jax.ShapeDtypeStruct((rows, width), bf16),
             jax.ShapeDtypeStruct((rows, width), f32),
+            jax.ShapeDtypeStruct((rows, width), bf16),
             jax.ShapeDtypeStruct((1, width), f32),
             up_shape, up_shape, down_shape, down_shape,
         ],
-        compiler_params=params(1),
+        compiler_params=pltpu.CompilerParams(
+            dimension_semantics=("arbitrary",),
+            vmem_limit_bytes=VMEM,
+            collective_id=number,
+            has_side_effects=True,
+        ),
         name="feed",
-        cost_estimate=cost(45),
-    )(me, x, g, gain, weights, weights)
+        cost_estimate=cost(40),
+    )(x, g, gain, weights, weights)
 
 
 def gather_kernel(devices, lanes, tracks, x_ref, out, own_sem, send_sem, recv_sem):
@@ -642,38 +781,36 @@
     return lax.ppermute(values, AXES, [(i, i ^ bit) for i in range(devices)])
 
 
-def cross_core(halves, devices, lanes):
-    send, keep = (half.reshape(-1, devices // 2, *half.shape[-2:]) for half in halves)
-    arrived = swap(send, devices, lanes)
-    return [(keep[kind], arrived[kind]) for kind in range(keep.shape[0])]
-
-
-def halved(pairs, devices, left, bit):
-    inner = 1 << left.index(bit)
-
-    def total(pair, pick):
-        keep, arrived = pair
-        shape = (keep.shape[0] // (2 * inner), 2, inner, *keep.shape[1:])
-        a, b = keep.reshape(shape)[:, pick], arrived.reshape(shape)[:, pick]
-        return (a.astype(f32) + b.astype(f32)).astype(bf16).reshape(-1, *keep.shape[1:])
-
-    out, keep = (jnp.concatenate([total(pair, pick) for pair in pairs], axis=-1) for pick in (1, 0))
-    return keep, swap(out, devices, 1 << bit)
-
-
-def owner_sums(pairs, devices, lanes, order, late=()):
-    left = list(range(lanes.bit_length() - 1))
-    for stage, bit in enumerate(order):
-        pairs = [halved(pairs, devices, left, bit)]
-        if stage == 0 and late:
-            pairs.append(halved(late, devices, left, bit))
-        left.remove(bit)
-    ((keep, arrived),) = pairs
-    result = keep[0].astype(f32) + arrived[0].astype(f32)
-    for high in range(1, devices // (2 * lanes)):
-        out = (keep[high].astype(f32) + arrived[high].astype(f32)).astype(bf16)
-        result += swap(out, devices, high * 2 * lanes).astype(f32)
-    return result
+def plus(a, b):
+    return (a.astype(f32) + b.astype(f32)).astype(bf16)
+
+
+def owner_sums(halves, devices, lanes, way, late=None):
+    bits = stages(devices, lanes, way)
+    out, keep = halves
+    for stage, bit in enumerate(bits):
+        arrived = swap(out, devices, 1 << bit)
+        if stage == len(bits) - 1:
+            return keep[0].astype(f32) + arrived[0].astype(f32)
+        half = keep.shape[0] // 2
+        out, keep = plus(keep[half:], arrived[half:]), plus(keep[:half], arrived[:half])
+        if stage == 0 and late is not None:
+            late_out, late_keep = late
+            late_arrived = swap(late_out, devices, 1 << bit)
+            out = jnp.concatenate([out, plus(late_keep[half:], late_arrived[half:])], axis=-1)
+            keep = jnp.concatenate([keep, plus(late_keep[:half], late_arrived[:half])], axis=-1)
+
+
+def gain_halves(values, devices, lanes, way, me):
+    kinds, depth = values.shape
+    blocks = jnp.pad(values.T, ((0, 0), (0, 128 - kinds))).astype(bf16)
+    every = range(devices)
+    core = lanes.bit_length() - 1
+    order = sorted(every, key=lambda r: (1 - bit_of(r, core), 1 - bit_of(r, way[0]), place_of(r, devices, lanes, way)))
+    blocks = blocks.reshape(devices, depth // devices, 128)[jnp.array(order) ^ me]
+    arrived = swap(blocks[: devices // 2], devices, lanes)
+    sums = plus(blocks[devices // 2 :], arrived)
+    return sums[: devices // 4], sums[devices // 4 :]
 
 
 def after(values, first):
@@ -683,14 +820,6 @@
 def orders(lanes):
     low = list(range(lanes.bit_length() - 1))
     return low, low[::-1]
-
-
-def gain_halves(values, devices, lanes, me):
-    kinds, depth = values.shape
-    blocks = jnp.pad(values.T, ((0, 0), (0, 128 - kinds))).astype(bf16)
-    blocks = blocks.reshape(devices, depth // devices, 128)[jnp.arange(devices) ^ me]
-    blocks = blocks.reshape(-1, 2, lanes, depth // devices, 128)
-    return blocks[:, 1], blocks[:, 0]
 
 
 def shards(devices, lanes, tokens, images, segment_ids, image_map, out_grad, norm_self, attn_query,
@@ -745,54 +874,48 @@
     mixed_two, log_two = cross_forward(count, query_two, kv)
     after_cross = after_self + product(mixed_two, w_cross_out)
 
-    (output, grad_after_cross, grad_gain_ffn, up_send, up_keep, down_send, down_keep) = feed(
-        me_ref, devices, lanes, after_cross, grad_out, gains[2:3], feed_set
+    one_way, other_way = orders(lanes)
+    (output, grad_after_cross, branch_two, grad_gain_ffn, *halves) = feed(
+        2, devices, lanes, (one_way, other_way), after_cross, grad_out, gains[2:3], feed_set
     )
-    one_way, other_way = orders(lanes)
-
-    def sums(way, *pairs, late=()):
-        return owner_sums(sum(pairs, []), devices, lanes, way, late)
-
-    def halves_of(left, right):
-        return weight_grad(me_ref, devices, lanes, left, right)
-
-    def paired(halves):
-        return cross_core(halves, devices, lanes)
-
-    grad_up = sums(one_way, paired((up_send, up_keep)))
-    grad_down = sums(other_way, paired((down_send, down_keep)))
-
-    branch_two = grad_after_cross.astype(bf16)
+
+    def sums(way, halves, late=None):
+        return owner_sums(halves, devices, lanes, way, late)
+
+    def halves_of(number, way, left, right, **options):
+        return weight_grad(number, devices, lanes, way, left, right, 2 * width, **options)
+
+    grad_up = sums(one_way, halves[:2])
+    grad_down = sums(other_way, halves[2:])
+
     grad_mixed_two = product_t(branch_two, w_cross_out).astype(bf16)
-    halves = halves_of(mixed_two[None], branch_two[None, None])
-    pair_out_two = paired(halves)
-    grad_mixed_two = after(grad_mixed_two, halves[0])
     grad_query_two, grad_kv = cross_backward(count, query_two, kv, grad_mixed_two, log_two)
-    halves = halves_of(images, grad_kv)
-    pair_kv = paired(halves)
-    halves = halves_of(hidden_two[None], after(grad_query_two, halves[0])[None, None])
-    pair_query_two = paired(halves)
-    grad_c = sums(one_way, pair_out_two, pair_query_two)
-    grad_d = sums(other_way, pair_kv)
+    halves = halves_of(3, one_way, mixed_two[None], after(branch_two, grad_kv)[None, None])
+    halves = halves_of(4, one_way, hidden_two[None], grad_query_two[None, None], first=width, into=halves)
+    grad_c = sums(one_way, halves)
+    halves = halves_of(5, other_way, images, after(grad_kv, halves[0]))
+    grad_d = sums(other_way, halves)
     grad_after_self, branch_one, grad_gain_cross = norm_grad(
         after(grad_query_two, halves[0])[None], second_set, 1, unit_two, inverse_two, gains[1:2], grad_after_cross
     )
     grad_mixed_one = product_t(branch_one, w_out).astype(bf16)
     grad_qkv = self_backward(pages, qkv, grad_mixed_one, log_one)
-    halves = halves_of(mixed_one[None], after(branch_one, grad_qkv)[None, None])
-    pair_out_one = paired(halves)
-    halves = halves_of(hidden_one[None], after(grad_qkv, halves[0])[:, None])
-    pair_qkv = paired(halves)
+    halves = halves_of(6, one_way, mixed_one[None], after(branch_one, grad_qkv)[None, None])
+    options = dict(first=width, into=halves, only=(0, 1))
+    halves = halves_of(7, one_way, hidden_one[None], grad_qkv[:, None], **options)
+    grad_qkv_again = after(grad_qkv, halves[0])
     _, grad_inputs, grad_gain_self = norm_grad(
-        after(grad_qkv, halves[0]), first_set, 0, unit_one, inverse_one, gains[0:1], grad_after_self
+        grad_qkv_again, first_set, 0, unit_one, inverse_one, gains[0:1], grad_after_self
     )
+    grad_qkv_again = after(grad_qkv, grad_inputs)
+    halves_kv = halves_of(8, one_way, hidden_one[None], grad_qkv_again[:, None], only=(1, 3))
     gain_grads = jnp.concatenate([grad_gain_self, grad_gain_cross, grad_gain_ffn])
-    pair_gains = paired(gain_halves(gain_grads, devices, lanes, me))
-    grad_a = sums(one_way, pair_out_one, pair_qkv[:1])
-    grad_b = sums(other_way, pair_qkv[1:], late=pair_gains)
+    late = gain_halves(gain_grads, devices, lanes, one_way, me)
+    grad_a = sums(one_way, halves)
+    grad_b = sums(one_way, halves_kv, late)
     gain_sums = grad_b[:, 2 * width :]
 
-    grad_kv = after(grad_kv, grad_inputs)
+    grad_kv = after(grad_kv, halves_kv[0])
     back = (((2,), (1,)), ((), ()))
     grad_images = lax.dot_general(grad_kv[0], w_kv[:, :width], back, preferred_element_type=f32)
     grad_images += lax.dot_general(grad_kv[1], w_kv[:, width:], back, preferred_element_type=f32)

time: 642 us -> 600 us (0.935)
  Pallas kernels: 299 us -> 327 us
  waiting for transfers between devices: 163 us -> 135 us
  starting transfers between devices: 38.6 us -> 22.7 us
  other arithmetic: 32.9 us -> 20.2 us
  local copies, waits for them, and re-layouts: 33.9 us -> 24.7 us
    ppermute x39 -> x26, waiting for transfers between devices: 163 us -> 135 us  [swap(): return lax.ppermute(values, AXES, [(i, i ^ bit) for i in range(devices)])]
    pallas_call x6 -> x7, Pallas kernels: 72.5 us -> 99.6 us  [the longest x6 52.8 us: weight_grad(): pl.pallas_call(functools.partial(weight_grad_kernel, devices, lanes, way,...]
    ppermute x39 -> x26, starting transfers between devices: 38.5 us -> 22.7 us  [swap(): return lax.ppermute(values, AXES, [(i, i ^ bit) for i in range(devices)])]
    convert_element_type x30 -> x20, other arithmetic: 16.8 us -> 8.45 us  [plus(): return (a.astype(f32) + b.astype(f32)).astype(bf16)]
    slice x8 -> x2, local copies, waits for them, and re-layouts: 8.39 us -> 0.04 us  [the longest x1 0.03 us: gain_halves(): arrived = swap(blocks[:devices // 2], devices, lanes)]
  transfers between devices with their start and end apart: 40 -> 27, of which waited for: 18 -> 12; matrix products, arithmetic and copies ran while one was open for 16% -> 13% of each run, Pallas kernels for 31% -> 29%
where the time goes in v1:
time: 600 us; the launch traced here: 595 us
  Pallas kernels  327 us (54%)
  waiting for transfers between devices  135 us (22%)
  matrix products  50.6 us (8%)
  local copies, waits for them, and re-layouts  24.7 us (4%)
  starting transfers between devices  22.7 us (4%)
  other arithmetic  20.2 us (3%)
  between operations  15.9 us (3%)
    ppermute x26, waiting for transfers between devices, swap(): return lax.ppermute(values, AXES, [(i, i ^ bit) for i in range(devices)])  135 us
    pallas_call x2, Pallas kernels, gather(): pl.pallas_call(functools.partial(gather_kernel, devices, lanes, tracks),...  114 us
    pallas_call x6, Pallas kernels, weight_grad(): pl.pallas_call(functools.partial(weight_grad_kernel, devices, lanes, way,...  52.8 us
    pallas_call x1, Pallas kernels, feed(): pl.pallas_call(functools.partial(feed_kernel, devices, lanes, ways), grid...  46.7 us
    pallas_call x1, Pallas kernels, cross_backward(): pl.pallas_call(cross_backward_kernel, grid_spec=pltpu.PrefetchScalarGridS...  34.9 us
    pallas_call x1, Pallas kernels, cross_forward(): pl.pallas_call(cross_forward_kernel, grid_spec=pltpu.PrefetchScalarGridSp...  29.9 us
    ppermute x26, starting transfers between devices, swap(): return lax.ppermute(values, AXES, [(i, i ^ bit) for i in range(devices)])  22.7 us
    dot_general x6, matrix products, product(): return jnp.dot(left, right, preferred_element_type=f32)  21.7 us
  transfers between devices with their start and end apart: 27, of which 12 were waited for; matrix products, arithmetic and copies ran while one was open for 13% of the time, Pallas kernels for 29%

profile of v1, /device:TPU:0, one launch (start us, length us, event | category | flops | bytes accessed | tf_op | source)
XLA Modules:
  0.0 595.4 jit_solution(9064576482154264970)
XLA Ops:
  7.2 0.9 constant_dynamic-update-slice_fusion.5
  13.1 60.7 %gather.19 = bf16[32,32,5248]{2,1,0:T(8,128)(2,1)} custom-call(bf16[32,5248]{1,0:T(8,128)(2,1)} %copy-done.24), custom_call_target="tpu_custom_call" | custom-call | flops 40000000000 | tf_op jit(solution)/shard_map/gather/pallas_call | solution.py:764
  74.9 1.5 pad_maximum_fusion.1
  76.4 1.0 copy.106
  77.4 1.8 slice_convert_fusion
  79.2 1.2 copy.115
  83.0 2.2 copy.104.refs_0_
  87.0 1.3 fusion.48
  89.8 5.0 fusion.2.q.k.v
  94.9 6.9 %convert_bitcast_fusion.k.v = bf16[2,588,2048]{2,1,0:T(8,128)(2,1)} fusion(bf16[1024,5248]{1,0:T(8,128)(2,1)S(1)} %bitcast.108, bf16[2,588,1024]{2,0,1:T(2,128)(2,1)S(1)} %copy-done.6), kind=kOutput, calls=%fused_computation.4 | convolution fusion | flops 4934909952 | bytes 11419648 | tf_op jit(solution)/shard_map/dot_general | solution.py:865
  101.8 14.1 %self_forward.1 = (bf16[512,1024]{1,0:T(8,128)(2,1)}, f32[8,2,512]{2,1,0:T(2,128)}) custom-call(s32[512,1]{1,0:T(8,128)} %copy.103.page_column, s32[1,512]{1,0:T(1,128)} %bitcast.99, bf16[512,3072]{1,0:T(8,128)(2,1)} %fusion.2.q.k.v, bf16[512,3072]{1,0:T(8,128)(2,1)} %fusion.2.q.k.v, bf16[512,3072]{1,0:T(8,128)(2,1)} %fusion.2.q.k.v), custom_call_target="tpu_custom_call" | custom-call | flops 14000000000 | tf_op jit(solution)/shard_map/self_forward/pallas_call | solution.py:119
  115.9 53.2 %gather.20 = bf16[32,32,3072]{2,1,0:T(8,128)(2,1)} custom-call(bf16[32,3072]{1,0:T(8,128)(2,1)} %pad_maximum_fusion.3.x_ref), custom_call_target="tpu_custom_call" | custom-call | flops 40000000000 | tf_op jit(solution)/shard_map/gather/pallas_call | solution.py:764
  169.1 3.3 fusion.58
  172.4 1.3 copy-done.4
  176.4 2.9 convolution_convert_fusion.2.g_ref
  179.3 1.3 fusion.49
  180.6 4.6 fusion.36.q
  185.3 29.9 %cross_forward.1 = (bf16[512,1024]{1,0:T(8,128)(2,1)}, f32[8,2,512]{2,1,0:T(2,128)}) custom-call(s32[1]{0:T(128)} %bitcast.14.count_ref, bf16[512,1024]{1,0:T(8,128)(2,1)} %fusion.36.q, bf16[2,588,2048]{2,1,0:T(8,128)(2,1)} %convert_bitcast_fusion.k.v, bf16[2,588,2048]{2,1,0:T(8,128)(2,1)} %convert_bitcast_fusion.k.v), custom_call_target="tpu_custom_call" | custom-call | flops 24000000000 | tf_op jit(solution)/shard_map/cross_forward/pallas_call | solution.py:243
  215.1 5.1 fusion.27.x_ref
  220.3 46.7 %feed.1 = (bf16[512,1024]{1,0:T(8,128)(2,1)}, f32[512,1024]{1,0:T(8,128)}, bf16[512,1024]{1,0:T(8,128)(2,1)}, f32[1,1024]{1,0:T(1,128)}, bf16[8,32,4096]{2,1,0:T...) custom-call(f32[512,1024]{1,0:T(8,128)} %fusion.27.x_ref, ...), custom_call_target="tpu_custom_call" | custom-call | flops 40000000000 | tf_op jit(solution)/shard_map/feed/pallas_call | solution.py:643
  267.0 4.2 fusion.33.g
  271.2 34.9 %cross_backward.1 = (bf16[512,1024]{1,0:T(8,128)(2,1)}, bf16[2,2,588,1024]{3,2,1,0:T(8,128)(2,1)}) custom-call(s32[1]{0:T(128)} %bitcast.14.count_ref, bf16[512,1024]{1,0:T(8,128)(2,1)} %fusion.36.q, bf16[2,588,2048]{2,1,0:T(8,128)(2,1)} %convert_bitcast_fusion.k.v, bf16[2,588,2048]{2,1,0:T(8,128)(2,1)} %convert_bitcast_fusion.k.v, ...), custom_call_target="tpu_custom_call" | custom-call | flops 28000000000 | tf_op jit(solution)/shard_map/cross_backward/pallas_call | solution.py:308
  306.1 7.4 %weight_grad.6 = (bf16[8,32,2048]{2,1,0:T(8,128)(2,1)}, bf16[8,32,2048]{2,1,0:T(8,128)(2,1)}) custom-call(bf16[1,512,1024]{2,1,0:T(8,128)(2,1)} %bitcast.126, bf16[1,1,512,1024]{3,2,1,0:T(8,128)(2,1)} %bitcast.127), custom_call_target="tpu_custom_call" | custom-call | flops 3000000000 | tf_op jit(solution)/shard_map/weight_grad/pallas_call | solution.py:449
  313.4 7.2 %weight_grad.7 = (bf16[8,32,2048]{2,1,0:T(8,128)(2,1)}, bf16[8,32,2048]{2,1,0:T(8,128)(2,1)}) custom-call(bf16[1,512,1024]{2,1,0:T(8,128)(2,1)} %get-tuple-element.199.refs_0_, bf16[1,1,512,1024]{3,2,1,0:T(8,128)(2,1)} %bitcast.124, bf16[8,32,2048]{2,1,0:T(8,128)(2,1)} %get-tuple-element.66.refs_2_, ...), custom_call_target="tpu_custom_call", output_to_operand_aliasing={{0}: (2, {}), {1}: (3, {})} | custom-call | flops 3000000000 | tf_op jit(solution)/shard_map/weight_grad/pallas_call | solution.py:449
  320.6 1.3 collective-permute-start.10
  321.9 14.3 %weight_grad.8 = (bf16[8,32,2048]{2,1,0:T(8,128)(2,1)}, bf16[8,32,2048]{2,1,0:T(8,128)(2,1)}) custom-call(bf16[2,588,1024]{2,1,0:T(8,128)(2,1)} %copy.104.refs_0_, bf16[2,2,588,1024]{3,2,1,0:T(8,128)(2,1)} %get-tuple-element.84.refs_1_), custom_call_target="tpu_custom_call" | custom-call | flops 12000000000 | tf_op jit(solution)/shard_map/weight_grad/pallas_call | solution.py:449
  336.3 8.2 %norm_grad.2 = (f32[512,1024]{1,0:T(8,128)}, bf16[512,1024]{1,0:T(8,128)(2,1)}, f32[1,1024]{1,0:T(1,128)}) custom-call(bf16[1,512,1024]{2,1,0:T(8,128)(2,1)} %bitcast.125, bf16[1024,3072]{1,0:T(8,128)(2,1)} %bitcast.119, f32[512,1024]{1,0:T(8,128)} %copy-done.10, f32[512,1]{1,0:T(8,128)} %copy.108.inverse, f32[1,1024]{1,0:T(1,128)} %copy-done.23, ...), custom_call_target="tpu_custom_call" | custom-call | flops 4000000000 | tf_op jit(solution)/shard_map/norm_grad/pallas_call | solution.py:505
  344.4 4.2 fusion.30.g
  348.7 15.0 %self_backward.1.d_ref = bf16[3,512,1024]{2,1,0:T(8,128)(2,1)} custom-call(s32[512,1]{1,0:T(8,128)} %copy.103.page_column, s32[1,512]{1,0:T(1,128)} %bitcast.100, bf16[512,3072]{1,0:T(8,128)(2,1)} %fusion.2.q.k.v, bf16[512,3072]{1,0:T(8,128)(2,1)} %fusion.2.q.k.v, bf16[512,3072]{1,0:T(8,128)(2,1)} %fusion.2.q.k.v, bf16[512,1024]{1,0:T(8,128)(2,1)} %fusion.30.g, ...), custom_call_target="tpu_custom_call" | custom-call | flops 15000000512 | tf_op jit(solution)/shard_map/self_backward/pallas_call | solution.py:176
  363.7 7.0 %weight_grad.9 = (bf16[8,32,2048]{2,1,0:T(8,128)(2,1)}, bf16[8,32,2048]{2,1,0:T(8,128)(2,1)}) custom-call(bf16[1,512,1024]{2,1,0:T(8,128)(2,1)} %bitcast.123, bf16[1,1,512,1024]{3,2,1,0:T(8,128)(2,1)} %bitcast.128), custom_call_target="tpu_custom_call" | custom-call | flops 3000000000 | tf_op jit(solution)/shard_map/weight_grad/pallas_call | solution.py:449
  370.7 7.2 %weight_grad.10 = (bf16[8,32,2048]{2,1,0:T(8,128)(2,1)}, bf16[8,32,2048]{2,1,0:T(8,128)(2,1)}) custom-call(bf16[1,512,1024]{2,1,0:T(8,128)(2,1)} %get-tuple-element.197.refs_0_, bf16[3,1,512,1024]{3,2,1,0:T(8,128)(2,1)} %bitcast.121, bf16[8,32,2048]{2,1,0:T(8,128)(2,1)} %get-tuple-element.76.refs_2_, ...), custom_call_target="tpu_custom_call", output_to_operand_aliasing={{0}: (2, {}), {1}: (3, {})} | custom-call | flops 3000000000 | tf_op jit(solution)/shard_map/weight_grad/pallas_call | solution.py:449
  377.9 1.9 collective-permute-start.6
  379.8 11.0 %norm_grad.3 = (f32[512,1024]{1,0:T(8,128)}, bf16[512,1024]{1,0:T(8,128)(2,1)}, f32[1,1024]{1,0:T(1,128)}) custom-call(bf16[3,512,1024]{2,1,0:T(8,128)(2,1)} %self_backward.1.d_ref, bf16[1024,5248]{1,0:T(8,128)(2,1)} %bitcast.104, f32[512,1024]{1,0:T(8,128)} %copy-done.9, f32[512,1]{1,0:T(8,128)} %copy.110.inverse, f32[1,1024]{1,0:T(1,128)} %copy-done.22, ...), custom_call_target="tpu_custom_call" | custom-call | flops 12000000000 | tf_op jit(solution)/shard_map/norm_grad/pallas_call | solution.py:505
  390.9 9.8 %weight_grad.11 = (bf16[8,32,2048]{2,1,0:T(8,128)(2,1)}, bf16[8,32,2048]{2,1,0:T(8,128)(2,1)}) custom-call(bf16[1,512,1024]{2,1,0:T(8,128)(2,1)} %get-tuple-element.197.refs_0_, bf16[3,1,512,1024]{3,2,1,0:T(8,128)(2,1)} %bitcast.122), custom_call_target="tpu_custom_call" | custom-call | flops 6000000000 | tf_op jit(solution)/shard_map/weight_grad/pallas_call | solution.py:449
  402.5 5.2 fusion.6
  407.8 4.9 add_convert_fusion
  412.7 1.7 fusion.40
  414.5 1.8 collective-permute-start.2
  416.3 1.7 fusion.39
  418.0 3.9 copy.113
  421.9 5.9 collective-permute-done.2
  427.8 1.4 collective-permute-start.22
  430.2 1.6 add_convert_fusion.10
  431.8 1.3 collective-permute-start.15
  433.1 1.6 add_convert_fusion.12
  435.3 1.6 add_convert_fusion.14
  436.9 1.5 collective-permute-start.7
  438.9 48.6 %collective-permute-done.15 = bf16[4,32,2048]{2,1,0:T(8,128)(2,1)S(1)} collective-permute-done((bf16[4,32,2048]{2,1,0:T(8,128)(2,1)S(1)}, bf16[4,32,2048]{2,1,0:T(8,128)(2,1)S(1)}, u32[]{:S(2)}, u32[]{:S(2)}) %collective-permute-start.15) | collective-permute-done | bytes 524320 | tf_op jit(solution)/shard_map/ppermute | solution.py:781
  488.3 10.5 %collective-permute-done.7 = bf16[4,32,2048]{2,1,0:T(8,128)(2,1)S(1)} collective-permute-done((bf16[4,32,2048]{2,1,0:T(8,128)(2,1)S(1)}, bf16[4,32,2048]{2,1,0:T(8,128)(2,1)S(1)}, u32[]{:S(2)}, u32[]{:S(2)}) %collective-permute-start.7) | collective-permute-done | bytes 524320 | tf_op jit(solution)/shard_map/ppermute | solution.py:781
  498.9 10.4 %collective-permute-done.3 = bf16[4,32,2176]{2,1,0:T(8,128)(2,1)S(1)} collective-permute-done((bf16[4,32,2176]{2,1,0:T(8,128)(2,1)S(1)}, bf16[4,32,2176]{2,1,0:T(8,128)(2,1)S(1)}, u32[]{:S(2)}, u32[]{:S(2)}) %collective-permute-start.3) | collective-permute-done | bytes 557088 | tf_op jit(solution)/shard_map/ppermute | solution.py:781
  509.4 2.1 collective-permute-start.4
  511.7 11.0 %collective-permute-done.8 = bf16[2,32,2048]{2,1,0:T(8,128)(2,1)S(1)} collective-permute-done((bf16[2,32,2048]{2,1,0:T(8,128)(2,1)S(1)}, bf16[2,32,2048]{2,1,0:T(8,128)(2,1)S(1)}, u32[]{:S(2)}, u32[]{:S(2)}) %collective-permute-start.8) | collective-permute-done | bytes 262176 | tf_op jit(solution)/shard_map/ppermute | solution.py:781
  522.7 3.6 collective-permute-done.4
  526.4 3.0 collective-permute-start.5
  530.1 5.9 collective-permute-done.13
  536.1 1.0 add_convert_fusion.2
  537.2 1.2 collective-permute-start.23
  541.5 12.1 %collective-permute-done.23 = bf16[4,128,1024]{2,1,0:T(8,128)(2,1)S(1)} collective-permute-done((bf16[4,128,1024]{2,1,0:T(8,128)(2,1)S(1)}, bf16[4,128,1024]{2,1,0:T(8,128)(2,1)S(1)}, u32[]{:S(2)}, u32[]{:S(2)}) %collective-permute-start.23) | collective-permute-done | bytes 1048608 | tf_op jit(solution)/shard_map/ppermute | solution.py:781
  554.1 0.9 collective-permute-done.19
  555.3 1.1 collective-permute-start.20
  557.2 9.7 %collective-permute-done.24 = bf16[2,128,1024]{2,1,0:T(8,128)(2,1)S(1)} collective-permute-done((bf16[2,128,1024]{2,1,0:T(8,128)(2,1)S(1)}, bf16[2,128,1024]{2,1,0:T(8,128)(2,1)S(1)}, u32[]{:S(2)}, u32[]{:S(2)}) %collective-permute-start.24) | collective-permute-done | bytes 524320 | tf_op jit(solution)/shard_map/ppermute | solution.py:781
  567.0 2.4 collective-permute-start.25
  569.3 8.7 %collective-permute-done.20 = bf16[2,32,4096]{2,1,0:T(8,128)(2,1)S(1)} collective-permute-done((bf16[2,32,4096]{2,1,0:T(8,128)(2,1)S(1)}, bf16[2,32,4096]{2,1,0:T(8,128)(2,1)S(1)}, u32[]{:S(2)}, u32[]{:S(2)}) %collective-permute-start.20) | collective-permute-done | bytes 524320 | tf_op jit(solution)/shard_map/ppermute | solution.py:781
  579.8 7.4 %collective-permute-done.21 = bf16[1,32,4096]{2,1,0:T(8,128)(2,1)S(1)} collective-permute-done((bf16[1,32,4096]{2,1,0:T(8,128)(2,1)S(1)}, bf16[1,32,4096]{2,1,0:T(8,128)(2,1)S(1)}, u32[]{:S(2)}, u32[]{:S(2)}) %collective-permute-start.21) | collective-permute-done | bytes 262176 | tf_op jit(solution)/shard_map/ppermute | solution.py:781
  (175 shorter events, 27.3 us)
Async XLA Ops:
  7.2 78.0 %copy-start = (bf16[1,512,1024]{2,1,0:T(8,128)(2,1)S(1)}, bf16[1,512,1024]{2,1,0:T(8,128)(2,1)}, u32[]{:S(2)}) copy-start(bf16[1,512,1024]{2,1,0:T(8,128)(2,1)} %param.19) | copy-start | bytes 3145732
  7.2 213.1 %all-gather.3.cloned.1.call-start = ((), (), s32[]{:S(2)}) async-start(), calls=%async_computation | async-start | bytes 17301504 | tf_op jit(solution)/shard_map/all_gather | solution.py:840
  13.1 60.7 %copy-start.15 = (bf16[32,4096]{1,0:T(8,128)(2,1)S(1)}, bf16[32,4096]{1,0:T(8,128)(2,1)}, u32[]{:S(2)}) copy-start(bf16[32,4096]{1,0:T(8,128)(2,1)} %param.35) | copy-start | bytes 786436
  13.1 61.6 %copy-start.16 = (bf16[128,1024]{1,0:T(8,128)(2,1)S(1)}, bf16[128,1024]{1,0:T(8,128)(2,1)}, u32[]{:S(2)}) copy-start(bf16[128,1024]{1,0:T(8,128)(2,1)} %param.36) | copy-start | bytes 786436
  74.9 5.5 copy-start.26
  74.9 5.5 copy-start.31
  74.9 8.1 %copy-start.6 = (bf16[2,588,1024]{2,0,1:T(2,128)(2,1)S(1)}, bf16[2,588,1024]{2,0,1:T(2,128)(2,1)}, u32[]{:S(2)}) copy-start(bf16[2,588,1024]{2,0,1:T(2,128)(2,1)} %param.20) | copy-start | bytes 7225348
  81.9 94.4 %copy-start.20 = (s32[512]{0:T(512)}, s32[512]{0:T(512)S(1)}, u32[]{:S(2)}) copy-start(s32[512]{0:T(512)S(1)} %subtract_select_fusion) | copy-start | bytes 6148
  82.1 3.0 copy-start.25
  83.0 6.8 %copy-start.27 = (bf16[32,32,5248]{2,1,0:T(8,128)(2,1)S(1)}, bf16[32,32,5248]{2,1,0:T(8,128)(2,1)}, u32[]{:S(2)}) copy-start(bf16[32,32,5248]{2,1,0:T(8,128)(2,1)} %gather.19) | copy-start | bytes 32243716
  86.0 2.4 copy-start.2
  87.0 2.8 copy-start.22
  87.0 93.7 %copy-start.23 = (f32[1,1024]{1,0:T(1,128)}, f32[1,1024]{1,0:T(1,128)S(1)}, u32[]{:S(2)}) copy-start(f32[1,1024]{1,0:T(1,128)S(1)} %get-tuple-element.236.gain) | copy-start | bytes 12292
  87.0 2.0 copy-start.17
  87.0 2.1 copy-start.18
  87.0 2.1 copy-start.19
  89.1 5.8 copy-start.9
  115.8 53.2 %copy-start.3 = (f32[512,1024]{1,0:T(8,128)S(1)}, f32[512,1024]{1,0:T(8,128)}, u32[]{:S(2)}) copy-start(f32[512,1024]{1,0:T(8,128)} %copy-done.2) | copy-start | bytes 6291460
  172.3 3.4 copy-start.34
  174.0 5.3 copy-start.5
  180.6 4.6 copy-start.10
  320.6 111.2 %collective-permute-start.10 = (bf16[8,32,2048]{2,1,0:T(8,128)(2,1)}, bf16[8,32,2048]{2,1,0:T(8,128)(2,1)}, u32[]{:S(2)}, u32[]{:S(2)}) collective-permute-start(bf16[8,32,2048]{2,1,0:T(8,128)(2,1)} %get-tuple-element.68), channel_id=1, source_target_pairs={{0,1},{1,0},{2,3},{3,2},{4,5},{5,4},{6,7},{7,6},{8,9},{9,8},{10,11... | collective-permute-start | bytes 3145736 | tf_op jit(solution)/shard_map/ppermute | solution.py:781
  336.2 93.1 %collective-permute-start.14 = (bf16[8,32,2048]{2,1,0:T(8,128)(2,1)}, bf16[8,32,2048]{2,1,0:T(8,128)(2,1)}, u32[]{:S(2)}, u32[]{:S(2)}) collective-permute-start(bf16[8,32,2048]{2,1,0:T(8,128)(2,1)} %get-tuple-element.70), channel_id=1, source_target_pairs={{0,2},{1,3},{2,0},{3,1},{4,6},{5,7},{6,4},{7,5},{8,10},{9,11},{10,... | collective-permute-start | bytes 3145736 | tf_op jit(solution)/shard_map/ppermute | solution.py:781
  377.9 56.8 %collective-permute-start.6 = (bf16[8,32,2048]{2,1,0:T(8,128)(2,1)}, bf16[8,32,2048]{2,1,0:T(8,128)(2,1)}, u32[]{:S(2)}, u32[]{:S(2)}) collective-permute-start(bf16[8,32,2048]{2,1,0:T(8,128)(2,1)} %get-tuple-element.78), channel_id=1, source_target_pairs={{0,1},{1,0},{2,3},{3,2},{4,5},{5,4},{6,7},{7,6},{8,9},{9,8},{10,11... | collective-permute-start | bytes 3145736 | tf_op jit(solution)/shard_map/ppermute | solution.py:781
  390.9 10.1 %copy-start.30 = (f32[1,1024]{1,0:T(1,128)S(1)}, f32[1,1024]{1,0:T(1,128)}, u32[]{:S(2)}) copy-start(f32[1,1024]{1,0:T(1,128)} %get-tuple-element.86) | copy-start | bytes 12292
  390.9 10.1 %copy-start.29 = (f32[1,1024]{1,0:T(1,128)S(1)}, f32[1,1024]{1,0:T(1,128)}, u32[]{:S(2)}) copy-start(f32[1,1024]{1,0:T(1,128)} %get-tuple-element.87) | copy-start | bytes 12292
  390.9 10.1 %copy-start.28 = (f32[1,1024]{1,0:T(1,128)S(1)}, f32[1,1024]{1,0:T(1,128)}, u32[]{:S(2)}) copy-start(f32[1,1024]{1,0:T(1,128)} %get-tuple-element.88) | copy-start | bytes 12292
  400.7 36.2 %collective-permute-start = (bf16[8,32,2048]{2,1,0:T(8,128)(2,1)}, bf16[8,32,2048]{2,1,0:T(8,128)(2,1)S(1)}, u32[]{:S(2)}, u32[]{:S(2)}) collective-permute-start(bf16[8,32,2048]{2,1,0:T(8,128)(2,1)} %get-tuple-element.83), channel_id=1, source_target_pairs={{0,1},{1,0},{2,3},{3,2},{4,5},{5,4},{6,7},{7,6},{8,9},{9,8},{10,11... | collective-permute-start | bytes 3145736 | tf_op jit(solution)/shard_map/ppermute | solution.py:781
  402.2 5.6 slice-start
  402.2 5.5 slice-start.1
  402.2 12.2 %collective-permute-start.1 = (bf16[16,32,128]{2,1,0:T(8,128)(2,1)S(1)}, bf16[16,32,128]{2,1,0:T(8,128)(2,1)S(1)}, u32[]{:S(2)}, u32[]{:S(2)}) collective-permute-start(bf16[16,32,128]{2,1,0:T(8,128)(2,1)S(1)} %pad_slice_fusion.2), channel_id=1, source_target_pairs={{0,4},{1,5},{2,6},{3,7},{4,0},{5,1},{6,2},{7,3},{8,12},{9,13},{10,... | collective-permute-start | bytes 393224 | tf_op jit(solution)/shard_map/ppermute | solution.py:781
  407.8 4.9 copy-start.21
  407.8 4.9 copy-start.36
  412.7 3.6 copy-start.35
  414.5 13.3 %collective-permute-start.2 = (bf16[8,32,128]{2,1,0:T(8,128)(2,1)S(1)}, bf16[8,32,128]{2,1,0:T(8,128)(2,1)S(1)}, u32[]{:S(2)}, u32[]{:S(2)}) collective-permute-start(bf16[8,32,128]{2,1,0:T(8,128)(2,1)S(1)} %slice.438), channel_id=1, source_target_pairs={{0,1},{1,0},{2,3},{3,2},{4,5},{5,4},{6,7},{7,6},{8,9},{9,8},{10,11... | collective-permute-start | bytes 196616 | tf_op jit(solution)/shard_map/ppermute | solution.py:781
  416.3 11.5 %copy-start.33 = (bf16[8,128,1024]{2,1,0:T(8,128)(2,1)S(1)}, bf16[8,128,1024]{2,1,0:T(8,128)(2,1)}, u32[]{:S(2)}) copy-start(bf16[8,128,1024]{2,1,0:T(8,128)(2,1)} %get-tuple-element.95) | copy-start | bytes 6291460
  418.0 11.3 %copy-start.32 = (bf16[8,32,4096]{2,1,0:T(8,128)(2,1)S(1)}, bf16[8,32,4096]{2,1,0:T(8,128)(2,1)}, u32[]{:S(2)}) copy-start(bf16[8,32,4096]{2,1,0:T(8,128)(2,1)} %get-tuple-element.93) | copy-start | bytes 6291460
  418.0 12.2 %copy-start.11 = (bf16[8,32,2048]{2,1,0:T(8,128)(2,1)S(1)}, bf16[8,32,2048]{2,1,0:T(8,128)(2,1)}, u32[]{:S(2)}) copy-start(bf16[8,32,2048]{2,1,0:T(8,128)(2,1)} %get-tuple-element.91) | copy-start | bytes 3145732
  421.9 11.1 %copy-start.13 = (bf16[8,32,2048]{2,1,0:T(8,128)(2,1)S(1)}, bf16[8,32,2048]{2,1,0:T(8,128)(2,1)}, u32[]{:S(2)}) copy-start(bf16[8,32,2048]{2,1,0:T(8,128)(2,1)} %get-tuple-element.90) | copy-start | bytes 3145732
  427.8 108.3 %collective-permute-start.22 = (bf16[8,128,1024]{2,1,0:T(8,128)(2,1)S(1)}, bf16[8,128,1024]{2,1,0:T(8,128)(2,1)S(1)}, u32[]{:S(2)}, u32[]{:S(2)}) collective-permute-start(bf16[8,128,1024]{2,1,0:T(8,128)(2,1)S(1)} %copy-done.33), channel_id=1, source_target_pairs={{0,2},{1,3},{2,0},{3,1},{4,6},{5,7},{6,4},{7,5},{8,10},{9,11},{10,... | collective-permute-start | bytes 6291464 | tf_op jit(solution)/shard_map/ppermute | solution.py:781
  429.3 109.1 %collective-permute-start.18 = (bf16[8,32,4096]{2,1,0:T(8,128)(2,1)S(1)}, bf16[8,32,4096]{2,1,0:T(8,128)(2,1)S(1)}, u32[]{:S(2)}, u32[]{:S(2)}) collective-permute-start(bf16[8,32,4096]{2,1,0:T(8,128)(2,1)S(1)} %copy-done.32), channel_id=1, source_target_pairs={{0,1},{1,0},{2,3},{3,2},{4,5},{5,4},{6,7},{7,6},{8,9},{9,8},{10,11... | collective-permute-start | bytes 6291464 | tf_op jit(solution)/shard_map/ppermute | solution.py:781
  431.8 3.6 copy-start.14
  431.8 55.7 %collective-permute-start.15 = (bf16[4,32,2048]{2,1,0:T(8,128)(2,1)S(1)}, bf16[4,32,2048]{2,1,0:T(8,128)(2,1)S(1)}, u32[]{:S(2)}, u32[]{:S(2)}) collective-permute-start(bf16[4,32,2048]{2,1,0:T(8,128)(2,1)S(1)} %get-tuple-element.210), channel_id=1, source_target_pairs={{0,1},{1,0},{2,3},{3,2},{4,5},{5,4},{6,7},{7,6},{8,9},{9,8},{10,11... | collective-permute-start | bytes 1572872 | tf_op jit(solution)/shard_map/ppermute | solution.py:781
  434.6 3.8 copy-start.12
  434.7 53.4 %collective-permute-start.11 = (bf16[4,32,2048]{2,1,0:T(8,128)(2,1)S(1)}, bf16[4,32,2048]{2,1,0:T(8,128)(2,1)S(1)}, u32[]{:S(2)}, u32[]{:S(2)}) collective-permute-start(bf16[4,32,2048]{2,1,0:T(8,128)(2,1)S(1)} %get-tuple-element.212), channel_id=1, source_target_pairs={{0,2},{1,3},{2,0},{3,1},{4,6},{5,7},{6,4},{7,5},{8,10},{9,11},{10,... | collective-permute-start | bytes 1572872 | tf_op jit(solution)/shard_map/ppermute | solution.py:781
  436.9 61.8 %collective-permute-start.7 = (bf16[4,32,2048]{2,1,0:T(8,128)(2,1)S(1)}, bf16[4,32,2048]{2,1,0:T(8,128)(2,1)S(1)}, u32[]{:S(2)}, u32[]{:S(2)}) collective-permute-start(bf16[4,32,2048]{2,1,0:T(8,128)(2,1)S(1)} %get-tuple-element.214), channel_id=1, source_target_pairs={{0,2},{1,3},{2,0},{3,1},{4,6},{5,7},{6,4},{7,5},{8,10},{9,11},{10,... | collective-permute-start | bytes 1572872 | tf_op jit(solution)/shard_map/ppermute | solution.py:781
  487.5 21.8 %collective-permute-start.3 = (bf16[4,32,2176]{2,1,0:T(8,128)(2,1)S(1)}, bf16[4,32,2176]{2,1,0:T(8,128)(2,1)S(1)}, u32[]{:S(2)}, u32[]{:S(2)}) collective-permute-start(bf16[4,32,2176]{2,1,0:T(8,128)(2,1)S(1)} %pad_maximum_fusion), channel_id=1, source_target_pairs={{0,2},{1,3},{2,0},{3,1},{4,6},{5,7},{6,4},{7,5},{8,10},{9,11},{10,... | collective-permute-start | bytes 1671176 | tf_op jit(solution)/shard_map/ppermute | solution.py:781
  488.1 21.3 %collective-permute-start.16 = (bf16[2,32,2048]{2,1,0:T(8,128)(2,1)S(1)}, bf16[2,32,2048]{2,1,0:T(8,128)(2,1)S(1)}, u32[]{:S(2)}, u32[]{:S(2)}) collective-permute-start(bf16[2,32,2048]{2,1,0:T(8,128)(2,1)S(1)} %get-tuple-element.220), channel_id=1, source_target_pairs={{0,8},{1,9},{2,10},{3,11},{4,12},{5,13},{6,14},{7,15},{8,0},{9,1},... | collective-permute-start | bytes 786440 | tf_op jit(solution)/shard_map/ppermute | solution.py:781
  498.8 12.8 %collective-permute-start.12 = (bf16[2,32,2048]{2,1,0:T(8,128)(2,1)S(1)}, bf16[2,32,2048]{2,1,0:T(8,128)(2,1)S(1)}, u32[]{:S(2)}, u32[]{:S(2)}) collective-permute-start(bf16[2,32,2048]{2,1,0:T(8,128)(2,1)S(1)} %get-tuple-element.222), channel_id=1, source_target_pairs={{0,8},{1,9},{2,10},{3,11},{4,12},{5,13},{6,14},{7,15},{8,0},{9,1},... | collective-permute-start | bytes 786440 | tf_op jit(solution)/shard_map/ppermute | solution.py:781
  509.3 13.4 %collective-permute-start.8 = (bf16[2,32,2048]{2,1,0:T(8,128)(2,1)S(1)}, bf16[2,32,2048]{2,1,0:T(8,128)(2,1)S(1)}, u32[]{:S(2)}, u32[]{:S(2)}) collective-permute-start(bf16[2,32,2048]{2,1,0:T(8,128)(2,1)S(1)} %get-tuple-element.224), channel_id=1, source_target_pairs={{0,8},{1,9},{2,10},{3,11},{4,12},{5,13},{6,14},{7,15},{8,0},{9,1},... | collective-permute-start | bytes 786440 | tf_op jit(solution)/shard_map/ppermute | solution.py:781
  509.4 26.7 %copy-start.8 = (bf16[8,128,1024]{2,1,0:T(8,128)(2,1)S(1)}, bf16[8,128,1024]{2,1,0:T(8,128)(2,1)}, u32[]{:S(2)}) copy-start(bf16[8,128,1024]{2,1,0:T(8,128)(2,1)} %get-tuple-element.94) | copy-start | bytes 6291460
  509.4 16.9 %collective-permute-start.4 = (bf16[2,32,2176]{2,1,0:T(8,128)(2,1)S(1)}, bf16[2,32,2176]{2,1,0:T(8,128)(2,1)S(1)}, u32[]{:S(2)}, u32[]{:S(2)}) collective-permute-start(bf16[2,32,2176]{2,1,0:T(8,128)(2,1)S(1)} %get-tuple-element.218), channel_id=1, source_target_pairs={{0,8},{1,9},{2,10},{3,11},{4,12},{5,13},{6,14},{7,15},{8,0},{9,1},... | collective-permute-start | bytes 835592 | tf_op jit(solution)/shard_map/ppermute | solution.py:781
  511.6 14.8 %collective-permute-start.17 = (bf16[1,32,2048]{2,1,0:T(8,128)(2,1)S(1)}, bf16[1,32,2048]{2,1,0:T(8,128)(2,1)S(1)}, u32[]{:S(2)}, u32[]{:S(2)}) collective-permute-start(bf16[1,32,2048]{2,1,0:T(8,128)(2,1)S(1)} %add_convert_fusion.31), channel_id=1, source_target_pairs={{0,16},{1,17},{2,18},{3,19},{4,20},{5,21},{6,22},{7,23},{8,24},{9,... | collective-permute-start | bytes 393224 | tf_op jit(solution)/shard_map/ppermute | solution.py:781
  522.6 13.4 %collective-permute-start.13 = (bf16[1,32,2048]{2,1,0:T(8,128)(2,1)S(1)}, bf16[1,32,2048]{2,1,0:T(8,128)(2,1)S(1)}, u32[]{:S(2)}, u32[]{:S(2)}) collective-permute-start(bf16[1,32,2048]{2,1,0:T(8,128)(2,1)S(1)} %add_convert_fusion.33), channel_id=1, source_target_pairs={{0,16},{1,17},{2,18},{3,19},{4,20},{5,21},{6,22},{7,23},{8,24},{9,... | collective-permute-start | bytes 393224 | tf_op jit(solution)/shard_map/ppermute | solution.py:781
  526.3 14.4 %collective-permute-start.9 = (bf16[1,32,2048]{2,1,0:T(8,128)(2,1)S(1)}, bf16[1,32,2048]{2,1,0:T(8,128)(2,1)S(1)}, u32[]{:S(2)}, u32[]{:S(2)}) collective-permute-start(bf16[1,32,2048]{2,1,0:T(8,128)(2,1)S(1)} %add_convert_fusion.35), channel_id=1, source_target_pairs={{0,16},{1,17},{2,18},{3,19},{4,20},{5,21},{6,22},{7,23},{8,24},{9,... | collective-permute-start | bytes 393224 | tf_op jit(solution)/shard_map/ppermute | solution.py:781
  526.4 30.1 %collective-permute-start.5 = (bf16[1,32,2176]{2,1,0:T(8,128)(2,1)S(1)}, bf16[1,32,2176]{2,1,0:T(8,128)(2,1)S(1)}, u32[]{:S(2)}, u32[]{:S(2)}) collective-permute-start(bf16[1,32,2176]{2,1,0:T(8,128)(2,1)S(1)} %add_convert_fusion.29), channel_id=1, source_target_pairs={{0,16},{1,17},{2,18},{3,19},{4,20},{5,21},{6,22},{7,23},{8,24},{9,... | collective-permute-start | bytes 417800 | tf_op jit(solution)/shard_map/ppermute | solution.py:781
  536.1 2.3 copy-start.7
  537.2 16.4 %collective-permute-start.23 = (bf16[4,128,1024]{2,1,0:T(8,128)(2,1)S(1)}, bf16[4,128,1024]{2,1,0:T(8,128)(2,1)S(1)}, u32[]{:S(2)}, u32[]{:S(2)}) collective-permute-start(bf16[4,128,1024]{2,1,0:T(8,128)(2,1)S(1)} %get-tuple-element.202), channel_id=1, source_target_pairs={{0,1},{1,0},{2,3},{3,2},{4,5},{5,4},{6,7},{7,6},{8,9},{9,8},{10,11... | collective-permute-start | bytes 3145736 | tf_op jit(solution)/shard_map/ppermute | solution.py:781
  539.2 15.9 %collective-permute-start.19 = (bf16[4,32,4096]{2,1,0:T(8,128)(2,1)S(1)}, bf16[4,32,4096]{2,1,0:T(8,128)(2,1)S(1)}, u32[]{:S(2)}, u32[]{:S(2)}) collective-permute-start(bf16[4,32,4096]{2,1,0:T(8,128)(2,1)S(1)} %get-tuple-element.204), channel_id=1, source_target_pairs={{0,2},{1,3},{2,0},{3,1},{4,6},{5,7},{6,4},{7,5},{8,10},{9,11},{10,... | collective-permute-start | bytes 3145736 | tf_op jit(solution)/shard_map/ppermute | solution.py:781
  554.0 12.9 %collective-permute-start.24 = (bf16[2,128,1024]{2,1,0:T(8,128)(2,1)S(1)}, bf16[2,128,1024]{2,1,0:T(8,128)(2,1)S(1)}, u32[]{:S(2)}, u32[]{:S(2)}) collective-permute-start(bf16[2,128,1024]{2,1,0:T(8,128)(2,1)S(1)} %get-tuple-element.206), channel_id=1, source_target_pairs={{0,8},{1,9},{2,10},{3,11},{4,12},{5,13},{6,14},{7,15},{8,0},{9,1},... | collective-permute-start | bytes 1572872 | tf_op jit(solution)/shard_map/ppermute | solution.py:781
  555.3 22.7 %collective-permute-start.20 = (bf16[2,32,4096]{2,1,0:T(8,128)(2,1)S(1)}, bf16[2,32,4096]{2,1,0:T(8,128)(2,1)S(1)}, u32[]{:S(2)}, u32[]{:S(2)}) collective-permute-start(bf16[2,32,4096]{2,1,0:T(8,128)(2,1)S(1)} %get-tuple-element.208), channel_id=1, source_target_pairs={{0,8},{1,9},{2,10},{3,11},{4,12},{5,13},{6,14},{7,15},{8,0},{9,1},... | collective-permute-start | bytes 1572872 | tf_op jit(solution)/shard_map/ppermute | solution.py:781
  566.9 21.2 %copy-start.1 = (bf16[1,512,1024]{2,1,0:T(8,128)(2,1)S(1)}, bf16[1,512,1024]{2,1,0:T(8,128)(2,1)}, u32[]{:S(2)}) copy-start(bf16[1,512,1024]{2,1,0:T(8,128)(2,1)} %param.19) | copy-start | bytes 3145732
  567.0 11.9 %collective-permute-start.25 = (bf16[1,128,1024]{2,1,0:T(8,128)(2,1)S(1)}, bf16[1,128,1024]{2,1,0:T(8,128)(2,1)S(1)}, u32[]{:S(2)}, u32[]{:S(2)}) collective-permute-start(bf16[1,128,1024]{2,1,0:T(8,128)(2,1)S(1)} %add_convert_fusion.19), channel_id=1, source_target_pairs={{0,16},{1,17},{2,18},{3,19},{4,20},{5,21},{6,22},{7,23},{8,24},{9,... | collective-permute-start | bytes 786440 | tf_op jit(solution)/shard_map/ppermute | solution.py:781
  578.1 9.1 %collective-permute-start.21 = (bf16[1,32,4096]{2,1,0:T(8,128)(2,1)S(1)}, bf16[1,32,4096]{2,1,0:T(8,128)(2,1)S(1)}, u32[]{:S(2)}, u32[]{:S(2)}) collective-permute-start(bf16[1,32,4096]{2,1,0:T(8,128)(2,1)S(1)} %add_convert_fusion.21), channel_id=1, source_target_pairs={{0,16},{1,17},{2,18},{3,19},{4,20},{5,21},{6,22},{7,23},{8,24},{9,... | collective-permute-start | bytes 786440 | tf_op jit(solution)/shard_map/ppermute | solution.py:781
  (2 other events, 2.1 us)
Sparse Core Ops, SparseCore 0:
  77.5 126.7 all-gather.2

commit v2 on v1

--- a/solution.py
+++ b/solution.py
@@ -74,6 +74,103 @@
 
 def twice(row):
     return jnp.concatenate([row, row], axis=1)
+
+
+def arrange_kernel(
+    map_ref, page_column, page_row, tokens, g, columns,
+    count, order, new_column, new_row, inputs, new_g, hidden, unit, inverse, *gains,
+):
+    rows = tokens.shape[0]
+
+    def second_of(pages):
+        return sum(jnp.where(pages == p, map_ref[p], 0) for p in range(map_ref.shape[0])).astype(f32)
+
+    column, row = second_of(page_column[...]), second_of(page_row[...])
+    i = lax.broadcasted_iota(jnp.int32, (rows, rows), 0)
+    j = lax.broadcasted_iota(jnp.int32, (rows, rows), 1)
+    before_column = jnp.sum(jnp.where(j < i, row, 0.0), axis=1, keepdims=True)
+    before_row = jnp.sum(jnp.where(i < j, column, 0.0), axis=0, keepdims=True)
+    first = rows - jnp.sum(row)
+    count[0] = first.astype(jnp.int32)
+    at_column = lax.broadcasted_iota(jnp.int32, (rows, 1), 0).astype(f32)
+    at_row = lax.broadcasted_iota(jnp.int32, (1, rows), 1).astype(f32)
+    place_column = jnp.where(column > 0, first + before_column, at_column - before_column)
+    place_row = jnp.where(row > 0, first + before_row, at_row - before_row)
+    moved = i.astype(f32) == place_row
+    order[...] = moved.astype(f32).astype(bf16)
+    pages = page_row[...].astype(f32)
+    new_column[...] = jnp.sum(jnp.where(moved, pages, 0.0), axis=1, keepdims=True).astype(jnp.int32)
+    pages = page_column[...].astype(f32)
+    back = place_column == j.astype(f32)
+    new_row[...] = jnp.sum(jnp.where(back, pages, 0.0), axis=0, keepdims=True).astype(jnp.int32)
+    new_g[...] = product(order[...], g[...]).astype(bf16)
+    flat = columns[...].astype(f32).T
+    for number, gain in enumerate(gains):
+        gain[...] = flat[number : number + 1, :]
+    inputs[...] = product(order[...], tokens[...])
+    h, unit[...], inverse[...] = normed(inputs[...], gains[0][...])
+    hidden[...] = h.astype(bf16)
+
+
+def arrange(image_map, pages, tokens, g, weights, first):
+    rows, width = tokens.shape
+
+    def whole(*shape):
+        return pl.BlockSpec(shape, lambda s: (0,) * len(shape))
+
+    scalars = pl.BlockSpec(memory_space=pltpu.SMEM)
+    kinds = [
+        ((rows, rows), bf16), ((rows, 1), jnp.int32), ((1, rows), jnp.int32),
+        ((rows, width), f32), ((rows, width), bf16), ((rows, width), bf16),
+        ((rows, width), f32), ((rows, 1), f32), *[((1, width), f32)] * 3,
+    ]
+    return pl.pallas_call(
+        arrange_kernel,
+        grid=(1,),
+        in_specs=[
+            scalars, whole(rows, 1), whole(1, rows), whole(rows, width), whole(rows, width),
+            pl.BlockSpec((width, 128), lambda s: (0, first)),
+        ],
+        out_specs=[scalars] + [whole(*shape) for shape, _ in kinds],
+        out_shape=[jax.ShapeDtypeStruct((1,), jnp.int32)]
+        + [jax.ShapeDtypeStruct(shape, dtype) for shape, dtype in kinds],
+        compiler_params=params(1),
+        name="arrange",
+        cost_estimate=cost(6),
+    )(image_map, pages[:, None], pages[None, :], tokens, g, weights)
+
+
+def between_kernel(x_ref, mixed, w_out, w_query, gain, x_out, hidden, unit, inverse, query):
+    x = x_ref[...] + product(mixed[...], w_out[...])
+    x_out[...] = x
+    h, unit[...], inverse[...] = normed(x, gain[...])
+    hidden[...] = h.astype(bf16)
+    query[...] = product(hidden[...], w_query[...]).astype(bf16)
+
+
+def between(x, mixed, weights, gain):
+    rows, width = x.shape
+    tile = rows // 2
+
+    def part(columns):
+        return pl.BlockSpec((tile, columns), lambda s: (s, 0))
+
+    kinds = ((width, f32), (width, bf16), (width, f32), (1, f32), (width, bf16))
+    return pl.pallas_call(
+        between_kernel,
+        grid=(2,),
+        in_specs=[
+            part(width), part(width),
+            pl.BlockSpec((width, width), lambda s: (0, 0)),
+            pl.BlockSpec((width, width), lambda s: (0, 1)),
+            pl.BlockSpec((1, width), lambda s: (0, 0)),
+        ],
+        out_specs=[part(columns) for columns, _ in kinds],
+        out_shape=[jax.ShapeDtypeStruct((rows, columns), dtype) for columns, dtype in kinds],
+        compiler_params=params(1),
+        name="between",
+        cost_estimate=cost(8),
+    )(x, mixed, weights, weights, gain)
 
 
 def key_range(tile):
@@ -113,7 +210,7 @@
         totals[0, 1:2, here] = level[:, TILE:]
 
 
-def self_forward(pages, qkv):
+def self_forward(page_column, page_row, qkv):
     rows, width = qkv.shape[0], qkv.shape[1] // 3
     pairs = width // 128
     return pl.pallas_call(
@@ -138,7 +235,7 @@
         compiler_params=params(1),
         name="self_forward",
         cost_estimate=cost(14),
-    )(pages[:, None], pages[None, :], qkv, qkv, qkv)
+    )(page_column, page_row, qkv, qkv, qkv)
 
 
 def self_backward_kernel(page_column, page_row, q, k, v, g, totals, out, bias, dk, dv):
@@ -170,7 +267,7 @@
     out[2] = dv[...].astype(bf16)
 
 
-def self_backward(pages, qkv, grads, totals):
+def self_backward(page_column, page_row, qkv, grads, totals):
     rows, width = qkv.shape[0], qkv.shape[1] // 3
     pairs = width // 128
     return pl.pallas_call(
@@ -195,7 +292,7 @@
         compiler_params=params(1),
         name="self_backward",
         cost_estimate=cost(15),
-    )(pages[:, None], pages[None, :], qkv, qkv, qkv, grads, totals)
+    )(page_column, page_row, qkv, qkv, qkv, grads, totals)
 
 
 def cross_steps(count, tiles):
@@ -477,7 +574,9 @@
     )(left, right, *into)
 
 
-def norm_grad_kernel(d_ref, w_ref, unit, inverse, gain, g_ref, out, low, gain_out, total):
+def norm_grad_kernel(d_ref, w_ref, unit, inverse, gain, g_ref, *refs):
+    *then, total = refs
+    then_w, out, low, gain_out, then_out = then if len(then) == 5 else (None, *then, None)
     step = pl.program_id(0)
     kinds, _, width = d_ref.shape
     part = product_t(d_ref[0], w_ref[:, :width])
@@ -493,9 +592,11 @@
         out[...] = result
         low[...] = result.astype(bf16)
         gain_out[...] = gain_grad[None, :]
-
-
-def norm_grad(grads, weights, first, unit, inverse, gain, g):
+        if then_w is not None:
+            then_out[...] = product_t(low[...], then_w[...]).astype(bf16)
+
+
+def norm_grad(grads, weights, first, unit, inverse, gain, g, then=False):
     kinds, rows, width = grads.shape
     wide = 256
 
@@ -509,23 +610,26 @@
             whole((kinds, rows, width)),
             pl.BlockSpec((wide, kinds * width), lambda j: (j, first)),
             whole((rows, width)), whole((rows, 1)), whole((1, width)), whole((rows, width)),
-        ],
-        out_specs=[whole((rows, width)), whole((rows, width)), whole((1, width))],
+            *[whole((width, width))] * then,
+        ],
+        out_specs=[whole((rows, width)), whole((rows, width)), whole((1, width))]
+        + [whole((rows, width))] * then,
         out_shape=[
             jax.ShapeDtypeStruct((rows, width), f32),
             jax.ShapeDtypeStruct((rows, width), bf16),
             jax.ShapeDtypeStruct((1, width), f32),
+            *[jax.ShapeDtypeStruct((rows, width), bf16)] * then,
         ],
         scratch_shapes=[pltpu.VMEM((rows, width), f32)],
         compiler_params=params(1),
         name="norm_grad",
         cost_estimate=cost(4 * kinds),
-    )(grads, weights, unit, inverse, gain, g)
+    )(grads, weights, unit, inverse, gain, g, *[weights] * then)
 
 
 def feed_kernel(
-    devices, lanes, ways, x_ref, g_ref, gain_ref, up_ref, down_ref,
-    out, gx, low_gx, ggain, up_out, up_keep, down_out, down_keep,
+    devices, lanes, ways, x_ref, mixed_ref, w_ref, g_ref, gain_ref, up_ref, down_ref,
+    out, gx, low_gx, grad_mixed, ggain, up_out, up_keep, down_out, down_keep,
     unit, inverse, hidden, staged, flipped, total, back,
     up_sent, up_own, up_came, down_sent, down_own, down_came,
     up_send_sem, up_recv_sem, down_send_sem, down_recv_sem,
@@ -538,13 +642,14 @@
     @pl.when(step == 0)
     def _():
         greet(partner)
-        h, u, i = normed(x_ref[...], gain_ref[...])
+        x = x_ref[...] + product(mixed_ref[...], w_ref[...])
+        h, u, i = normed(x, gain_ref[...])
         unit[...] = u
         inverse[...] = i
         hidden[...] = h.astype(bf16)
         put_rows(me, devices, lanes, ways[0], h, staged)
         flipped[...] = staged[...].astype(bf16)
-        total[...] = jnp.zeros_like(total)
+        total[...] = x
         back[...] = jnp.zeros_like(back)
 
     def up_copy(at):
@@ -586,11 +691,12 @@
 
     @pl.when(step == groups)
     def _():
-        out[...] = (x_ref[...] + total[...]).astype(bf16)
+        out[...] = total[...].astype(bf16)
         gx_norm, gain_grad = norm_back(unit[...], inverse[...], gain_ref[...], back[...])
         result = g_ref[...].astype(f32) + gx_norm
         gx[...] = result
         low_gx[...] = result.astype(bf16)
+        grad_mixed[...] = product_t(low_gx[...], w_ref[...]).astype(bf16)
         ggain[...] = gain_grad[None, :]
 
     @pl.when(step > 0)
@@ -623,7 +729,7 @@
                     down_keep[place] = piece
 
 
-def feed(number, devices, lanes, ways, x, g, gain, weights):
+def feed(number, devices, lanes, ways, x, mixed, projection, g, gain, weights):
     rows, width = x.shape
     pieces, depth = weights.shape[2:4]
     hidden = pieces * width
@@ -635,8 +741,9 @@
         return jnp.minimum(s, groups - 1)
 
     def whole(shape):
-        return pl.BlockSpec(shape, lambda s: (0,) * len(shape))
-
+        return pl.BlockSpec(shape, lambda s: (0,) * len(shape), pipeline_mode=pl.Buffered(1))
+
+    last = projection.shape[1] // width - 1
     up_block = pl.BlockSpec((devices // 4, depth, tile), lambda s: (0, 0, jnp.maximum(s - 1, 0)))
     up_shape = jax.ShapeDtypeStruct((devices // 4, depth, hidden), bf16)
     down_shape = jax.ShapeDtypeStruct((devices // 4, hidden // devices, width), bf16)
@@ -646,6 +753,8 @@
         in_specs=[
             whole((rows, width)),
             whole((rows, width)),
+            pl.BlockSpec((width, width), lambda s: (0, last), pipeline_mode=pl.Buffered(1)),
+            whole((rows, width)),
             whole((1, width)),
             pl.BlockSpec(
                 (devices, None, None, depth, tile),
@@ -654,7 +763,7 @@
             pl.BlockSpec((lanes, None, pieces, depth, width), lambda s: (group(s), 1, 0, 0, 0)),
         ],
         out_specs=[
-            whole((rows, width)), whole((rows, width)), whole((rows, width)), whole((1, width)),
+            *[whole((rows, width))] * 4, whole((1, width)),
             up_block, up_block, whole(down_shape.shape), whole(down_shape.shape),
         ],
         scratch_shapes=[
@@ -680,6 +789,7 @@
             jax.ShapeDtypeStruct((rows, width), bf16),
             jax.ShapeDtypeStruct((rows, width), f32),
             jax.ShapeDtypeStruct((rows, width), bf16),
+            jax.ShapeDtypeStruct((rows, width), bf16),
             jax.ShapeDtypeStruct((1, width), f32),
             up_shape, up_shape, down_shape, down_shape,
         ],
@@ -691,7 +801,7 @@
         ),
         name="feed",
         cost_estimate=cost(40),
-    )(x, g, gain, weights, weights)
+    )(x, mixed, projection, g, gain, weights, weights)
 
 
 def gather_kernel(devices, lanes, tracks, x_ref, out, own_sem, send_sem, recv_sem):
@@ -840,43 +950,19 @@
     feed_set = lax.all_gather(after(feed_set, first_set), AXES, axis=0)
     w_qkv = first_set[:, : 3 * width]
     w_kv = first_set[:, 3 * width : 5 * width]
-    gains = first_set[:, 5 * width : 5 * width + 3].T.astype(f32)
-
-    pages = segment_ids[0]
-    length = pages.shape[0]
-    page_index = jnp.arange(image_map.shape[1])
-    second = jnp.sum(jnp.where(pages[:, None] == page_index[None, :], image_map[0][None, :], 0), axis=1)
-    place_now = jnp.arange(length)
-    earlier = place_now[None, :] < place_now[:, None]
-    ones_before = jnp.sum(jnp.where(earlier, second[None, :], 0), axis=1)
-    count = length - jnp.sum(second)
-    place = jnp.where(second == 1, count + ones_before, place_now - ones_before)
-    moved = place_now[:, None] == place[None, :]
-    order = moved.astype(bf16)
-    count = count.astype(jnp.int32)[None]
-    pages = jnp.sum(jnp.where(moved, pages[None, :], 0), axis=1)
-    inputs = product(order, tokens[0])
-    grad_out = product(order, out_grad[0]).astype(bf16)
-
-    hidden_one, unit_one, inverse_one = normed(inputs, gains[0:1])
-    hidden_one = hidden_one.astype(bf16)
+    (count, order, page_column, page_row, inputs, grad_out, hidden_one, unit_one, inverse_one, *gains) = arrange(
+        image_map[0], segment_ids[0], tokens[0], out_grad[0], first_set, 5 * width // 128
+    )
     qkv = product(hidden_one, w_qkv).astype(bf16)
-    mixed_one, log_one = self_forward(pages, qkv)
+    mixed_one, log_one = self_forward(page_column, page_row, qkv)
     kv = lax.dot_general(images, w_kv, (((2,), (0,)), ((), ())), preferred_element_type=f32).astype(bf16)
     second_set = gather(1, devices, lanes, after(second_set, (mixed_one, kv)))
-    w_out = second_set[:, :width]
-    w_cross_query = second_set[:, width : 2 * width]
-    w_cross_out = second_set[:, 2 * width :]
-    after_self = inputs + product(mixed_one, w_out)
-    hidden_two, unit_two, inverse_two = normed(after_self, gains[1:2])
-    hidden_two = hidden_two.astype(bf16)
-    query_two = product(hidden_two, w_cross_query).astype(bf16)
+    after_self, hidden_two, unit_two, inverse_two, query_two = between(inputs, mixed_one, second_set, gains[1])
     mixed_two, log_two = cross_forward(count, query_two, kv)
-    after_cross = after_self + product(mixed_two, w_cross_out)
 
     one_way, other_way = orders(lanes)
-    (output, grad_after_cross, branch_two, grad_gain_ffn, *halves) = feed(
-        2, devices, lanes, (one_way, other_way), after_cross, grad_out, gains[2:3], feed_set
+    (output, grad_after_cross, branch_two, grad_mixed_two, grad_gain_ffn, *halves) = feed(
+        2, devices, lanes, (one_way, other_way), after_self, mixed_two, second_set, grad_out, gains[2], feed_set
     )
 
     def sums(way, halves, late=None):
@@ -888,34 +974,33 @@
     grad_up = sums(one_way, halves[:2])
     grad_down = sums(other_way, halves[2:])
 
-    grad_mixed_two = product_t(branch_two, w_cross_out).astype(bf16)
     grad_query_two, grad_kv = cross_backward(count, query_two, kv, grad_mixed_two, log_two)
     halves = halves_of(3, one_way, mixed_two[None], after(branch_two, grad_kv)[None, None])
     halves = halves_of(4, one_way, hidden_two[None], grad_query_two[None, None], first=width, into=halves)
     grad_c = sums(one_way, halves)
     halves = halves_of(5, other_way, images, after(grad_kv, halves[0]))
     grad_d = sums(other_way, halves)
-    grad_after_self, branch_one, grad_gain_cross = norm_grad(
-        after(grad_query_two, halves[0])[None], second_set, 1, unit_two, inverse_two, gains[1:2], grad_after_cross
+    grad_query_again = after(grad_query_two, halves[0])[None]
+    grad_after_self, branch_one, grad_gain_cross, grad_mixed_one = norm_grad(
+        grad_query_again, second_set, 1, unit_two, inverse_two, gains[1], grad_after_cross, then=True
     )
-    grad_mixed_one = product_t(branch_one, w_out).astype(bf16)
-    grad_qkv = self_backward(pages, qkv, grad_mixed_one, log_one)
+    grad_qkv = self_backward(page_column, page_row, qkv, grad_mixed_one, log_one)
     halves = halves_of(6, one_way, mixed_one[None], after(branch_one, grad_qkv)[None, None])
     options = dict(first=width, into=halves, only=(0, 1))
     halves = halves_of(7, one_way, hidden_one[None], grad_qkv[:, None], **options)
     grad_qkv_again = after(grad_qkv, halves[0])
+    halves_kv = halves_of(8, one_way, hidden_one[None], grad_qkv_again[:, None], only=(1, 3))
+    grad_qkv_again = after(grad_qkv, halves_kv[0])
     _, grad_inputs, grad_gain_self = norm_grad(
-        grad_qkv_again, first_set, 0, unit_one, inverse_one, gains[0:1], grad_after_self
+        grad_qkv_again, first_set, 0, unit_one, inverse_one, gains[0], grad_after_self
     )
-    grad_qkv_again = after(grad_qkv, grad_inputs)
-    halves_kv = halves_of(8, one_way, hidden_one[None], grad_qkv_again[:, None], only=(1, 3))
     gain_grads = jnp.concatenate([grad_gain_self, grad_gain_cross, grad_gain_ffn])
     late = gain_halves(gain_grads, devices, lanes, one_way, me)
     grad_a = sums(one_way, halves)
     grad_b = sums(one_way, halves_kv, late)
     gain_sums = grad_b[:, 2 * width :]
 
-    grad_kv = after(grad_kv, halves_kv[0])
+    grad_kv = after(grad_kv, late[0])
     back = (((2,), (1,)), ((), ()))
     grad_images = lax.dot_general(grad_kv[0], w_kv[:, :width], back, preferred_element_type=f32)
     grad_images += lax.dot_general(grad_kv[1], w_kv[:, width:], back, preferred_element_type=f32)

time: 600 us -> 591 us (0.985)
  Pallas kernels: 327 us -> 347 us
  matrix products: 50.6 us -> 32.1 us
  starting transfers between devices: 22.7 us -> 31.2 us
  waiting for transfers between devices: 135 us -> 128 us
  other arithmetic: 20.2 us -> 13.6 us
  local copies, waits for them, and re-layouts: 24.7 us -> 18.2 us
    pallas_call x0 -> x2, Pallas kernels: none -> 13.6 us  [the longest x1 7.27 us: between(): pl.pallas_call(between_kernel, grid=(2,), in_specs=[part(width), part(wid...]
    dot_general x6 -> x1, matrix products: 21.7 us -> 8.35 us  [product(): return jnp.dot(left, right, preferred_element_type=f32)]
    ppermute x26, starting transfers between devices: 22.7 us -> 31.1 us  [swap(): return lax.ppermute(values, AXES, [(i, i ^ bit) for i in range(devices)])]
    dot_general x2 -> x0, matrix products: 8.39 us -> none  [product_t(): lax.dot_general(left, right, (((1,), (1,)), ((), ())), preferred_element_...]
    ppermute x26, waiting for transfers between devices: 135 us -> 128 us  [swap(): return lax.ppermute(values, AXES, [(i, i ^ bit) for i in range(devices)])]
    unnamed x86 -> x55, local copies, waits for them, and re-layouts: 14.5 us -> 11.1 us
  transfers between devices with their start and end apart: 27 -> 27, of which waited for: 12 -> 12; matrix products, arithmetic and copies ran while one was open for 13% -> 10% of each run, Pallas kernels for 29% -> 32%
where the time goes in v2:
time: 591 us; the launch traced here: 584 us
  Pallas kernels  347 us (59%)
  waiting for transfers between devices  128 us (22%)
  matrix products  32.1 us (5%)
  starting transfers between devices  31.2 us (5%)
  local copies, waits for them, and re-layouts  18.2 us (3%)
  between operations  15.1 us (3%)
  other arithmetic  13.6 us (2%)
    ppermute x26, waiting for transfers between devices, swap(): return lax.ppermute(values, AXES, [(i, i ^ bit) for i in range(devices)])  128 us
    pallas_call x2, Pallas kernels, gather(): pl.pallas_call(functools.partial(gather_kernel, devices, lanes, tracks),...  114 us
    pallas_call x6, Pallas kernels, weight_grad(): pl.pallas_call(functools.partial(weight_grad_kernel, devices, lanes, way,...  52.6 us
    pallas_call x1, Pallas kernels, feed(): pl.pallas_call(functools.partial(feed_kernel, devices, lanes, ways), grid...  49.5 us
    pallas_call x1, Pallas kernels, cross_backward(): pl.pallas_call(cross_backward_kernel, grid_spec=pltpu.PrefetchScalarGridS...  35.5 us
    ppermute x26, starting transfers between devices, swap(): return lax.ppermute(values, AXES, [(i, i ^ bit) for i in range(devices)])  31.1 us
    pallas_call x1, Pallas kernels, cross_forward(): pl.pallas_call(cross_forward_kernel, grid_spec=pltpu.PrefetchScalarGridSp...  30.5 us
    pallas_call x2, Pallas kernels, norm_grad(): pl.pallas_call(norm_grad_kernel, grid=(width // wide,), in_specs=[whole((...  21.3 us
  transfers between devices with their start and end apart: 27, of which 12 were waited for; matrix products, arithmetic and copies ran while one was open for 10% of the time, Pallas kernels for 32%

profile of v2, /device:TPU:0, one launch (start us, length us, event | category | flops | bytes accessed | tf_op | source)
XLA Modules:
  0.0 584.3 jit_solution(12803484075496235410)
XLA Ops:
  7.2 0.8 constant_dynamic-update-slice_fusion.5
  8.9 0.8 constant_dynamic-update-slice_fusion.4
  9.7 0.8 constant_dynamic-update-slice_fusion.3
  10.6 0.8 constant_dynamic-update-slice_fusion.2
  11.4 0.8 constant_dynamic-update-slice_fusion.1
  13.0 60.7 %gather.19 = bf16[32,32,5248]{2,1,0:T(8,128)(2,1)} custom-call(bf16[32,5248]{1,0:T(8,128)(2,1)} %copy-done.13), custom_call_target="tpu_custom_call" | custom-call | flops 40000000000 | tf_op jit(solution)/shard_map/gather/pallas_call | solution.py:874
  74.5 1.0 copy.75
  75.5 0.9 copy.72.page_column
  76.4 2.2 copy.73.refs_0_
  79.2 6.3 %arrange.1 = (s32[1]{0:T(128)}, bf16[512,512]{1,0:T(8,128)(2,1)}, s32[512,1]{1,0:T(8,128)}, s32[1,512]{1,0:T(1,128)}, f32[512,1024]{1,0:T(8,128)}, /*index=5*/bf...) custom-call(s32[4]{0:T(128)} %bitcast.90, ...), custom_call_target="tpu_custom_call" | custom-call | flops 6000000000 | tf_op jit(solution)/shard_map/arrange/pallas_call | solution.py:127
  85.6 8.3 %fusion.2.q.k.v = bf16[512,3072]{1,0:T(8,128)(2,1)} fusion(bf16[512,1024]{1,0:T(8,128)(2,1)} %get-tuple-element.79, bf16[1024,5248]{1,0:T(8,128)(2,1)} %bitcast.92), kind=kOutput, calls=%fused_computation.5 | convolution fusion | flops 3222798336 | bytes 10485760 | tf_op jit(solution)/shard_map/dot_general | solution.py:24
  94.0 9.2 %convert_bitcast_fusion.k.v = bf16[2,588,2048]{2,1,0:T(8,128)(2,1)} fusion(bf16[1024,5248]{1,0:T(8,128)(2,1)} %bitcast.93, bf16[2,588,1024]{2,0,1:T(2,128)(2,1)S(1)} %copy-done.1), kind=kOutput, calls=%fused_computation.4 | convolution fusion | flops 4934909952 | bytes 11419648 | tf_op jit(solution)/shard_map/dot_general | solution.py:958
  103.1 14.1 %self_forward.1 = (bf16[512,1024]{1,0:T(8,128)(2,1)}, f32[8,2,512]{2,1,0:T(2,128)}) custom-call(s32[512,1]{1,0:T(8,128)} %get-tuple-element.77.page_column, s32[1,512]{1,0:T(1,128)} %get-tuple-element.78.page_row, bf16[512,3072]{1,0:T(8,128)(2,1)} %fusion.2.q.k.v, bf16[512,3072]{1,0:T(8,128)(2,1)} %fusion.2.q.k.v, bf16[512,3072]{1,0:T(8,128)(2,1)} %fusion.2.q.k.v), custom_call_target="tpu_custom_call" | custom-call | flops 14000000000 | tf_op jit(solution)/shard_map/self_forward/pallas_call | solution.py:216
  117.9 53.7 %gather.20 = bf16[32,32,3072]{2,1,0:T(8,128)(2,1)} custom-call(bf16[32,3072]{1,0:T(8,128)(2,1)} %pad_maximum_fusion.3.x_ref), custom_call_target="tpu_custom_call" | custom-call | flops 40000000000 | tf_op jit(solution)/shard_map/gather/pallas_call | solution.py:874
  171.6 7.3 %between.1 = (f32[512,1024]{1,0:T(8,128)}, bf16[512,1024]{1,0:T(8,128)(2,1)}, f32[512,1024]{1,0:T(8,128)}, f32[512,1]{1,0:T(8,128)}, bf16[512,1024]{1,0:T(8,128)(2,1)}) custom-call(f32[512,1024]{1,0:T(8,128)} %get-tuple-element.76.x_ref, bf16[512,1024]{1,0:T(8,128)(2,1)} %get-tuple-element.80.mixed, bf16[1024,3072]{1,0:T(8,128)(2,1)} %bitcast.72, ...), custom_call_target="tpu_custom_call" | custom-call | flops 8000000000 | tf_op jit(solution)/shard_map/between/pallas_call | solution.py:159
  178.8 30.5 %cross_forward.1 = (bf16[512,1024]{1,0:T(8,128)(2,1)}, f32[8,2,512]{2,1,0:T(2,128)}) custom-call(s32[1]{0:T(128)} %get-tuple-element.84.count_ref, bf16[512,1024]{1,0:T(8,128)(2,1)} %get-tuple-element.85.q, bf16[2,588,2048]{2,1,0:T(8,128)(2,1)} %convert_bitcast_fusion.k.v, bf16[2,588,2048]{2,1,0:T(8,128)(2,1)} %convert_bitcast_fusion.k.v), custom_call_target="tpu_custom_call" | custom-call | flops 24000000000 | tf_op jit(solution)/shard_map/cross_forward/pallas_call | solution.py:340
  209.4 49.5 %feed.1 = (bf16[512,1024]{1,0:T(8,128)(2,1)}, f32[512,1024]{1,0:T(8,128)}, bf16[512,1024]{1,0:T(8,128)(2,1)}, bf16[512,1024]{1,0:T(8,128)(2,1)}, f32[1,1024]{1,0...) custom-call(f32[512,1024]{1,0:T(8,128)} %get-tuple-element.83.x_ref,, ...), custom_call_target="tpu_custom_call" | custom-call | flops 40000000000 | tf_op jit(solution)/shard_map/feed/pallas_call | solution.py:750
  258.8 35.5 %cross_backward.1 = (bf16[512,1024]{1,0:T(8,128)(2,1)}, bf16[2,2,588,1024]{3,2,1,0:T(8,128)(2,1)}) custom-call(s32[1]{0:T(128)} %get-tuple-element.84.count_ref, bf16[512,1024]{1,0:T(8,128)(2,1)} %get-tuple-element.85.q, bf16[2,588,2048]{2,1,0:T(8,128)(2,1)} %convert_bitcast_fusion.k.v, bf16[2,588,2048]{2,1,0:T(8,128)(2,1)} %convert_bitcast_fusion.k.v, ...), custom_call_target="tpu_custom_call" | custom-call | flops 28000000000 | tf_op jit(solution)/shard_map/cross_backward/pallas_call | solution.py:405
  294.4 7.1 %weight_grad.6 = (bf16[8,32,2048]{2,1,0:T(8,128)(2,1)}, bf16[8,32,2048]{2,1,0:T(8,128)(2,1)}) custom-call(bf16[1,512,1024]{2,1,0:T(8,128)(2,1)} %bitcast.103, bf16[1,1,512,1024]{3,2,1,0:T(8,128)(2,1)} %bitcast.104), custom_call_target="tpu_custom_call" | custom-call | flops 3000000000 | tf_op jit(solution)/shard_map/weight_grad/pallas_call | solution.py:546
  301.5 7.2 %weight_grad.7 = (bf16[8,32,2048]{2,1,0:T(8,128)(2,1)}, bf16[8,32,2048]{2,1,0:T(8,128)(2,1)}) custom-call(bf16[1,512,1024]{2,1,0:T(8,128)(2,1)} %bitcast.102, bf16[1,1,512,1024]{3,2,1,0:T(8,128)(2,1)} %bitcast.77, bf16[8,32,2048]{2,1,0:T(8,128)(2,1)} %get-tuple-element.98.refs_2_, ...), custom_call_target="tpu_custom_call", output_to_operand_aliasing={{0}: (2, {}), {1}: (3, {})} | custom-call | flops 3000000000 | tf_op jit(solution)/shard_map/weight_grad/pallas_call | solution.py:546
  308.7 2.7 collective-permute-start.10
  311.4 14.3 %weight_grad.8 = (bf16[8,32,2048]{2,1,0:T(8,128)(2,1)}, bf16[8,32,2048]{2,1,0:T(8,128)(2,1)}) custom-call(bf16[2,588,1024]{2,1,0:T(8,128)(2,1)} %copy.73.refs_0_, bf16[2,2,588,1024]{3,2,1,0:T(8,128)(2,1)} %get-tuple-element.125.refs_1_), custom_call_target="tpu_custom_call" | custom-call | flops 12000000000 | tf_op jit(solution)/shard_map/weight_grad/pallas_call | solution.py:546
  325.9 10.2 %norm_grad.2 = (f32[512,1024]{1,0:T(8,128)}, bf16[512,1024]{1,0:T(8,128)(2,1)}, f32[1,1024]{1,0:T(1,128)}, bf16[512,1024]{1,0:T(8,128)(2,1)}) custom-call(bf16[1,512,1024]{2,1,0:T(8,128)(2,1)} %bitcast.78, bf16[1024,3072]{1,0:T(8,128)(2,1)} %bitcast.75, f32[512,1024]{1,0:T(8,128)} %get-tuple-element.104.unit, f32[512,1]{1,0:T(8,128)} %get-tuple-element.105.inverse, ...), custom_call_target="tpu_custom_call" | custom-call | flops 4000000000 | tf_op jit(solution)/shard_map/norm_grad/pallas_call | solution.py:606
  336.1 15.0 %self_backward.1.d_ref = bf16[3,512,1024]{2,1,0:T(8,128)(2,1)} custom-call(s32[512,1]{1,0:T(8,128)} %get-tuple-element.77.page_column, s32[1,512]{1,0:T(1,128)} %get-tuple-element.78.page_row, bf16[512,3072]{1,0:T(8,128)(2,1)} %fusion.2.q.k.v, bf16[512,3072]{1,0:T(8,128)(2,1)} %fusion.2.q.k.v, bf16[512,3072]{1,0:T(8,128)(2,1)} %fusion.2.q.k.v, ...), custom_call_target="tpu_custom_call" | custom-call | flops 15000000512 | tf_op jit(solution)/shard_map/self_backward/pallas_call | solution.py:273
  351.1 7.0 %weight_grad.9 = (bf16[8,32,2048]{2,1,0:T(8,128)(2,1)}, bf16[8,32,2048]{2,1,0:T(8,128)(2,1)}) custom-call(bf16[1,512,1024]{2,1,0:T(8,128)(2,1)} %bitcast.101, bf16[1,1,512,1024]{3,2,1,0:T(8,128)(2,1)} %bitcast.89), custom_call_target="tpu_custom_call" | custom-call | flops 3000000000 | tf_op jit(solution)/shard_map/weight_grad/pallas_call | solution.py:546
  358.1 7.2 %weight_grad.10 = (bf16[8,32,2048]{2,1,0:T(8,128)(2,1)}, bf16[8,32,2048]{2,1,0:T(8,128)(2,1)}) custom-call(bf16[1,512,1024]{2,1,0:T(8,128)(2,1)} %bitcast.99, bf16[3,1,512,1024]{3,2,1,0:T(8,128)(2,1)} %bitcast.97, bf16[8,32,2048]{2,1,0:T(8,128)(2,1)} %get-tuple-element.111.refs_2_, ...), custom_call_target="tpu_custom_call", output_to_operand_aliasing={{0}: (2, {}), {1}: (3, {})} | custom-call | flops 3000000000 | tf_op jit(solution)/shard_map/weight_grad/pallas_call | solution.py:546
  365.3 2.0 collective-permute-start.6
  367.3 9.8 %weight_grad.11 = (bf16[8,32,2048]{2,1,0:T(8,128)(2,1)}, bf16[8,32,2048]{2,1,0:T(8,128)(2,1)}) custom-call(bf16[1,512,1024]{2,1,0:T(8,128)(2,1)} %bitcast.100, bf16[3,1,512,1024]{3,2,1,0:T(8,128)(2,1)} %bitcast.98), custom_call_target="tpu_custom_call" | custom-call | flops 6000000000 | tf_op jit(solution)/shard_map/weight_grad/pallas_call | solution.py:546
  377.3 11.1 %norm_grad.3 = (f32[512,1024]{1,0:T(8,128)}, bf16[512,1024]{1,0:T(8,128)(2,1)}, f32[1,1024]{1,0:T(1,128)}) custom-call(bf16[3,512,1024]{2,1,0:T(8,128)(2,1)} %self_backward.1.d_ref, bf16[1024,5248]{1,0:T(8,128)(2,1)} %bitcast.94, f32[512,1024]{1,0:T(8,128)} %get-tuple-element.117.unit, f32[512,1]{1,0:T(8,128)} %get-tuple-element.118.inverse, ...), custom_call_target="tpu_custom_call" | custom-call | flops 12000000000 | tf_op jit(solution)/shard_map/norm_grad/pallas_call | solution.py:606
  390.7 2.9 fusion.15
  393.7 1.7 fusion.14
  395.5 1.9 collective-permute-start.2
  397.3 5.0 fusion.6
  402.4 5.0 add_convert_fusion
  407.4 3.9 copy.79
  411.3 3.6 collective-permute-done.2
  414.9 1.7 collective-permute-start.22
  417.0 1.7 add_convert_fusion.10
  418.7 1.8 collective-permute-start.15
  421.3 1.6 add_convert_fusion.14
  422.9 1.7 collective-permute-start.7
  424.7 1.6 add_convert_fusion.16
  426.3 48.2 %collective-permute-done.15 = bf16[4,32,2048]{2,1,0:T(8,128)(2,1)S(1)} collective-permute-done((bf16[4,32,2048]{2,1,0:T(8,128)(2,1)S(1)}, bf16[4,32,2048]{2,1,0:T(8,128)(2,1)S(1)}, u32[]{:S(2)}, u32[]{:S(2)}) %collective-permute-start.15) | collective-permute-done | bytes 524320 | tf_op jit(solution)/shard_map/ppermute | solution.py:891
  475.4 10.5 %collective-permute-done.7 = bf16[4,32,2048]{2,1,0:T(8,128)(2,1)S(1)} collective-permute-done((bf16[4,32,2048]{2,1,0:T(8,128)(2,1)S(1)}, bf16[4,32,2048]{2,1,0:T(8,128)(2,1)S(1)}, u32[]{:S(2)}, u32[]{:S(2)}) %collective-permute-start.7) | collective-permute-done | bytes 524320 | tf_op jit(solution)/shard_map/ppermute | solution.py:891
  486.0 10.3 %collective-permute-done.3 = bf16[4,32,2176]{2,1,0:T(8,128)(2,1)S(1)} collective-permute-done((bf16[4,32,2176]{2,1,0:T(8,128)(2,1)S(1)}, bf16[4,32,2176]{2,1,0:T(8,128)(2,1)S(1)}, u32[]{:S(2)}, u32[]{:S(2)}) %collective-permute-start.3) | collective-permute-done | bytes 557088 | tf_op jit(solution)/shard_map/ppermute | solution.py:891
  496.5 2.1 collective-permute-start.4
  498.6 3.1 collective-permute-start.17
  501.8 8.0 %collective-permute-done.8 = bf16[2,32,2048]{2,1,0:T(8,128)(2,1)S(1)} collective-permute-done((bf16[2,32,2048]{2,1,0:T(8,128)(2,1)S(1)}, bf16[2,32,2048]{2,1,0:T(8,128)(2,1)S(1)}, u32[]{:S(2)}, u32[]{:S(2)}) %collective-permute-start.8) | collective-permute-done | bytes 262176 | tf_op jit(solution)/shard_map/ppermute | solution.py:891
  509.7 2.5 collective-permute-start.13
  512.3 1.1 collective-permute-done.4
  513.4 2.4 collective-permute-start.9
  517.2 8.8 %collective-permute-done.13 = bf16[1,32,2048]{2,1,0:T(8,128)(2,1)S(1)} collective-permute-done((bf16[1,32,2048]{2,1,0:T(8,128)(2,1)S(1)}, bf16[1,32,2048]{2,1,0:T(8,128)(2,1)S(1)}, u32[]{:S(2)}, u32[]{:S(2)}) %collective-permute-start.13) | collective-permute-done | bytes 131104 | tf_op jit(solution)/shard_map/ppermute | solution.py:891
  526.0 1.0 add_convert_fusion.2
  527.8 0.8 add_convert_fusion.4
  530.6 11.3 %collective-permute-done.23 = bf16[4,128,1024]{2,1,0:T(8,128)(2,1)S(1)} collective-permute-done((bf16[4,128,1024]{2,1,0:T(8,128)(2,1)S(1)}, bf16[4,128,1024]{2,1,0:T(8,128)(2,1)S(1)}, u32[]{:S(2)}, u32[]{:S(2)}) %collective-permute-start.23) | collective-permute-done | bytes 1048608 | tf_op jit(solution)/shard_map/ppermute | solution.py:891
  542.3 1.0 collective-permute-start.24
  543.7 1.0 collective-permute-start.20
  545.5 10.1 %collective-permute-done.24 = bf16[2,128,1024]{2,1,0:T(8,128)(2,1)S(1)} collective-permute-done((bf16[2,128,1024]{2,1,0:T(8,128)(2,1)S(1)}, bf16[2,128,1024]{2,1,0:T(8,128)(2,1)S(1)}, u32[]{:S(2)}, u32[]{:S(2)}) %collective-permute-start.24) | collective-permute-done | bytes 524320 | tf_op jit(solution)/shard_map/ppermute | solution.py:891
  555.6 2.1 collective-permute-start.25
  557.7 8.2 %collective-permute-done.20 = bf16[2,32,4096]{2,1,0:T(8,128)(2,1)S(1)} collective-permute-done((bf16[2,32,4096]{2,1,0:T(8,128)(2,1)S(1)}, bf16[2,32,4096]{2,1,0:T(8,128)(2,1)S(1)}, u32[]{:S(2)}, u32[]{:S(2)}) %collective-permute-start.20) | collective-permute-done | bytes 524320 | tf_op jit(solution)/shard_map/ppermute | solution.py:891
  566.0 1.2 collective-permute-start.21
  567.9 0.9 add_bitcast_fusion
  568.8 7.3 %collective-permute-done.21 = bf16[1,32,4096]{2,1,0:T(8,128)(2,1)S(1)} collective-permute-done((bf16[1,32,4096]{2,1,0:T(8,128)(2,1)S(1)}, bf16[1,32,4096]{2,1,0:T(8,128)(2,1)S(1)}, u32[]{:S(2)}, u32[]{:S(2)}) %collective-permute-start.21) | collective-permute-done | bytes 262176 | tf_op jit(solution)/shard_map/ppermute | solution.py:891
  576.2 0.9 add_bitcast_fusion.1
  (123 shorter events, 15.5 us)
Async XLA Ops:
  7.2 202.2 %all-gather.3.cloned.1.call-start = ((), (), s32[]{:S(2)}) async-start(), calls=%async_computation | async-start | bytes 17301504 | tf_op jit(solution)/shard_map/all_gather | solution.py:950
  12.3 0.7 copy-start.13
  13.0 60.7 %copy-start.8 = (bf16[32,4096]{1,0:T(8,128)(2,1)S(1)}, bf16[32,4096]{1,0:T(8,128)(2,1)}, u32[]{:S(2)}) copy-start(bf16[32,4096]{1,0:T(8,128)(2,1)} %param.35) | copy-start | bytes 786436
  13.0 60.9 %copy-start.9 = (bf16[128,1024]{1,0:T(8,128)(2,1)S(1)}, bf16[128,1024]{1,0:T(8,128)(2,1)}, u32[]{:S(2)}) copy-start(bf16[128,1024]{1,0:T(8,128)(2,1)} %param.36) | copy-start | bytes 786436
  73.7 1.8 copy-start.16
  73.7 2.7 copy-start
  76.4 2.2 copy-start.10
  76.4 2.2 copy-start.11
  76.4 2.2 copy-start.12
  85.6 8.4 %copy-start.1 = (bf16[2,588,1024]{2,0,1:T(2,128)(2,1)S(1)}, bf16[2,588,1024]{2,0,1:T(2,128)(2,1)}, u32[]{:S(2)}) copy-start(bf16[2,588,1024]{2,0,1:T(2,128)(2,1)} %param.20) | copy-start | bytes 7225348
  103.1 14.1 %copy-start.19 = (s32[32]{0:T(128)S(1)}, s32[32]{0:T(128)}, u32[]{:S(2)}) copy-start(s32[32]{0:T(128)} %constant.22.clone) | copy-start | bytes 388
  308.7 110.0 %collective-permute-start.10 = (bf16[8,32,2048]{2,1,0:T(8,128)(2,1)}, bf16[8,32,2048]{2,1,0:T(8,128)(2,1)S(1)}, u32[]{:S(2)}, u32[]{:S(2)}) collective-permute-start(bf16[8,32,2048]{2,1,0:T(8,128)(2,1)} %get-tuple-element.100), channel_id=1, source_target_pairs={{0,1},{1,0},{2,3},{3,2},{4,5},{5,4},{6,7},{7,6},{8,9},{9,8},{10,11... | collective-permute-start | bytes 3145736 | tf_op jit(solution)/shard_map/ppermute | solution.py:891
  325.7 90.9 %collective-permute-start.14 = (bf16[8,32,2048]{2,1,0:T(8,128)(2,1)}, bf16[8,32,2048]{2,1,0:T(8,128)(2,1)}, u32[]{:S(2)}, u32[]{:S(2)}) collective-permute-start(bf16[8,32,2048]{2,1,0:T(8,128)(2,1)} %get-tuple-element.102), channel_id=1, source_target_pairs={{0,2},{1,3},{2,0},{3,1},{4,6},{5,7},{6,4},{7,5},{8,10},{9,11},{10,... | collective-permute-start | bytes 3145736 | tf_op jit(solution)/shard_map/ppermute | solution.py:891
  365.3 55.6 %collective-permute-start.6 = (bf16[8,32,2048]{2,1,0:T(8,128)(2,1)}, bf16[8,32,2048]{2,1,0:T(8,128)(2,1)}, u32[]{:S(2)}, u32[]{:S(2)}) collective-permute-start(bf16[8,32,2048]{2,1,0:T(8,128)(2,1)} %get-tuple-element.113), channel_id=1, source_target_pairs={{0,1},{1,0},{2,3},{3,2},{4,5},{5,4},{6,7},{7,6},{8,9},{9,8},{10,11... | collective-permute-start | bytes 3145736 | tf_op jit(solution)/shard_map/ppermute | solution.py:891
  377.1 45.8 %collective-permute-start.1 = (bf16[8,32,2048]{2,1,0:T(8,128)(2,1)}, bf16[8,32,2048]{2,1,0:T(8,128)(2,1)}, u32[]{:S(2)}, u32[]{:S(2)}) collective-permute-start(bf16[8,32,2048]{2,1,0:T(8,128)(2,1)} %get-tuple-element.115), channel_id=1, source_target_pairs={{0,1},{1,0},{2,3},{3,2},{4,5},{5,4},{6,7},{7,6},{8,9},{9,8},{10,11... | collective-permute-start | bytes 3145736 | tf_op jit(solution)/shard_map/ppermute | solution.py:891
  377.3 11.8 %copy-start.15 = (f32[1,1024]{1,0:T(1,128)S(1)}, f32[1,1024]{1,0:T(1,128)}, u32[]{:S(2)}) copy-start(f32[1,1024]{1,0:T(1,128)} %get-tuple-element.123) | copy-start | bytes 12292
  377.3 11.8 %copy-start.14 = (f32[1,1024]{1,0:T(1,128)S(1)}, f32[1,1024]{1,0:T(1,128)}, u32[]{:S(2)}) copy-start(f32[1,1024]{1,0:T(1,128)} %get-tuple-element.124) | copy-start | bytes 12292
  377.3 13.5 %copy-start.21 = (bf16[512,512]{1,0:T(8,128)(2,1)S(1)}, bf16[512,512]{1,0:T(8,128)(2,1)}, u32[]{:S(2)}) copy-start(bf16[512,512]{1,0:T(8,128)(2,1)} %get-tuple-element.75) | copy-start | bytes 1572868
  390.3 3.4 copy-start.20
  390.3 5.0 collective-permute-start
  395.4 7.0 %slice-start = ((s8[4849664]{0:T(1024)(128)(4,1)}), s8[4194304]{0:T(1024)(128)(4,1)S(1)}, s32[]{:S(2)}) async-start(s8[4849664]{0:T(1024)(128)(4,1)} %bitcast.105), calls=%async_computation.1 | async-start | bytes 8388608
  395.4 6.9 %slice-start.1 = ((s8[4849664]{0:T(1024)(128)(4,1)}), s8[655360]{0:T(1024)(128)(4,1)S(1)}, s32[]{:S(2)}) async-start(s8[4849664]{0:T(1024)(128)(4,1)} %bitcast.105), calls=%async_computation.2 | async-start | bytes 1310720
  395.5 19.4 %collective-permute-start.2 = (bf16[8,32,128]{2,1,0:T(8,128)(2,1)S(1)}, bf16[8,32,128]{2,1,0:T(8,128)(2,1)S(1)}, u32[]{:S(2)}, u32[]{:S(2)}) collective-permute-start(bf16[8,32,128]{2,1,0:T(8,128)(2,1)S(1)} %slice.397), channel_id=1, source_target_pairs={{0,1},{1,0},{2,3},{3,2},{4,5},{5,4},{6,7},{7,6},{8,9},{9,8},{10,11... | collective-permute-start | bytes 196616 | tf_op jit(solution)/shard_map/ppermute | solution.py:891
  402.4 12.5 %copy-start.18 = (bf16[8,128,1024]{2,1,0:T(8,128)(2,1)S(1)}, bf16[8,128,1024]{2,1,0:T(8,128)(2,1)}, u32[]{:S(2)}) copy-start(bf16[8,128,1024]{2,1,0:T(8,128)(2,1)} %get-tuple-element.133) | copy-start | bytes 6291460
  407.4 9.2 %copy-start.17 = (bf16[8,32,4096]{2,1,0:T(8,128)(2,1)S(1)}, bf16[8,32,4096]{2,1,0:T(8,128)(2,1)}, u32[]{:S(2)}) copy-start(bf16[8,32,4096]{2,1,0:T(8,128)(2,1)} %get-tuple-element.131) | copy-start | bytes 6291460
  407.4 9.6 %copy-start.4 = (bf16[8,32,2048]{2,1,0:T(8,128)(2,1)S(1)}, bf16[8,32,2048]{2,1,0:T(8,128)(2,1)}, u32[]{:S(2)}) copy-start(bf16[8,32,2048]{2,1,0:T(8,128)(2,1)} %get-tuple-element.129) | copy-start | bytes 3145732
  411.3 9.2 %copy-start.6 = (bf16[8,32,2048]{2,1,0:T(8,128)(2,1)S(1)}, bf16[8,32,2048]{2,1,0:T(8,128)(2,1)}, u32[]{:S(2)}) copy-start(bf16[8,32,2048]{2,1,0:T(8,128)(2,1)} %get-tuple-element.128) | copy-start | bytes 3145732
  414.9 111.1 %collective-permute-start.22 = (bf16[8,128,1024]{2,1,0:T(8,128)(2,1)S(1)}, bf16[8,128,1024]{2,1,0:T(8,128)(2,1)S(1)}, u32[]{:S(2)}, u32[]{:S(2)}) collective-permute-start(bf16[8,128,1024]{2,1,0:T(8,128)(2,1)S(1)} %copy-done.18), channel_id=1, source_target_pairs={{0,2},{1,3},{2,0},{3,1},{4,6},{5,7},{6,4},{7,5},{8,10},{9,11},{10,... | collective-permute-start | bytes 6291464 | tf_op jit(solution)/shard_map/ppermute | solution.py:891
  416.6 111.2 %collective-permute-start.18 = (bf16[8,32,4096]{2,1,0:T(8,128)(2,1)S(1)}, bf16[8,32,4096]{2,1,0:T(8,128)(2,1)S(1)}, u32[]{:S(2)}, u32[]{:S(2)}) collective-permute-start(bf16[8,32,4096]{2,1,0:T(8,128)(2,1)S(1)} %copy-done.17), channel_id=1, source_target_pairs={{0,1},{1,0},{2,3},{3,2},{4,5},{5,4},{6,7},{7,6},{8,9},{9,8},{10,11... | collective-permute-start | bytes 6291464 | tf_op jit(solution)/shard_map/ppermute | solution.py:891
  417.0 4.3 copy-start.7
  418.7 55.9 %collective-permute-start.15 = (bf16[4,32,2048]{2,1,0:T(8,128)(2,1)S(1)}, bf16[4,32,2048]{2,1,0:T(8,128)(2,1)S(1)}, u32[]{:S(2)}, u32[]{:S(2)}) collective-permute-start(bf16[4,32,2048]{2,1,0:T(8,128)(2,1)S(1)} %get-tuple-element.226), channel_id=1, source_target_pairs={{0,1},{1,0},{2,3},{3,2},{4,5},{5,4},{6,7},{7,6},{8,9},{9,8},{10,11... | collective-permute-start | bytes 1572872 | tf_op jit(solution)/shard_map/ppermute | solution.py:891
  420.5 4.2 copy-start.5
  420.9 54.2 %collective-permute-start.11 = (bf16[4,32,2048]{2,1,0:T(8,128)(2,1)S(1)}, bf16[4,32,2048]{2,1,0:T(8,128)(2,1)S(1)}, u32[]{:S(2)}, u32[]{:S(2)}) collective-permute-start(bf16[4,32,2048]{2,1,0:T(8,128)(2,1)S(1)} %get-tuple-element.228), channel_id=1, source_target_pairs={{0,2},{1,3},{2,0},{3,1},{4,6},{5,7},{6,4},{7,5},{8,10},{9,11},{10,... | collective-permute-start | bytes 1572872 | tf_op jit(solution)/shard_map/ppermute | solution.py:891
  422.9 62.9 %collective-permute-start.7 = (bf16[4,32,2048]{2,1,0:T(8,128)(2,1)S(1)}, bf16[4,32,2048]{2,1,0:T(8,128)(2,1)S(1)}, u32[]{:S(2)}, u32[]{:S(2)}) collective-permute-start(bf16[4,32,2048]{2,1,0:T(8,128)(2,1)S(1)} %get-tuple-element.230), channel_id=1, source_target_pairs={{0,2},{1,3},{2,0},{3,1},{4,6},{5,7},{6,4},{7,5},{8,10},{9,11},{10,... | collective-permute-start | bytes 1572872 | tf_op jit(solution)/shard_map/ppermute | solution.py:891
  474.6 21.8 %collective-permute-start.3 = (bf16[4,32,2176]{2,1,0:T(8,128)(2,1)S(1)}, bf16[4,32,2176]{2,1,0:T(8,128)(2,1)S(1)}, u32[]{:S(2)}, u32[]{:S(2)}) collective-permute-start(bf16[4,32,2176]{2,1,0:T(8,128)(2,1)S(1)} %pad_maximum_fusion), channel_id=1, source_target_pairs={{0,2},{1,3},{2,0},{3,1},{4,6},{5,7},{6,4},{7,5},{8,10},{9,11},{10,... | collective-permute-start | bytes 1671176 | tf_op jit(solution)/shard_map/ppermute | solution.py:891
  475.2 21.3 %collective-permute-start.16 = (bf16[2,32,2048]{2,1,0:T(8,128)(2,1)S(1)}, bf16[2,32,2048]{2,1,0:T(8,128)(2,1)S(1)}, u32[]{:S(2)}, u32[]{:S(2)}) collective-permute-start(bf16[2,32,2048]{2,1,0:T(8,128)(2,1)S(1)} %get-tuple-element.236), channel_id=1, source_target_pairs={{0,8},{1,9},{2,10},{3,11},{4,12},{5,13},{6,14},{7,15},{8,0},{9,1},... | collective-permute-start | bytes 786440 | tf_op jit(solution)/shard_map/ppermute | solution.py:891
  485.9 12.8 %collective-permute-start.12 = (bf16[2,32,2048]{2,1,0:T(8,128)(2,1)S(1)}, bf16[2,32,2048]{2,1,0:T(8,128)(2,1)S(1)}, u32[]{:S(2)}, u32[]{:S(2)}) collective-permute-start(bf16[2,32,2048]{2,1,0:T(8,128)(2,1)S(1)} %get-tuple-element.238), channel_id=1, source_target_pairs={{0,8},{1,9},{2,10},{3,11},{4,12},{5,13},{6,14},{7,15},{8,0},{9,1},... | collective-permute-start | bytes 786440 | tf_op jit(solution)/shard_map/ppermute | solution.py:891
  496.3 13.4 %collective-permute-start.8 = (bf16[2,32,2048]{2,1,0:T(8,128)(2,1)S(1)}, bf16[2,32,2048]{2,1,0:T(8,128)(2,1)S(1)}, u32[]{:S(2)}, u32[]{:S(2)}) collective-permute-start(bf16[2,32,2048]{2,1,0:T(8,128)(2,1)S(1)} %get-tuple-element.240), channel_id=1, source_target_pairs={{0,8},{1,9},{2,10},{3,11},{4,12},{5,13},{6,14},{7,15},{8,0},{9,1},... | collective-permute-start | bytes 786440 | tf_op jit(solution)/shard_map/ppermute | solution.py:891
  496.3 29.7 %copy-start.3 = (bf16[8,128,1024]{2,1,0:T(8,128)(2,1)S(1)}, bf16[8,128,1024]{2,1,0:T(8,128)(2,1)}, u32[]{:S(2)}) copy-start(bf16[8,128,1024]{2,1,0:T(8,128)(2,1)} %get-tuple-element.132) | copy-start | bytes 6291460
  496.5 16.9 %collective-permute-start.4 = (bf16[2,32,2176]{2,1,0:T(8,128)(2,1)S(1)}, bf16[2,32,2176]{2,1,0:T(8,128)(2,1)S(1)}, u32[]{:S(2)}, u32[]{:S(2)}) collective-permute-start(bf16[2,32,2176]{2,1,0:T(8,128)(2,1)S(1)} %get-tuple-element.234), channel_id=1, source_target_pairs={{0,8},{1,9},{2,10},{3,11},{4,12},{5,13},{6,14},{7,15},{8,0},{9,1},... | collective-permute-start | bytes 835592 | tf_op jit(solution)/shard_map/ppermute | solution.py:891
  498.6 17.2 %collective-permute-start.17 = (bf16[1,32,2048]{2,1,0:T(8,128)(2,1)S(1)}, bf16[1,32,2048]{2,1,0:T(8,128)(2,1)S(1)}, u32[]{:S(2)}, u32[]{:S(2)}) collective-permute-start(bf16[1,32,2048]{2,1,0:T(8,128)(2,1)S(1)} %add_convert_fusion.31), channel_id=1, source_target_pairs={{0,16},{1,17},{2,18},{3,19},{4,20},{5,21},{6,22},{7,23},{8,24},{9,... | collective-permute-start | bytes 393224 | tf_op jit(solution)/shard_map/ppermute | solution.py:891
  509.7 16.2 %collective-permute-start.13 = (bf16[1,32,2048]{2,1,0:T(8,128)(2,1)S(1)}, bf16[1,32,2048]{2,1,0:T(8,128)(2,1)S(1)}, u32[]{:S(2)}, u32[]{:S(2)}) collective-permute-start(bf16[1,32,2048]{2,1,0:T(8,128)(2,1)S(1)} %add_convert_fusion.33), channel_id=1, source_target_pairs={{0,16},{1,17},{2,18},{3,19},{4,20},{5,21},{6,22},{7,23},{8,24},{9,... | collective-permute-start | bytes 393224 | tf_op jit(solution)/shard_map/ppermute | solution.py:891
  513.4 16.5 %collective-permute-start.9 = (bf16[1,32,2048]{2,1,0:T(8,128)(2,1)S(1)}, bf16[1,32,2048]{2,1,0:T(8,128)(2,1)S(1)}, u32[]{:S(2)}, u32[]{:S(2)}) collective-permute-start(bf16[1,32,2048]{2,1,0:T(8,128)(2,1)S(1)} %add_convert_fusion.35), channel_id=1, source_target_pairs={{0,16},{1,17},{2,18},{3,19},{4,20},{5,21},{6,22},{7,23},{8,24},{9,... | collective-permute-start | bytes 393224 | tf_op jit(solution)/shard_map/ppermute | solution.py:891
  515.8 28.9 %collective-permute-start.5 = (bf16[1,32,2176]{2,1,0:T(8,128)(2,1)S(1)}, bf16[1,32,2176]{2,1,0:T(8,128)(2,1)S(1)}, u32[]{:S(2)}, u32[]{:S(2)}) collective-permute-start(bf16[1,32,2176]{2,1,0:T(8,128)(2,1)S(1)} %add_convert_fusion.29), channel_id=1, source_target_pairs={{0,16},{1,17},{2,18},{3,19},{4,20},{5,21},{6,22},{7,23},{8,24},{9,... | collective-permute-start | bytes 417800 | tf_op jit(solution)/shard_map/ppermute | solution.py:891
  526.0 1.8 copy-start.2
  527.0 14.9 %collective-permute-start.23 = (bf16[4,128,1024]{2,1,0:T(8,128)(2,1)S(1)}, bf16[4,128,1024]{2,1,0:T(8,128)(2,1)S(1)}, u32[]{:S(2)}, u32[]{:S(2)}) collective-permute-start(bf16[4,128,1024]{2,1,0:T(8,128)(2,1)S(1)} %get-tuple-element.218), channel_id=1, source_target_pairs={{0,1},{1,0},{2,3},{3,2},{4,5},{5,4},{6,7},{7,6},{8,9},{9,8},{10,11... | collective-permute-start | bytes 3145736 | tf_op jit(solution)/shard_map/ppermute | solution.py:891
  528.6 14.9 %collective-permute-start.19 = (bf16[4,32,4096]{2,1,0:T(8,128)(2,1)S(1)}, bf16[4,32,4096]{2,1,0:T(8,128)(2,1)S(1)}, u32[]{:S(2)}, u32[]{:S(2)}) collective-permute-start(bf16[4,32,4096]{2,1,0:T(8,128)(2,1)S(1)} %get-tuple-element.220), channel_id=1, source_target_pairs={{0,2},{1,3},{2,0},{3,1},{4,6},{5,7},{6,4},{7,5},{8,10},{9,11},{10,... | collective-permute-start | bytes 3145736 | tf_op jit(solution)/shard_map/ppermute | solution.py:891
  542.3 13.3 %collective-permute-start.24 = (bf16[2,128,1024]{2,1,0:T(8,128)(2,1)S(1)}, bf16[2,128,1024]{2,1,0:T(8,128)(2,1)S(1)}, u32[]{:S(2)}, u32[]{:S(2)}) collective-permute-start(bf16[2,128,1024]{2,1,0:T(8,128)(2,1)S(1)} %get-tuple-element.222), channel_id=1, source_target_pairs={{0,8},{1,9},{2,10},{3,11},{4,12},{5,13},{6,14},{7,15},{8,0},{9,1},... | collective-permute-start | bytes 1572872 | tf_op jit(solution)/shard_map/ppermute | solution.py:891
  543.7 22.3 %collective-permute-start.20 = (bf16[2,32,4096]{2,1,0:T(8,128)(2,1)S(1)}, bf16[2,32,4096]{2,1,0:T(8,128)(2,1)S(1)}, u32[]{:S(2)}, u32[]{:S(2)}) collective-permute-start(bf16[2,32,4096]{2,1,0:T(8,128)(2,1)S(1)} %get-tuple-element.224), channel_id=1, source_target_pairs={{0,8},{1,9},{2,10},{3,11},{4,12},{5,13},{6,14},{7,15},{8,0},{9,1},... | collective-permute-start | bytes 1572872 | tf_op jit(solution)/shard_map/ppermute | solution.py:891
  555.6 12.3 %collective-permute-start.25 = (bf16[1,128,1024]{2,1,0:T(8,128)(2,1)S(1)}, bf16[1,128,1024]{2,1,0:T(8,128)(2,1)S(1)}, u32[]{:S(2)}, u32[]{:S(2)}) collective-permute-start(bf16[1,128,1024]{2,1,0:T(8,128)(2,1)S(1)} %add_convert_fusion.19), channel_id=1, source_target_pairs={{0,16},{1,17},{2,18},{3,19},{4,20},{5,21},{6,22},{7,23},{8,24},{9,... | collective-permute-start | bytes 786440 | tf_op jit(solution)/shard_map/ppermute | solution.py:891
  566.0 10.1 %collective-permute-start.21 = (bf16[1,32,4096]{2,1,0:T(8,128)(2,1)S(1)}, bf16[1,32,4096]{2,1,0:T(8,128)(2,1)S(1)}, u32[]{:S(2)}, u32[]{:S(2)}) collective-permute-start(bf16[1,32,4096]{2,1,0:T(8,128)(2,1)S(1)} %add_convert_fusion.21), channel_id=1, source_target_pairs={{0,16},{1,17},{2,18},{3,19},{4,20},{5,21},{6,22},{7,23},{8,24},{9,... | collective-permute-start | bytes 786440 | tf_op jit(solution)/shard_map/ppermute | solution.py:891
Sparse Core Ops, SparseCore 0:
  75.6 129.5 all-gather.2

commit v3 on v2

--- a/solution.py
+++ b/solution.py
@@ -186,56 +186,23 @@
         bias[tile, : high - low, :] = jnp.where((keys <= queries) & same, 0.0, MASKED)
 
 
-def self_forward_kernel(page_column, page_row, q, k, v, out, totals, bias):
+def attend_pair(q, k, v, out, totals, bias):
     tiles = q.shape[0] // TILE
     scale = LOG2E * (q.shape[1] // 2) ** (-0.5)
-
-    @pl.when(pl.program_id(0) == 0)
-    def _():
-        fill_bias(page_column, page_row, bias, tiles)
-
     for tile in range(tiles):
         low, high = key_range(tile)
-        here = slice(tile * TILE, (tile + 1) * TILE)
-        scores = product_t(k[low:high, :], two_heads(q[here, :])) * scale + twice(
+        at = slice(tile * TILE, (tile + 1) * TILE)
+        scores = product_t(k[low:high, :], two_heads(q[at, :])) * scale + twice(
             bias[tile, : high - low, :]
         )
         highest = jnp.max(scores, axis=0, keepdims=True)
         weights = jnp.exp2(scores - highest)
         total = jnp.sum(weights, axis=0, keepdims=True)
         mixed = product_rows(v[low:high, :], weights.astype(bf16)) * (1.0 / total)
-        out[here, :] = join_heads(mixed).astype(bf16)
+        out[at, :] = join_heads(mixed).astype(bf16)
         level = highest + jnp.log2(total)
-        totals[0, 0:1, here] = level[:, :TILE]
-        totals[0, 1:2, here] = level[:, TILE:]
-
-
-def self_forward(page_column, page_row, qkv):
-    rows, width = qkv.shape[0], qkv.shape[1] // 3
-    pairs = width // 128
-    return pl.pallas_call(
-        self_forward_kernel,
-        grid=(pairs,),
-        in_specs=[
-            pl.BlockSpec((rows, 1), lambda j: (0, 0)),
-            pl.BlockSpec((1, rows), lambda j: (0, 0)),
-            pl.BlockSpec((rows, 128), lambda j: (0, j)),
-            pl.BlockSpec((rows, 128), lambda j: (0, pairs + j)),
-            pl.BlockSpec((rows, 128), lambda j: (0, 2 * pairs + j)),
-        ],
-        out_specs=[
-            pl.BlockSpec((rows, 128), lambda j: (0, j)),
-            pl.BlockSpec((1, 2, rows), lambda j: (j, 0, 0)),
-        ],
-        out_shape=[
-            jax.ShapeDtypeStruct((rows, width), bf16),
-            jax.ShapeDtypeStruct((pairs, 2, rows), f32),
-        ],
-        scratch_shapes=[pltpu.VMEM((rows // TILE, PAGE_MAX + TILE, TILE), f32)],
-        compiler_params=params(1),
-        name="self_forward",
-        cost_estimate=cost(14),
-    )(page_column, page_row, qkv, qkv, qkv)
+        totals[0, 0:1, at] = level[:, :TILE]
+        totals[0, 1:2, at] = level[:, TILE:]
 
 
 def self_backward_kernel(page_column, page_row, q, k, v, g, totals, out, bias, dk, dv):
@@ -268,7 +235,7 @@
 
 
 def self_backward(page_column, page_row, qkv, grads, totals):
-    rows, width = qkv.shape[0], qkv.shape[1] // 3
+    rows, width = grads.shape
     pairs = width // 128
     return pl.pallas_call(
         self_backward_kernel,
@@ -276,10 +243,7 @@
         in_specs=[
             pl.BlockSpec((rows, 1), lambda j: (0, 0)),
             pl.BlockSpec((1, rows), lambda j: (0, 0)),
-            pl.BlockSpec((rows, 128), lambda j: (0, j)),
-            pl.BlockSpec((rows, 128), lambda j: (0, pairs + j)),
-            pl.BlockSpec((rows, 128), lambda j: (0, 2 * pairs + j)),
-            pl.BlockSpec((rows, 128), lambda j: (0, j)),
+            *[pl.BlockSpec((rows, 128), lambda j: (0, j))] * 4,
             pl.BlockSpec((1, 2, rows), lambda j: (j, 0, 0)),
         ],
         out_specs=pl.BlockSpec((3, rows, 128), lambda j: (0, 0, j)),
@@ -292,7 +256,7 @@
         compiler_params=params(1),
         name="self_backward",
         cost_estimate=cost(15),
-    )(page_column, page_row, qkv, qkv, qkv, grads, totals)
+    )(page_column, page_row, *qkv, grads, totals)
 
 
 def cross_steps(count, tiles):
@@ -804,87 +768,219 @@
     )(x, mixed, projection, g, gain, weights, weights)
 
 
-def gather_kernel(devices, lanes, tracks, x_ref, out, own_sem, send_sem, recv_sem):
-    me = lax.axis_index("dp") * lanes + lax.axis_index("fsdp")
-    count = devices // 2
-
-    def device(bit):
-        other = me ^ bit
-        return (other // lanes, lax.rem(other, lanes))
-
-    barrier = pltpu.get_barrier_semaphore()
-    every = [1 << b for b in range(devices.bit_length() - 1)]
-    for bit in every:
-        pl.semaphore_signal(
-            barrier, inc=1, device_id=device(bit), device_id_type=pl.DeviceIdType.MESH
+class Spread:
+    def __init__(self, devices, lanes, tracks, x_ref, out, own_sem, send_sem, recv_sem):
+        self.devices, self.lanes, self.tracks = devices, lanes, tracks
+        self.x_ref, self.out, self.own_sem = x_ref, out, own_sem
+        self.send_sem, self.recv_sem = send_sem, recv_sem
+        self.count, self.me = devices // 2, here(lanes)
+        numbers = sorted(range(self.count), key=lambda k: (bin(k).count("1"), k))
+        self.sends = [
+            (track, number, place, bit)
+            for number in numbers
+            for track, (_, _, bits) in enumerate(tracks)
+            for place, bit in enumerate(bits + (lanes,))
+            if number >> place == 0 or bit == lanes
+        ]
+        self.numbers = numbers[1:]
+
+    def device(self, bit):
+        other = self.me ^ bit
+        return (other // self.lanes, lax.rem(other, self.lanes))
+
+    def block(self, track, number):
+        low, high, bits = self.tracks[track]
+        to_core = number >= self.count
+        number -= self.count * to_core
+        owner = self.me ^ sum(b for p, b in enumerate(bits) if (number >> p) & 1)
+        return self.out.at[owner ^ self.lanes if to_core else owner, :, low:high]
+
+    def copy(self, index):
+        track, number, place, bit = self.sends[index]
+        low, high, _ = self.tracks[track]
+        target = self.block(track, number)
+        return pltpu.make_async_remote_copy(
+            src_ref=target if number else self.x_ref.at[:, low:high],
+            dst_ref=target,
+            send_sem=self.send_sem.at[index],
+            recv_sem=self.recv_sem.at[track, number + (1 << place)],
+            device_id=self.device(bit),
+            device_id_type=pl.DeviceIdType.MESH,
         )
-    pl.semaphore_wait(barrier, len(every))
-    own = pltpu.make_async_copy(x_ref, out.at[me], own_sem)
-    own.start()
-    sends = []
-
-    def block(track, number, to_core):
-        low, high, bits = tracks[track]
-        owner = me ^ sum(b for p, b in enumerate(bits) if (number >> p) & 1)
-        return out.at[owner ^ lanes if to_core else owner, :, low:high]
-
-    def arrived(track, number):
-        to_core = number >= count
-        here = block(track, number - count if to_core else number, to_core)
+
+    def own(self):
+        return pltpu.make_async_copy(self.x_ref, self.out.at[self.me], self.own_sem)
+
+    def wait(self, track, number):
+        target = self.block(track, number)
         pltpu.make_async_remote_copy(
-            src_ref=here,
-            dst_ref=here,
-            send_sem=send_sem.at[0],
-            recv_sem=recv_sem.at[track, number],
-            device_id=device(lanes),
+            src_ref=target,
+            dst_ref=target,
+            send_sem=self.send_sem.at[0],
+            recv_sem=self.recv_sem.at[track, number],
+            device_id=self.device(self.lanes),
             device_id_type=pl.DeviceIdType.MESH,
         ).wait_recv()
-        return here
-
-    for number in sorted(range(count), key=lambda k: (bin(k).count("1"), k)):
-        for track, (low, high, bits) in enumerate(tracks):
-            there = block(track, number, False)
-            here = arrived(track, number) if number else x_ref.at[:, low:high]
-            for place, bit in enumerate(bits + (lanes,)):
-                if number >> place == 0 or bit == lanes:
-                    copy = pltpu.make_async_remote_copy(
-                        src_ref=here,
-                        dst_ref=there,
-                        send_sem=send_sem.at[len(sends)],
-                        recv_sem=recv_sem.at[track, number + (1 << place)],
-                        device_id=device(bit),
-                        device_id_type=pl.DeviceIdType.MESH,
-                    )
-                    copy.start()
-                    sends.append(copy)
-    for number in range(count, devices):
-        for track in range(len(tracks)):
-            arrived(track, number)
-    for copy in sends:
-        copy.wait_send()
-    own.wait()
-
-
-def gather(number, devices, lanes, values):
-    depth, columns = values.shape
+
+    def send(self, number):
+        for index, (_, sent, _, _) in enumerate(self.sends):
+            if sent == number:
+                self.copy(index).start()
+
+    def start(self):
+        barrier = pltpu.get_barrier_semaphore()
+        every = [1 << b for b in range(self.devices.bit_length() - 1)]
+        for bit in every:
+            pl.semaphore_signal(
+                barrier, inc=1, device_id=self.device(bit), device_id_type=pl.DeviceIdType.MESH
+            )
+        pl.semaphore_wait(barrier, len(every))
+        self.own().start()
+        self.send(0)
+
+    def forward(self, numbers):
+        for number in numbers:
+            for track in range(len(self.tracks)):
+                self.wait(track, number)
+            self.send(number)
+
+    def finish(self):
+        for number in range(self.count, self.devices):
+            for track in range(len(self.tracks)):
+                self.wait(track, number)
+        for index in range(len(self.sends)):
+            self.copy(index).wait_send()
+        self.own().wait()
+
+
+def tracks_of(devices, lanes, columns):
     middle = (columns // 256) * 128
     high = tuple(2 * lanes << b for b in range((devices // (2 * lanes)).bit_length() - 1))
     links = [high + tuple(1 << b for b in way) for way in orders(lanes)]
-    tracks = ((0, middle, links[0]), (middle, columns, links[1]))
+    return ((0, middle, links[0]), (middle, columns, links[1]))
+
+
+def spread_scratch(devices):
+    return [
+        pltpu.SemaphoreType.DMA,
+        pltpu.SemaphoreType.DMA((2 * (devices - 1),)),
+        pltpu.SemaphoreType.DMA((2, devices)),
+    ]
+
+
+def gather_kernel(devices, lanes, tracks, x_ref, out, own_sem, send_sem, recv_sem):
+    spread = Spread(devices, lanes, tracks, x_ref, out, own_sem, send_sem, recv_sem)
+    spread.start()
+    spread.forward(spread.numbers)
+    spread.finish()
+
+
+def gather(number, devices, lanes, values):
+    depth, columns = values.shape
     return pl.pallas_call(
-        functools.partial(gather_kernel, devices, lanes, tracks),
+        functools.partial(gather_kernel, devices, lanes, tracks_of(devices, lanes, columns)),
         in_specs=[pl.BlockSpec(memory_space=pltpu.VMEM)],
         out_specs=pl.BlockSpec(memory_space=pltpu.HBM),
         out_shape=jax.ShapeDtypeStruct((devices, depth, columns), values.dtype),
-        scratch_shapes=[
-            pltpu.SemaphoreType.DMA,
-            pltpu.SemaphoreType.DMA((len(tracks) * (devices - 1),)),
-            pltpu.SemaphoreType.DMA((len(tracks), devices)),
-        ],
+        scratch_shapes=spread_scratch(devices),
         compiler_params=pltpu.CompilerParams(collective_id=number, has_side_effects=True),
         name="gather",
-        cost_estimate=cost(40),
+        cost_estimate=cost(60),
     )(values).reshape(-1, columns)
+
+
+def attend_kernel(
+    devices, lanes, tracks, x_ref, page_column, page_row, hidden, w_q, w_k, w_v,
+    gathered, q, k, v, out, totals, own_sem, send_sem, recv_sem, bias,
+):
+    step = pl.program_id(0)
+    spread = Spread(devices, lanes, tracks, x_ref, gathered, own_sem, send_sem, recv_sem)
+
+    @pl.when(step == 0)
+    def _():
+        spread.start()
+        fill_bias(page_column, page_row, bias, hidden.shape[0] // TILE)
+
+    for ref, weights in ((q, w_q), (k, w_k), (v, w_v)):
+        ref[...] = product(hidden[...], weights[...]).astype(bf16)
+    attend_pair(q, k, v, out, totals, bias)
+
+    turns = hidden.shape[1] // 128
+    for turn in range(1, turns):
+        few = spread.numbers[
+            len(spread.numbers) * (turn - 1) // (turns - 1) : len(spread.numbers) * turn // (turns - 1)
+        ]
+
+        @pl.when(step == turn)
+        def _(few=few, last=turn == turns - 1):
+            spread.forward(few)
+            if last:
+                spread.finish()
+
+
+def attend(number, devices, lanes, values, page_column, page_row, hidden, weights):
+    depth, columns = values.shape
+    rows, width = hidden.shape
+    pairs = width // 128
+
+    def whole(*shape):
+        return pl.BlockSpec(shape, lambda j: (0,) * len(shape))
+
+    head = pl.BlockSpec((rows, 128), lambda j: (0, j))
+    results = pl.pallas_call(
+        functools.partial(attend_kernel, devices, lanes, tracks_of(devices, lanes, columns)),
+        grid=(pairs,),
+        in_specs=[
+            whole(depth, columns), whole(rows, 1), whole(1, rows), whole(rows, width),
+            pl.BlockSpec((width, 128), lambda j: (0, j)),
+            pl.BlockSpec((width, 128), lambda j: (0, pairs + j)),
+            pl.BlockSpec((width, 128), lambda j: (0, 2 * pairs + j)),
+        ],
+        out_specs=[
+            pl.BlockSpec(memory_space=pltpu.HBM), head, head, head, head,
+            pl.BlockSpec((1, 2, rows), lambda j: (j, 0, 0)),
+        ],
+        out_shape=[
+            jax.ShapeDtypeStruct((devices, depth, columns), values.dtype),
+            *[jax.ShapeDtypeStruct((rows, width), bf16)] * 4,
+            jax.ShapeDtypeStruct((pairs, 2, rows), f32),
+        ],
+        scratch_shapes=spread_scratch(devices)
+        + [pltpu.VMEM((rows // TILE, PAGE_MAX + TILE, TILE), f32)],
+        compiler_params=pltpu.CompilerParams(
+            dimension_semantics=("arbitrary",),
+            vmem_limit_bytes=VMEM,
+            collective_id=number,
+            has_side_effects=True,
+        ),
+        name="attend",
+        cost_estimate=cost(60),
+    )(values, page_column, page_row, hidden, weights, weights, weights)
+    gathered, q, k, v, *rest = results
+    return gathered.reshape(-1, columns), (q, k, v), *rest
+
+
+def image_kernel(images, weights, out):
+    for image in range(images.shape[0]):
+        out[image] = product(images[image], weights[...]).astype(bf16)
+
+
+def image_keys(images, weights, first):
+    count, length, width = images.shape
+    wide = 512
+    return pl.pallas_call(
+        image_kernel,
+        grid=(2 * width // wide,),
+        in_specs=[
+            pl.BlockSpec(images.shape, lambda j: (0, 0, 0)),
+            pl.BlockSpec((width, wide), lambda j: (0, first * width // wide + j)),
+        ],
+        out_specs=pl.BlockSpec((count, length, wide), lambda j: (0, 0, j)),
+        out_shape=jax.ShapeDtypeStruct((count, length, 2 * width), bf16),
+        compiler_params=params(1),
+        name="image_keys",
+        cost_estimate=cost(8),
+    )(images, weights)
 
 
 def swap(values, devices, bit):
@@ -940,23 +1036,22 @@
     depth, width = attn_query.shape
     gains = jnp.stack([norm_self, norm_cross, norm_ffn], axis=1)
     gains = jnp.pad(gains, ((0, 0), (0, 128 - 3)))
-    first_set = jnp.concatenate([attn_query, attn_key, attn_value, cross_key, cross_value, gains], axis=1)
-    second_set = jnp.concatenate([attn_out, cross_query, cross_out], axis=1)
+    first_set = jnp.concatenate([attn_query, attn_key, attn_value, gains], axis=1)
+    second_set = jnp.concatenate([attn_out, cross_query, cross_key, cross_value, cross_out], axis=1)
     pieces = ffn_up.shape[1] // width
     feed_set = jnp.stack(
         [ffn_up.reshape(depth, pieces, width).transpose(1, 0, 2), ffn_down.reshape(pieces, depth, width)]
     )
     first_set = gather(0, devices, lanes, first_set)
     feed_set = lax.all_gather(after(feed_set, first_set), AXES, axis=0)
-    w_qkv = first_set[:, : 3 * width]
-    w_kv = first_set[:, 3 * width : 5 * width]
     (count, order, page_column, page_row, inputs, grad_out, hidden_one, unit_one, inverse_one, *gains) = arrange(
-        image_map[0], segment_ids[0], tokens[0], out_grad[0], first_set, 5 * width // 128
+        image_map[0], segment_ids[0], tokens[0], out_grad[0], first_set, 3 * width // 128
     )
-    qkv = product(hidden_one, w_qkv).astype(bf16)
-    mixed_one, log_one = self_forward(page_column, page_row, qkv)
-    kv = lax.dot_general(images, w_kv, (((2,), (0,)), ((), ())), preferred_element_type=f32).astype(bf16)
-    second_set = gather(1, devices, lanes, after(second_set, (mixed_one, kv)))
+    second_set, qkv, mixed_one, log_one = attend(
+        1, devices, lanes, second_set, page_column, page_row, hidden_one, first_set
+    )
+    w_kv = second_set[:, 2 * width : 4 * width]
+    kv = image_keys(images, second_set, 2)
     after_self, hidden_two, unit_two, inverse_two, query_two = between(inputs, mixed_one, second_set, gains[1])
     mixed_two, log_two = cross_forward(count, query_two, kv)
 

time: 591 us -> 576 us (0.975)
  matrix products: 32.1 us -> 15.8 us
  starting transfers between devices: 31.2 us -> 23.9 us
  Pallas kernels: 347 us -> 354 us
    dot_general x2 -> x0, matrix products: 17.5 us -> none  [the longest x1 9.18 us: shards(): lax.dot_general(images, w_kv, (((2,), (0,)), ((), ())), preferred_element...]
    pallas_call x3, Pallas kernels: 128 us -> 137 us  [the longest x1 83.7 us: attend(): pl.pallas_call(functools.partial(attend_kernel, devices, lanes, tracks_of...]
    ppermute x26, starting transfers between devices: 31.1 us -> 23.8 us  [swap(): return lax.ppermute(values, AXES, [(i, i ^ bit) for i in range(devices)])]
  transfers between devices with their start and end apart: 27 -> 27, of which waited for: 12 -> 12; matrix products, arithmetic and copies ran while one was open for 10% -> 7% of each run, Pallas kernels for 32% -> 37%
where the time goes in v3:
time: 576 us; the launch traced here: 567 us
  Pallas kernels  354 us (61%)
  waiting for transfers between devices  131 us (23%)
  starting transfers between devices  23.9 us (4%)
  matrix products  15.8 us (3%)
  between operations  14.9 us (3%)
  other arithmetic  14.4 us (2%)
  local copies, waits for them, and re-layouts  13.3 us (2%)
    ppermute x26, waiting for transfers between devices, swap(): return lax.ppermute(values, AXES, [(i, i ^ bit) for i in range(devices)])  131 us
    pallas_call x1, Pallas kernels, attend(): pl.pallas_call(functools.partial(attend_kernel, devices, lanes, tracks_of...  83.7 us
    pallas_call x6, Pallas kernels, weight_grad(): pl.pallas_call(functools.partial(weight_grad_kernel, devices, lanes, way,...  52.6 us
    pallas_call x1, Pallas kernels, feed(): pl.pallas_call(functools.partial(feed_kernel, devices, lanes, ways), grid...  49.2 us
    pallas_call x1, Pallas kernels, gather(): pl.pallas_call(functools.partial(gather_kernel, devices, lanes, tracks_of...  43.7 us
    pallas_call x1, Pallas kernels, cross_backward(): pl.pallas_call(cross_backward_kernel, grid_spec=pltpu.PrefetchScalarGridS...  35.6 us
    pallas_call x1, Pallas kernels, cross_forward(): pl.pallas_call(cross_forward_kernel, grid_spec=pltpu.PrefetchScalarGridSp...  30.5 us
    ppermute x26, starting transfers between devices, swap(): return lax.ppermute(values, AXES, [(i, i ^ bit) for i in range(devices)])  23.8 us
  transfers between devices with their start and end apart: 27, of which 12 were waited for; matrix products, arithmetic and copies ran while one was open for 7% of the time, Pallas kernels for 37%

profile of v3, /device:TPU:0, one launch (start us, length us, event | category | flops | bytes accessed | tf_op | source)
XLA Modules:
  0.0 567.3 jit_solution(14000847978522986523)
XLA Ops:
  8.0 1.6 fusion.12.x_ref
  9.6 43.7 %gather.18 = bf16[32,32,3200]{2,1,0:T(8,128)(2,1)} custom-call(bf16[32,3200]{1,0:T(8,128)(2,1)} %fusion.12.x_ref), custom_call_target="tpu_custom_call" | custom-call | flops 60000002048 | tf_op jit(solution)/shard_map/gather/pallas_call | solution.py:880
  54.2 1.0 copy.75
  55.1 0.9 copy.72.page_column
  56.0 2.2 copy.73.images.refs_0_
  59.0 6.5 %arrange.1 = (s32[1]{0:T(128)}, bf16[512,512]{1,0:T(8,128)(2,1)}, s32[512,1]{1,0:T(8,128)}, s32[1,512]{1,0:T(1,128)}, f32[512,1024]{1,0:T(8,128)}, /*index=5*/bf...) custom-call(s32[4]{0:T(128)} %bitcast.85, ...), custom_call_target="tpu_custom_call" | custom-call | flops 6000000000 | tf_op jit(solution)/shard_map/arrange/pallas_call | solution.py:127
  65.5 83.7 %attend.1 = (bf16[32,32,5120]{2,1,0:T(8,128)(2,1)}, bf16[512,1024]{1,0:T(8,128)(2,1)}, bf16[512,1024]{1,0:T(8,128)(2,1)}, bf16[512,1024]{1,0:T(8,128)(2,1)}, bf1...) custom-call(bf16[32,5120]{1,0:T(8,128)(2,1)} %copy-done.14, s32[512,1]{1,0:T(8,128)} %get-tuple-element.80.page_column, ...), custom_call_target="tpu_custom_call" | custom-call | flops 60000002048 | tf_op jit(solution)/shard_map/attend/pallas_call | solution.py:930
  149.2 9.2 %image_keys.1.k.v = bf16[2,588,2048]{2,1,0:T(8,128)(2,1)} custom-call(bf16[2,588,1024]{2,1,0:T(8,128)(2,1)} %copy.73.images.refs_0_, bf16[1024,5120]{1,0:T(8,128)(2,1)} %bitcast.64), custom_call_target="tpu_custom_call" | custom-call | flops 8000000000 | tf_op jit(solution)/shard_map/image_keys/pallas_call | solution.py:971
  158.3 7.2 %between.1 = (f32[512,1024]{1,0:T(8,128)}, bf16[512,1024]{1,0:T(8,128)(2,1)}, f32[512,1024]{1,0:T(8,128)}, f32[512,1]{1,0:T(8,128)}, bf16[512,1024]{1,0:T(8,128)(2,1)}) custom-call(f32[512,1024]{1,0:T(8,128)} %get-tuple-element.79.x_ref, bf16[512,1024]{1,0:T(8,128)(2,1)} %get-tuple-element.83.mixed, bf16[1024,5120]{1,0:T(8,128)(2,1)} %bitcast.65, ...), custom_call_target="tpu_custom_call" | custom-call | flops 8000000000 | tf_op jit(solution)/shard_map/between/pallas_call | solution.py:159
  165.6 30.5 %cross_forward.1 = (bf16[512,1024]{1,0:T(8,128)(2,1)}, f32[8,2,512]{2,1,0:T(2,128)}) custom-call(s32[1]{0:T(128)} %get-tuple-element.87.count_ref, bf16[512,1024]{1,0:T(8,128)(2,1)} %get-tuple-element.88.q, bf16[2,588,2048]{2,1,0:T(8,128)(2,1)} %image_keys.1.k.v, bf16[2,588,2048]{2,1,0:T(8,128)(2,1)} %image_keys.1.k.v), custom_call_target="tpu_custom_call" | custom-call | flops 24000000000 | tf_op jit(solution)/shard_map/cross_forward/pallas_call | solution.py:304
  196.1 49.2 %feed.1 = (bf16[512,1024]{1,0:T(8,128)(2,1)}, f32[512,1024]{1,0:T(8,128)}, bf16[512,1024]{1,0:T(8,128)(2,1)}, bf16[512,1024]{1,0:T(8,128)(2,1)}, f32[1,1024]{1,0...) custom-call(f32[512,1024]{1,0:T(8,128)} %get-tuple-element.86.x_ref,, ...), custom_call_target="tpu_custom_call" | custom-call | flops 40000000000 | tf_op jit(solution)/shard_map/feed/pallas_call | solution.py:714
  245.4 35.6 %cross_backward.1 = (bf16[512,1024]{1,0:T(8,128)(2,1)}, bf16[2,2,588,1024]{3,2,1,0:T(8,128)(2,1)}) custom-call(s32[1]{0:T(128)} %get-tuple-element.87.count_ref, bf16[512,1024]{1,0:T(8,128)(2,1)} %get-tuple-element.88.q, bf16[2,588,2048]{2,1,0:T(8,128)(2,1)} %image_keys.1.k.v, bf16[2,588,2048]{2,1,0:T(8,128)(2,1)} %image_keys.1.k.v, ...), custom_call_target="tpu_custom_call" | custom-call | flops 28000000000 | tf_op jit(solution)/shard_map/cross_backward/pallas_call | solution.py:369
  280.9 7.1 %weight_grad.6 = (bf16[8,32,2048]{2,1,0:T(8,128)(2,1)}, bf16[8,32,2048]{2,1,0:T(8,128)(2,1)}) custom-call(bf16[1,512,1024]{2,1,0:T(8,128)(2,1)} %bitcast.97, bf16[1,1,512,1024]{3,2,1,0:T(8,128)(2,1)} %bitcast.98), custom_call_target="tpu_custom_call" | custom-call | flops 3000000000 | tf_op jit(solution)/shard_map/weight_grad/pallas_call | solution.py:510
  288.0 7.2 %weight_grad.7 = (bf16[8,32,2048]{2,1,0:T(8,128)(2,1)}, bf16[8,32,2048]{2,1,0:T(8,128)(2,1)}) custom-call(bf16[1,512,1024]{2,1,0:T(8,128)(2,1)} %bitcast.96, bf16[1,1,512,1024]{3,2,1,0:T(8,128)(2,1)} %bitcast.72, bf16[8,32,2048]{2,1,0:T(8,128)(2,1)} %get-tuple-element.104.refs_2_, ...), custom_call_target="tpu_custom_call", output_to_operand_aliasing={{0}: (2, {}), {1}: (3, {})} | custom-call | flops 3000000000 | tf_op jit(solution)/shard_map/weight_grad/pallas_call | solution.py:510
  295.3 0.8 collective-permute-start.10
  296.0 14.3 %weight_grad.8 = (bf16[8,32,2048]{2,1,0:T(8,128)(2,1)}, bf16[8,32,2048]{2,1,0:T(8,128)(2,1)}) custom-call(bf16[2,588,1024]{2,1,0:T(8,128)(2,1)} %copy.73.images.refs_0_, bf16[2,2,588,1024]{3,2,1,0:T(8,128)(2,1)} %get-tuple-element.131.refs_1_), custom_call_target="tpu_custom_call" | custom-call | flops 12000000000 | tf_op jit(solution)/shard_map/weight_grad/pallas_call | solution.py:510
  310.3 1.1 collective-permute-start.14
  311.4 10.2 %norm_grad.2 = (f32[512,1024]{1,0:T(8,128)}, bf16[512,1024]{1,0:T(8,128)(2,1)}, f32[1,1024]{1,0:T(1,128)}, bf16[512,1024]{1,0:T(8,128)(2,1)}) custom-call(bf16[1,512,1024]{2,1,0:T(8,128)(2,1)} %bitcast.73, bf16[1024,5120]{1,0:T(8,128)(2,1)} %bitcast.68, f32[512,1024]{1,0:T(8,128)} %get-tuple-element.110.unit, f32[512,1]{1,0:T(8,128)} %get-tuple-element.111.inverse, ...), custom_call_target="tpu_custom_call" | custom-call | flops 4000000000 | tf_op jit(solution)/shard_map/norm_grad/pallas_call | solution.py:570
  321.6 14.9 %self_backward.1.d_ref = bf16[3,512,1024]{2,1,0:T(8,128)(2,1)} custom-call(s32[512,1]{1,0:T(8,128)} %get-tuple-element.80.page_column, s32[1,512]{1,0:T(1,128)} %get-tuple-element.81.page_row, bf16[512,1024]{1,0:T(8,128)(2,1)} %get-tuple-element.94.q, bf16[512,1024]{1,0:T(8,128)(2,1)} %get-tuple-element.95.k, bf16[512,1024]{1,0:T(8,128)(2,1)} %get-tuple-element.96.v, ...), custom_call_target="tpu_custom_call" | custom-call | flops 15000000512 | tf_op jit(solution)/shard_map/self_backward/pallas_call | solution.py:240
  336.5 6.9 %weight_grad.9 = (bf16[8,32,2048]{2,1,0:T(8,128)(2,1)}, bf16[8,32,2048]{2,1,0:T(8,128)(2,1)}) custom-call(bf16[1,512,1024]{2,1,0:T(8,128)(2,1)} %bitcast.95, bf16[1,1,512,1024]{3,2,1,0:T(8,128)(2,1)} %bitcast.84), custom_call_target="tpu_custom_call" | custom-call | flops 3000000000 | tf_op jit(solution)/shard_map/weight_grad/pallas_call | solution.py:510
  343.4 7.3 %weight_grad.10 = (bf16[8,32,2048]{2,1,0:T(8,128)(2,1)}, bf16[8,32,2048]{2,1,0:T(8,128)(2,1)}) custom-call(bf16[1,512,1024]{2,1,0:T(8,128)(2,1)} %bitcast.93, bf16[3,1,512,1024]{3,2,1,0:T(8,128)(2,1)} %bitcast.91, bf16[8,32,2048]{2,1,0:T(8,128)(2,1)} %get-tuple-element.117.refs_2_, ...), custom_call_target="tpu_custom_call", output_to_operand_aliasing={{0}: (2, {}), {1}: (3, {})} | custom-call | flops 3000000000 | tf_op jit(solution)/shard_map/weight_grad/pallas_call | solution.py:510
  350.8 2.0 collective-permute-start.6
  352.8 9.7 %weight_grad.11 = (bf16[8,32,2048]{2,1,0:T(8,128)(2,1)}, bf16[8,32,2048]{2,1,0:T(8,128)(2,1)}) custom-call(bf16[1,512,1024]{2,1,0:T(8,128)(2,1)} %bitcast.94, bf16[3,1,512,1024]{3,2,1,0:T(8,128)(2,1)} %bitcast.92), custom_call_target="tpu_custom_call" | custom-call | flops 6000000000 | tf_op jit(solution)/shard_map/weight_grad/pallas_call | solution.py:510
  362.7 11.1 %norm_grad.3 = (f32[512,1024]{1,0:T(8,128)}, bf16[512,1024]{1,0:T(8,128)(2,1)}, f32[1,1024]{1,0:T(1,128)}) custom-call(bf16[3,512,1024]{2,1,0:T(8,128)(2,1)} %self_backward.1.d_ref, bf16[1024,3200]{1,0:T(8,128)(2,1)} %bitcast.90, f32[512,1024]{1,0:T(8,128)} %get-tuple-element.123.unit, f32[512,1]{1,0:T(8,128)} %get-tuple-element.124.inverse, ...), custom_call_target="tpu_custom_call" | custom-call | flops 12000000000 | tf_op jit(solution)/shard_map/norm_grad/pallas_call | solution.py:570
  374.7 0.7 gather_fusion
  376.2 2.9 fusion.9
  379.1 2.9 fusion.8
  382.1 1.8 collective-permute-start.2
  383.9 5.0 fusion
  389.0 4.9 add_convert_fusion
  393.9 3.9 copy.79
  397.8 2.6 collective-permute-done.2
  400.4 0.8 collective-permute-start.22
  401.2 1.4 collective-permute-start.18
  402.6 1.6 add_convert_fusion.10
  404.2 0.8 collective-permute-start.15
  405.4 1.3 collective-permute-start.11
  406.7 1.6 add_convert_fusion.14
  408.3 0.8 collective-permute-start.7
  409.1 1.6 add_convert_fusion.16
  410.7 48.4 %collective-permute-done.15 = bf16[4,32,2048]{2,1,0:T(8,128)(2,1)S(1)} collective-permute-done((bf16[4,32,2048]{2,1,0:T(8,128)(2,1)S(1)}, bf16[4,32,2048]{2,1,0:T(8,128)(2,1)S(1)}, u32[]{:S(2)}, u32[]{:S(2)}) %collective-permute-start.15) | collective-permute-done | bytes 524320 | tf_op jit(solution)/shard_map/ppermute | solution.py:987
  459.1 1.4 collective-permute-start.3
  460.8 10.5 %collective-permute-done.7 = bf16[4,32,2048]{2,1,0:T(8,128)(2,1)S(1)} collective-permute-done((bf16[4,32,2048]{2,1,0:T(8,128)(2,1)S(1)}, bf16[4,32,2048]{2,1,0:T(8,128)(2,1)S(1)}, u32[]{:S(2)}, u32[]{:S(2)}) %collective-permute-start.7) | collective-permute-done | bytes 524320 | tf_op jit(solution)/shard_map/ppermute | solution.py:987
  471.5 10.3 %collective-permute-done.3 = bf16[4,32,2176]{2,1,0:T(8,128)(2,1)S(1)} collective-permute-done((bf16[4,32,2176]{2,1,0:T(8,128)(2,1)S(1)}, bf16[4,32,2176]{2,1,0:T(8,128)(2,1)S(1)}, u32[]{:S(2)}, u32[]{:S(2)}) %collective-permute-start.3) | collective-permute-done | bytes 557088 | tf_op jit(solution)/shard_map/ppermute | solution.py:987
  482.0 2.1 collective-permute-start.4
  484.6 10.6 %collective-permute-done.8 = bf16[2,32,2048]{2,1,0:T(8,128)(2,1)S(1)} collective-permute-done((bf16[2,32,2048]{2,1,0:T(8,128)(2,1)S(1)}, bf16[2,32,2048]{2,1,0:T(8,128)(2,1)S(1)}, u32[]{:S(2)}, u32[]{:S(2)}) %collective-permute-start.8) | collective-permute-done | bytes 262176 | tf_op jit(solution)/shard_map/ppermute | solution.py:987
  495.2 3.6 collective-permute-done.4
  498.9 3.0 collective-permute-start.5
  501.9 0.7 fusion.15
  502.7 6.2 %collective-permute-done.13 = bf16[1,32,2048]{2,1,0:T(8,128)(2,1)S(1)} collective-permute-done((bf16[1,32,2048]{2,1,0:T(8,128)(2,1)S(1)}, bf16[1,32,2048]{2,1,0:T(8,128)(2,1)S(1)}, u32[]{:S(2)}, u32[]{:S(2)}) %collective-permute-start.13) | collective-permute-done | bytes 131104 | tf_op jit(solution)/shard_map/ppermute | solution.py:987
  509.0 1.0 add_convert_fusion.2
  510.0 1.6 collective-permute-start.23
  511.6 0.8 add_convert_fusion.4
  513.8 0.7 fusion.16
  514.5 11.6 %collective-permute-done.23 = bf16[4,128,1024]{2,1,0:T(8,128)(2,1)S(1)} collective-permute-done((bf16[4,128,1024]{2,1,0:T(8,128)(2,1)S(1)}, bf16[4,128,1024]{2,1,0:T(8,128)(2,1)S(1)}, u32[]{:S(2)}, u32[]{:S(2)}) %collective-permute-start.23) | collective-permute-done | bytes 1048608 | tf_op jit(solution)/shard_map/ppermute | solution.py:987
  526.6 1.5 collective-permute-done.19
  529.0 0.7 fusion.13
  529.7 9.4 %collective-permute-done.24 = bf16[2,128,1024]{2,1,0:T(8,128)(2,1)S(1)} collective-permute-done((bf16[2,128,1024]{2,1,0:T(8,128)(2,1)S(1)}, bf16[2,128,1024]{2,1,0:T(8,128)(2,1)S(1)}, u32[]{:S(2)}, u32[]{:S(2)}) %collective-permute-start.24) | collective-permute-done | bytes 524320 | tf_op jit(solution)/shard_map/ppermute | solution.py:987
  539.1 2.6 collective-permute-start.25
  541.7 8.4 %collective-permute-done.20 = bf16[2,32,4096]{2,1,0:T(8,128)(2,1)S(1)} collective-permute-done((bf16[2,32,4096]{2,1,0:T(8,128)(2,1)S(1)}, bf16[2,32,4096]{2,1,0:T(8,128)(2,1)S(1)}, u32[]{:S(2)}, u32[]{:S(2)}) %collective-permute-start.20) | collective-permute-done | bytes 524320 | tf_op jit(solution)/shard_map/ppermute | solution.py:987
  550.3 0.7 slice_reduce_fusion
  551.1 0.9 add_bitcast_fusion
  552.0 7.4 %collective-permute-done.21 = bf16[1,32,4096]{2,1,0:T(8,128)(2,1)S(1)} collective-permute-done((bf16[1,32,4096]{2,1,0:T(8,128)(2,1)S(1)}, bf16[1,32,4096]{2,1,0:T(8,128)(2,1)S(1)}, u32[]{:S(2)}, u32[]{:S(2)}) %collective-permute-start.21) | collective-permute-done | bytes 262176 | tf_op jit(solution)/shard_map/ppermute | solution.py:987
  559.4 0.9 add_bitcast_fusion.1
  (120 shorter events, 8.8 us)
Async XLA Ops:
  7.2 188.9 %all-gather.3.cloned.1.call-start = ((), (), s32[]{:S(2)}) async-start(), calls=%async_computation | async-start | bytes 17301504 | tf_op jit(solution)/shard_map/all_gather | solution.py:1046
  9.6 43.7 %copy-start.7 = (bf16[32,4096]{1,0:T(8,128)(2,1)S(1)}, bf16[32,4096]{1,0:T(8,128)(2,1)}, u32[]{:S(2)}) copy-start(bf16[32,4096]{1,0:T(8,128)(2,1)} %param.35) | copy-start | bytes 786436
  9.6 43.9 %copy-start.8 = (bf16[128,1024]{1,0:T(8,128)(2,1)S(1)}, bf16[128,1024]{1,0:T(8,128)(2,1)}, u32[]{:S(2)}) copy-start(bf16[128,1024]{1,0:T(8,128)(2,1)} %param.36) | copy-start | bytes 786436
  53.3 1.8 copy-start.17
  53.4 2.6 copy-start
  56.0 2.2 copy-start.20
  56.0 2.8 copy-start.9
  56.0 2.9 copy-start.10
  56.0 2.9 copy-start.11
  56.0 2.9 copy-start.12
  56.0 2.9 copy-start.13
  59.0 6.6 %copy-start.14 = (bf16[32,5120]{1,0:T(8,128)(2,1)}, bf16[32,5120]{1,0:T(8,128)(2,1)S(1)}, u32[]{:S(2)}) copy-start(bf16[32,5120]{1,0:T(8,128)(2,1)S(1)} %constant_dynamic-update-slice_fusion.x_ref) | copy-start | bytes 983044
  295.3 109.0 %collective-permute-start.10 = (bf16[8,32,2048]{2,1,0:T(8,128)(2,1)}, bf16[8,32,2048]{2,1,0:T(8,128)(2,1)S(1)}, u32[]{:S(2)}, u32[]{:S(2)}) collective-permute-start(bf16[8,32,2048]{2,1,0:T(8,128)(2,1)} %get-tuple-element.106), channel_id=1, source_target_pairs={{0,1},{1,0},{2,3},{3,2},{4,5},{5,4},{6,7},{7,6},{8,9},{9,8},{10,11... | collective-permute-start | bytes 3145736 | tf_op jit(solution)/shard_map/ppermute | solution.py:987
  310.3 90.9 %collective-permute-start.14 = (bf16[8,32,2048]{2,1,0:T(8,128)(2,1)}, bf16[8,32,2048]{2,1,0:T(8,128)(2,1)}, u32[]{:S(2)}, u32[]{:S(2)}) collective-permute-start(bf16[8,32,2048]{2,1,0:T(8,128)(2,1)} %get-tuple-element.108), channel_id=1, source_target_pairs={{0,2},{1,3},{2,0},{3,1},{4,6},{5,7},{6,4},{7,5},{8,10},{9,11},{10,... | collective-permute-start | bytes 3145736 | tf_op jit(solution)/shard_map/ppermute | solution.py:987
  350.8 54.6 %collective-permute-start.6 = (bf16[8,32,2048]{2,1,0:T(8,128)(2,1)}, bf16[8,32,2048]{2,1,0:T(8,128)(2,1)}, u32[]{:S(2)}, u32[]{:S(2)}) collective-permute-start(bf16[8,32,2048]{2,1,0:T(8,128)(2,1)} %get-tuple-element.119), channel_id=1, source_target_pairs={{0,1},{1,0},{2,3},{3,2},{4,5},{5,4},{6,7},{7,6},{8,9},{9,8},{10,11... | collective-permute-start | bytes 3145736 | tf_op jit(solution)/shard_map/ppermute | solution.py:987
  362.6 45.7 %collective-permute-start.1 = (bf16[8,32,2048]{2,1,0:T(8,128)(2,1)}, bf16[8,32,2048]{2,1,0:T(8,128)(2,1)}, u32[]{:S(2)}, u32[]{:S(2)}) collective-permute-start(bf16[8,32,2048]{2,1,0:T(8,128)(2,1)} %get-tuple-element.121), channel_id=1, source_target_pairs={{0,1},{1,0},{2,3},{3,2},{4,5},{5,4},{6,7},{7,6},{8,9},{9,8},{10,11... | collective-permute-start | bytes 3145736 | tf_op jit(solution)/shard_map/ppermute | solution.py:987
  362.7 11.8 %copy-start.16 = (f32[1,1024]{1,0:T(1,128)S(1)}, f32[1,1024]{1,0:T(1,128)}, u32[]{:S(2)}) copy-start(f32[1,1024]{1,0:T(1,128)} %get-tuple-element.129) | copy-start | bytes 12292
  362.7 11.8 %copy-start.15 = (f32[1,1024]{1,0:T(1,128)S(1)}, f32[1,1024]{1,0:T(1,128)}, u32[]{:S(2)}) copy-start(f32[1,1024]{1,0:T(1,128)} %get-tuple-element.130) | copy-start | bytes 12292
  362.7 13.4 %copy-start.21 = (bf16[512,512]{1,0:T(8,128)(2,1)S(1)}, bf16[512,512]{1,0:T(8,128)(2,1)}, u32[]{:S(2)}) copy-start(bf16[512,512]{1,0:T(8,128)(2,1)} %get-tuple-element.78) | copy-start | bytes 1572868
  375.8 6.3 %collective-permute-start = (bf16[16,32,128]{2,1,0:T(8,128)(2,1)S(1)}, bf16[16,32,128]{2,1,0:T(8,128)(2,1)S(1)}, u32[]{:S(2)}, u32[]{:S(2)}) collective-permute-start(bf16[16,32,128]{2,1,0:T(8,128)(2,1)S(1)} %pad_slice_fusion.2), channel_id=1, source_target_pairs={{0,4},{1,5},{2,6},{3,7},{4,0},{5,1},{6,2},{7,3},{8,12},{9,13},{10,... | collective-permute-start | bytes 393224 | tf_op jit(solution)/shard_map/ppermute | solution.py:987
  382.1 6.8 %slice-start = ((s8[4849664]{0:T(1024)(128)(4,1)}), s8[4194304]{0:T(1024)(128)(4,1)S(1)}, s32[]{:S(2)}) async-start(s8[4849664]{0:T(1024)(128)(4,1)} %bitcast.99), calls=%async_computation.1 | async-start | bytes 8388608
  382.1 6.8 %slice-start.1 = ((s8[4849664]{0:T(1024)(128)(4,1)}), s8[655360]{0:T(1024)(128)(4,1)S(1)}, s32[]{:S(2)}) async-start(s8[4849664]{0:T(1024)(128)(4,1)} %bitcast.99), calls=%async_computation.2 | async-start | bytes 1310720
  382.1 18.3 %collective-permute-start.2 = (bf16[8,32,128]{2,1,0:T(8,128)(2,1)S(1)}, bf16[8,32,128]{2,1,0:T(8,128)(2,1)S(1)}, u32[]{:S(2)}, u32[]{:S(2)}) collective-permute-start(bf16[8,32,128]{2,1,0:T(8,128)(2,1)S(1)} %slice.388), channel_id=1, source_target_pairs={{0,1},{1,0},{2,3},{3,2},{4,5},{5,4},{6,7},{7,6},{8,9},{9,8},{10,11... | collective-permute-start | bytes 196616 | tf_op jit(solution)/shard_map/ppermute | solution.py:987
  388.9 11.4 %copy-start.19 = (bf16[8,128,1024]{2,1,0:T(8,128)(2,1)S(1)}, bf16[8,128,1024]{2,1,0:T(8,128)(2,1)}, u32[]{:S(2)}) copy-start(bf16[8,128,1024]{2,1,0:T(8,128)(2,1)} %get-tuple-element.139) | copy-start | bytes 6291460
  393.8 7.4 %copy-start.18 = (bf16[8,32,4096]{2,1,0:T(8,128)(2,1)S(1)}, bf16[8,32,4096]{2,1,0:T(8,128)(2,1)}, u32[]{:S(2)}) copy-start(bf16[8,32,4096]{2,1,0:T(8,128)(2,1)} %get-tuple-element.137) | copy-start | bytes 6291460
  393.8 8.8 %copy-start.3 = (bf16[8,32,2048]{2,1,0:T(8,128)(2,1)S(1)}, bf16[8,32,2048]{2,1,0:T(8,128)(2,1)}, u32[]{:S(2)}) copy-start(bf16[8,32,2048]{2,1,0:T(8,128)(2,1)} %get-tuple-element.135) | copy-start | bytes 3145732
  397.7 7.2 %copy-start.5 = (bf16[8,32,2048]{2,1,0:T(8,128)(2,1)S(1)}, bf16[8,32,2048]{2,1,0:T(8,128)(2,1)}, u32[]{:S(2)}) copy-start(bf16[8,32,2048]{2,1,0:T(8,128)(2,1)} %get-tuple-element.134) | copy-start | bytes 3145732
  400.4 108.6 %collective-permute-start.22 = (bf16[8,128,1024]{2,1,0:T(8,128)(2,1)S(1)}, bf16[8,128,1024]{2,1,0:T(8,128)(2,1)S(1)}, u32[]{:S(2)}, u32[]{:S(2)}) collective-permute-start(bf16[8,128,1024]{2,1,0:T(8,128)(2,1)S(1)} %copy-done.19), channel_id=1, source_target_pairs={{0,2},{1,3},{2,0},{3,1},{4,6},{5,7},{6,4},{7,5},{8,10},{9,11},{10,... | collective-permute-start | bytes 6291464 | tf_op jit(solution)/shard_map/ppermute | solution.py:987
  401.2 110.4 %collective-permute-start.18 = (bf16[8,32,4096]{2,1,0:T(8,128)(2,1)S(1)}, bf16[8,32,4096]{2,1,0:T(8,128)(2,1)S(1)}, u32[]{:S(2)}, u32[]{:S(2)}) collective-permute-start(bf16[8,32,4096]{2,1,0:T(8,128)(2,1)S(1)} %copy-done.18), channel_id=1, source_target_pairs={{0,1},{1,0},{2,3},{3,2},{4,5},{5,4},{6,7},{7,6},{8,9},{9,8},{10,11... | collective-permute-start | bytes 6291464 | tf_op jit(solution)/shard_map/ppermute | solution.py:987
  404.2 2.5 copy-start.6
  404.2 54.9 %collective-permute-start.15 = (bf16[4,32,2048]{2,1,0:T(8,128)(2,1)S(1)}, bf16[4,32,2048]{2,1,0:T(8,128)(2,1)S(1)}, u32[]{:S(2)}, u32[]{:S(2)}) collective-permute-start(bf16[4,32,2048]{2,1,0:T(8,128)(2,1)S(1)} %get-tuple-element.232), channel_id=1, source_target_pairs={{0,1},{1,0},{2,3},{3,2},{4,5},{5,4},{6,7},{7,6},{8,9},{9,8},{10,11... | collective-permute-start | bytes 1572872 | tf_op jit(solution)/shard_map/ppermute | solution.py:987
  405.4 3.7 copy-start.4
  405.4 55.2 %collective-permute-start.11 = (bf16[4,32,2048]{2,1,0:T(8,128)(2,1)S(1)}, bf16[4,32,2048]{2,1,0:T(8,128)(2,1)S(1)}, u32[]{:S(2)}, u32[]{:S(2)}) collective-permute-start(bf16[4,32,2048]{2,1,0:T(8,128)(2,1)S(1)} %get-tuple-element.234), channel_id=1, source_target_pairs={{0,2},{1,3},{2,0},{3,1},{4,6},{5,7},{6,4},{7,5},{8,10},{9,11},{10,... | collective-permute-start | bytes 1572872 | tf_op jit(solution)/shard_map/ppermute | solution.py:987
  408.3 63.1 %collective-permute-start.7 = (bf16[4,32,2048]{2,1,0:T(8,128)(2,1)S(1)}, bf16[4,32,2048]{2,1,0:T(8,128)(2,1)S(1)}, u32[]{:S(2)}, u32[]{:S(2)}) collective-permute-start(bf16[4,32,2048]{2,1,0:T(8,128)(2,1)S(1)} %get-tuple-element.236), channel_id=1, source_target_pairs={{0,2},{1,3},{2,0},{3,1},{4,6},{5,7},{6,4},{7,5},{8,10},{9,11},{10,... | collective-permute-start | bytes 1572872 | tf_op jit(solution)/shard_map/ppermute | solution.py:987
  459.1 22.7 %collective-permute-start.3 = (bf16[4,32,2176]{2,1,0:T(8,128)(2,1)S(1)}, bf16[4,32,2176]{2,1,0:T(8,128)(2,1)S(1)}, u32[]{:S(2)}, u32[]{:S(2)}) collective-permute-start(bf16[4,32,2176]{2,1,0:T(8,128)(2,1)S(1)} %pad_maximum_fusion), channel_id=1, source_target_pairs={{0,2},{1,3},{2,0},{3,1},{4,6},{5,7},{6,4},{7,5},{8,10},{9,11},{10,... | collective-permute-start | bytes 1671176 | tf_op jit(solution)/shard_map/ppermute | solution.py:987
  460.6 21.3 %collective-permute-start.16 = (bf16[2,32,2048]{2,1,0:T(8,128)(2,1)S(1)}, bf16[2,32,2048]{2,1,0:T(8,128)(2,1)S(1)}, u32[]{:S(2)}, u32[]{:S(2)}) collective-permute-start(bf16[2,32,2048]{2,1,0:T(8,128)(2,1)S(1)} %get-tuple-element.242), channel_id=1, source_target_pairs={{0,8},{1,9},{2,10},{3,11},{4,12},{5,13},{6,14},{7,15},{8,0},{9,1},... | collective-permute-start | bytes 786440 | tf_op jit(solution)/shard_map/ppermute | solution.py:987
  471.3 12.8 %collective-permute-start.12 = (bf16[2,32,2048]{2,1,0:T(8,128)(2,1)S(1)}, bf16[2,32,2048]{2,1,0:T(8,128)(2,1)S(1)}, u32[]{:S(2)}, u32[]{:S(2)}) collective-permute-start(bf16[2,32,2048]{2,1,0:T(8,128)(2,1)S(1)} %get-tuple-element.244), channel_id=1, source_target_pairs={{0,8},{1,9},{2,10},{3,11},{4,12},{5,13},{6,14},{7,15},{8,0},{9,1},... | collective-permute-start | bytes 786440 | tf_op jit(solution)/shard_map/ppermute | solution.py:987
  481.8 13.4 %collective-permute-start.8 = (bf16[2,32,2048]{2,1,0:T(8,128)(2,1)S(1)}, bf16[2,32,2048]{2,1,0:T(8,128)(2,1)S(1)}, u32[]{:S(2)}, u32[]{:S(2)}) collective-permute-start(bf16[2,32,2048]{2,1,0:T(8,128)(2,1)S(1)} %get-tuple-element.246), channel_id=1, source_target_pairs={{0,8},{1,9},{2,10},{3,11},{4,12},{5,13},{6,14},{7,15},{8,0},{9,1},... | collective-permute-start | bytes 786440 | tf_op jit(solution)/shard_map/ppermute | solution.py:987
  482.0 27.0 %copy-start.2 = (bf16[8,128,1024]{2,1,0:T(8,128)(2,1)S(1)}, bf16[8,128,1024]{2,1,0:T(8,128)(2,1)}, u32[]{:S(2)}) copy-start(bf16[8,128,1024]{2,1,0:T(8,128)(2,1)} %get-tuple-element.138) | copy-start | bytes 6291460
  482.0 16.9 %collective-permute-start.4 = (bf16[2,32,2176]{2,1,0:T(8,128)(2,1)S(1)}, bf16[2,32,2176]{2,1,0:T(8,128)(2,1)S(1)}, u32[]{:S(2)}, u32[]{:S(2)}) collective-permute-start(bf16[2,32,2176]{2,1,0:T(8,128)(2,1)S(1)} %get-tuple-element.240), channel_id=1, source_target_pairs={{0,8},{1,9},{2,10},{3,11},{4,12},{5,13},{6,14},{7,15},{8,0},{9,1},... | collective-permute-start | bytes 835592 | tf_op jit(solution)/shard_map/ppermute | solution.py:987
  484.1 14.8 %collective-permute-start.17 = (bf16[1,32,2048]{2,1,0:T(8,128)(2,1)S(1)}, bf16[1,32,2048]{2,1,0:T(8,128)(2,1)S(1)}, u32[]{:S(2)}, u32[]{:S(2)}) collective-permute-start(bf16[1,32,2048]{2,1,0:T(8,128)(2,1)S(1)} %add_convert_fusion.31), channel_id=1, source_target_pairs={{0,16},{1,17},{2,18},{3,19},{4,20},{5,21},{6,22},{7,23},{8,24},{9,... | collective-permute-start | bytes 393224 | tf_op jit(solution)/shard_map/ppermute | solution.py:987
  495.2 13.7 %collective-permute-start.13 = (bf16[1,32,2048]{2,1,0:T(8,128)(2,1)S(1)}, bf16[1,32,2048]{2,1,0:T(8,128)(2,1)S(1)}, u32[]{:S(2)}, u32[]{:S(2)}) collective-permute-start(bf16[1,32,2048]{2,1,0:T(8,128)(2,1)S(1)} %add_convert_fusion.33), channel_id=1, source_target_pairs={{0,16},{1,17},{2,18},{3,19},{4,20},{5,21},{6,22},{7,23},{8,24},{9,... | collective-permute-start | bytes 393224 | tf_op jit(solution)/shard_map/ppermute | solution.py:987
  498.8 14.9 %collective-permute-start.9 = (bf16[1,32,2048]{2,1,0:T(8,128)(2,1)S(1)}, bf16[1,32,2048]{2,1,0:T(8,128)(2,1)S(1)}, u32[]{:S(2)}, u32[]{:S(2)}) collective-permute-start(bf16[1,32,2048]{2,1,0:T(8,128)(2,1)S(1)} %add_convert_fusion.35), channel_id=1, source_target_pairs={{0,16},{1,17},{2,18},{3,19},{4,20},{5,21},{6,22},{7,23},{8,24},{9,... | collective-permute-start | bytes 393224 | tf_op jit(solution)/shard_map/ppermute | solution.py:987
  498.9 30.0 %collective-permute-start.5 = (bf16[1,32,2176]{2,1,0:T(8,128)(2,1)S(1)}, bf16[1,32,2176]{2,1,0:T(8,128)(2,1)S(1)}, u32[]{:S(2)}, u32[]{:S(2)}) collective-permute-start(bf16[1,32,2176]{2,1,0:T(8,128)(2,1)S(1)} %add_convert_fusion.29), channel_id=1, source_target_pairs={{0,16},{1,17},{2,18},{3,19},{4,20},{5,21},{6,22},{7,23},{8,24},{9,... | collective-permute-start | bytes 417800 | tf_op jit(solution)/shard_map/ppermute | solution.py:987
  509.0 2.7 copy-start.1
  510.0 16.1 %collective-permute-start.23 = (bf16[4,128,1024]{2,1,0:T(8,128)(2,1)S(1)}, bf16[4,128,1024]{2,1,0:T(8,128)(2,1)S(1)}, u32[]{:S(2)}, u32[]{:S(2)}) collective-permute-start(bf16[4,128,1024]{2,1,0:T(8,128)(2,1)S(1)} %get-tuple-element.224), channel_id=1, source_target_pairs={{0,1},{1,0},{2,3},{3,2},{4,5},{5,4},{6,7},{7,6},{8,9},{9,8},{10,11... | collective-permute-start | bytes 3145736 | tf_op jit(solution)/shard_map/ppermute | solution.py:987
  512.4 15.7 %collective-permute-start.19 = (bf16[4,32,4096]{2,1,0:T(8,128)(2,1)S(1)}, bf16[4,32,4096]{2,1,0:T(8,128)(2,1)S(1)}, u32[]{:S(2)}, u32[]{:S(2)}) collective-permute-start(bf16[4,32,4096]{2,1,0:T(8,128)(2,1)S(1)} %get-tuple-element.226), channel_id=1, source_target_pairs={{0,2},{1,3},{2,0},{3,1},{4,6},{5,7},{6,4},{7,5},{8,10},{9,11},{10,... | collective-permute-start | bytes 3145736 | tf_op jit(solution)/shard_map/ppermute | solution.py:987
  526.5 12.6 %collective-permute-start.24 = (bf16[2,128,1024]{2,1,0:T(8,128)(2,1)S(1)}, bf16[2,128,1024]{2,1,0:T(8,128)(2,1)S(1)}, u32[]{:S(2)}, u32[]{:S(2)}) collective-permute-start(bf16[2,128,1024]{2,1,0:T(8,128)(2,1)S(1)} %get-tuple-element.228), channel_id=1, source_target_pairs={{0,8},{1,9},{2,10},{3,11},{4,12},{5,13},{6,14},{7,15},{8,0},{9,1},... | collective-permute-start | bytes 1572872 | tf_op jit(solution)/shard_map/ppermute | solution.py:987
  528.3 21.8 %collective-permute-start.20 = (bf16[2,32,4096]{2,1,0:T(8,128)(2,1)S(1)}, bf16[2,32,4096]{2,1,0:T(8,128)(2,1)S(1)}, u32[]{:S(2)}, u32[]{:S(2)}) collective-permute-start(bf16[2,32,4096]{2,1,0:T(8,128)(2,1)S(1)} %get-tuple-element.230), channel_id=1, source_target_pairs={{0,8},{1,9},{2,10},{3,11},{4,12},{5,13},{6,14},{7,15},{8,0},{9,1},... | collective-permute-start | bytes 1572872 | tf_op jit(solution)/shard_map/ppermute | solution.py:987
  539.1 11.9 %collective-permute-start.25 = (bf16[1,128,1024]{2,1,0:T(8,128)(2,1)S(1)}, bf16[1,128,1024]{2,1,0:T(8,128)(2,1)S(1)}, u32[]{:S(2)}, u32[]{:S(2)}) collective-permute-start(bf16[1,128,1024]{2,1,0:T(8,128)(2,1)S(1)} %add_convert_fusion.19), channel_id=1, source_target_pairs={{0,16},{1,17},{2,18},{3,19},{4,20},{5,21},{6,22},{7,23},{8,24},{9,... | collective-permute-start | bytes 786440 | tf_op jit(solution)/shard_map/ppermute | solution.py:987
  550.3 9.1 %collective-permute-start.21 = (bf16[1,32,4096]{2,1,0:T(8,128)(2,1)S(1)}, bf16[1,32,4096]{2,1,0:T(8,128)(2,1)S(1)}, u32[]{:S(2)}, u32[]{:S(2)}) collective-permute-start(bf16[1,32,4096]{2,1,0:T(8,128)(2,1)S(1)} %add_convert_fusion.21), channel_id=1, source_target_pairs={{0,16},{1,17},{2,18},{3,19},{4,20},{5,21},{6,22},{7,23},{8,24},{9,... | collective-permute-start | bytes 786440 | tf_op jit(solution)/shard_map/ppermute | solution.py:987
Sparse Core Ops, SparseCore 0:
  55.3 134.8 all-gather.2

commit v4 on v3

--- a/solution.py
+++ b/solution.py
@@ -271,27 +271,34 @@
     return image, pl.multiple_of(tile * TILE, TILE)
 
 
+PARTS = 2
+
+
 def cross_forward_kernel(count_ref, q, k, v, out, totals):
-    scale = LOG2E * (q.shape[1] // 2) ** (-0.5)
+    scale = LOG2E * (q.shape[1] // (2 * PARTS)) ** (-0.5)
     count = count_ref[0]
     first, skip, steps = cross_steps(count, q.shape[0] // TILE)
 
     def one(step, carry):
         image, start = cross_step(step, first, skip)
-        here = pl.ds(start, TILE)
-        scores = product_t(k[image], two_heads(q[here, :])) * scale
-        highest = jnp.max(scores, axis=0, keepdims=True)
-        weights = jnp.exp2(scores - highest)
-        total = jnp.sum(weights, axis=0, keepdims=True)
-        mixed = product_rows(v[image], weights.astype(bf16)) * (1.0 / total)
+        at = pl.ds(start, TILE)
         row = start + lax.broadcasted_iota(jnp.int32, (TILE, 128), 0)
-        mine = (row >= count) == (image == 1)
-        out[here, :] = jnp.where(mine, join_heads(mixed), out[here, :].astype(f32)).astype(bf16)
-        level = highest + jnp.log2(total)
         lane = start + lax.broadcasted_iota(jnp.int32, (1, TILE), 1)
-        mine = (lane >= count) == (image == 1)
-        totals[0, 0:1, here] = jnp.where(mine, level[:, :TILE], totals[0, 0:1, here])
-        totals[0, 1:2, here] = jnp.where(mine, level[:, TILE:], totals[0, 1:2, here])
+        here_row, here_lane = ((x >= count) == (image == 1) for x in (row, lane))
+        lanes = [slice(128 * part, 128 * (part + 1)) for part in range(PARTS)]
+        scores = [product_t(k[image, :, l], two_heads(q[at, l])) * scale for l in lanes]
+        for part, l in enumerate(lanes):
+            highest = jnp.max(scores[part], axis=0, keepdims=True)
+            weights = jnp.exp2(scores[part] - highest)
+            total = jnp.sum(weights, axis=0, keepdims=True)
+            mixed = product_rows(v[image, :, l], weights.astype(bf16)) * (1.0 / total)
+            old = out[at, l].astype(f32)
+            out[at, l] = jnp.where(here_row, join_heads(mixed), old).astype(bf16)
+            level = highest + jnp.log2(total)
+            for head in range(2):
+                index = slice(2 * part + head, 2 * part + head + 1)
+                mine = level[:, head * TILE : (head + 1) * TILE]
+                totals[0, index, at] = jnp.where(here_lane, mine, totals[0, index, at])
         return carry
 
     lax.fori_loop(0, steps, one, 0)
@@ -299,26 +306,27 @@
 
 def cross_forward(count, query, kv):
     rows, width = query.shape
-    pairs = width // 128
+    wide = 128 * PARTS
+    turns = width // wide
     images, length = kv.shape[:2]
     return pl.pallas_call(
         cross_forward_kernel,
         grid_spec=pltpu.PrefetchScalarGridSpec(
             num_scalar_prefetch=1,
-            grid=(pairs,),
+            grid=(turns,),
             in_specs=[
-                pl.BlockSpec((rows, 128), lambda j, c: (0, j)),
-                pl.BlockSpec((images, length, 128), lambda j, c: (0, 0, j)),
-                pl.BlockSpec((images, length, 128), lambda j, c: (0, 0, pairs + j)),
+                pl.BlockSpec((rows, wide), lambda j, c: (0, j)),
+                pl.BlockSpec((images, length, wide), lambda j, c: (0, 0, j)),
+                pl.BlockSpec((images, length, wide), lambda j, c: (0, 0, turns + j)),
             ],
             out_specs=[
-                pl.BlockSpec((rows, 128), lambda j, c: (0, j)),
-                pl.BlockSpec((1, 2, rows), lambda j, c: (j, 0, 0)),
+                pl.BlockSpec((rows, wide), lambda j, c: (0, j)),
+                pl.BlockSpec((1, 2 * PARTS, rows), lambda j, c: (j, 0, 0)),
             ],
         ),
         out_shape=[
             jax.ShapeDtypeStruct((rows, width), bf16),
-            jax.ShapeDtypeStruct((pairs, 2, rows), f32),
+            jax.ShapeDtypeStruct((turns, 2 * PARTS, rows), f32),
         ],
         compiler_params=params(1),
         name="cross_forward",
@@ -327,7 +335,7 @@
 
 
 def cross_backward_kernel(count_ref, q, k, v, g, totals, dq_out, dkv_out, dq, dk, dv):
-    half_scale = (q.shape[1] // 2) ** (-0.5)
+    half_scale = (q.shape[1] // (2 * PARTS)) ** (-0.5)
     scale = LOG2E * half_scale
     count = count_ref[0]
     first, skip, steps = cross_steps(count, q.shape[0] // TILE)
@@ -337,23 +345,28 @@
 
     def one(step, carry):
         image, start = cross_step(step, first, skip)
-        here = pl.ds(start, TILE)
-        queries, grads = two_heads(q[here, :]), two_heads(g[here, :])
+        at = pl.ds(start, TILE)
         lane = start + lax.broadcasted_iota(jnp.int32, (1, TILE), 1)
         mine = (lane >= count) == (image == 1)
-        level = jnp.concatenate(
-            [
-                jnp.where(mine, totals[0, 0:1, here], -MASKED),
-                jnp.where(mine, totals[0, 1:2, here], -MASKED),
-            ],
-            axis=1,
-        )
-        weights = jnp.exp2(product_t(k[image], queries) * scale - level)
-        along = weights * product_t(v[image], grads)
-        change = (along - weights * jnp.sum(along, axis=0, keepdims=True)).astype(bf16)
-        dv[image] += product(weights.astype(bf16), grads)
-        dk[image] += product(change, queries)
-        dq[here, :] += join_heads(product_rows(k[image], change))
+        lanes = [slice(128 * part, 128 * (part + 1)) for part in range(PARTS)]
+        queries = [two_heads(q[at, l]) for l in lanes]
+        grads = [two_heads(g[at, l]) for l in lanes]
+        scores = [product_t(k[image, :, l], queries[part]) for part, l in enumerate(lanes)]
+        along = [product_t(v[image, :, l], grads[part]) for part, l in enumerate(lanes)]
+        for part, l in enumerate(lanes):
+            level = jnp.concatenate(
+                [
+                    jnp.where(mine, totals[0, 2 * part + head : 2 * part + head + 1, at], -MASKED)
+                    for head in range(2)
+                ],
+                axis=1,
+            )
+            weights = jnp.exp2(scores[part] * scale - level)
+            dv[image, :, l] += product(weights.astype(bf16), grads[part])
+            change = weights * along[part]
+            change = (change - weights * jnp.sum(change, axis=0, keepdims=True)).astype(bf16)
+            dk[image, :, l] += product(change, queries[part])
+            dq[at, l] += join_heads(product_rows(k[image, :, l], change))
         return carry
 
     lax.fori_loop(0, steps, one, 0)
@@ -364,28 +377,29 @@
 
 def cross_backward(count, query, kv, grads, totals):
     rows, width = query.shape
-    pairs = width // 128
+    wide = 128 * PARTS
+    turns = width // wide
     images, length = kv.shape[:2]
     return pl.pallas_call(
         cross_backward_kernel,
         grid_spec=pltpu.PrefetchScalarGridSpec(
             num_scalar_prefetch=1,
-            grid=(pairs,),
+            grid=(turns,),
             in_specs=[
-                pl.BlockSpec((rows, 128), lambda j, c: (0, j)),
-                pl.BlockSpec((images, length, 128), lambda j, c: (0, 0, j)),
-                pl.BlockSpec((images, length, 128), lambda j, c: (0, 0, pairs + j)),
-                pl.BlockSpec((rows, 128), lambda j, c: (0, j)),
-                pl.BlockSpec((1, 2, rows), lambda j, c: (j, 0, 0)),
+                pl.BlockSpec((rows, wide), lambda j, c: (0, j)),
+                pl.BlockSpec((images, length, wide), lambda j, c: (0, 0, j)),
+                pl.BlockSpec((images, length, wide), lambda j, c: (0, 0, turns + j)),
+                pl.BlockSpec((rows, wide), lambda j, c: (0, j)),
+                pl.BlockSpec((1, 2 * PARTS, rows), lambda j, c: (j, 0, 0)),
             ],
             out_specs=[
-                pl.BlockSpec((rows, 128), lambda j, c: (0, j)),
-                pl.BlockSpec((2, images, length, 128), lambda j, c: (0, 0, 0, j)),
+                pl.BlockSpec((rows, wide), lambda j, c: (0, j)),
+                pl.BlockSpec((2, images, length, wide), lambda j, c: (0, 0, 0, j)),
             ],
             scratch_shapes=[
-                pltpu.VMEM((rows, 128), f32),
-                pltpu.VMEM((images, length, 128), f32),
-                pltpu.VMEM((images, length, 128), f32),
+                pltpu.VMEM((rows, wide), f32),
+                pltpu.VMEM((images, length, wide), f32),
+                pltpu.VMEM((images, length, wide), f32),
             ],
         ),
         out_shape=[
@@ -1080,31 +1094,32 @@
         grad_query_again, second_set, 1, unit_two, inverse_two, gains[1], grad_after_cross, then=True
     )
     grad_qkv = self_backward(page_column, page_row, qkv, grad_mixed_one, log_one)
-    halves = halves_of(6, one_way, mixed_one[None], after(branch_one, grad_qkv)[None, None])
+    halves_kv = halves_of(8, other_way, hidden_one[None], grad_qkv[:, None], only=(1, 3))
+    branch_again = after(branch_one, halves_kv[0])[None, None]
+    halves = halves_of(6, one_way, mixed_one[None], branch_again)
     options = dict(first=width, into=halves, only=(0, 1))
     halves = halves_of(7, one_way, hidden_one[None], grad_qkv[:, None], **options)
     grad_qkv_again = after(grad_qkv, halves[0])
-    halves_kv = halves_of(8, one_way, hidden_one[None], grad_qkv_again[:, None], only=(1, 3))
-    grad_qkv_again = after(grad_qkv, halves_kv[0])
     _, grad_inputs, grad_gain_self = norm_grad(
         grad_qkv_again, first_set, 0, unit_one, inverse_one, gains[0], grad_after_self
     )
     gain_grads = jnp.concatenate([grad_gain_self, grad_gain_cross, grad_gain_ffn])
-    late = gain_halves(gain_grads, devices, lanes, one_way, me)
+    late = gain_halves(gain_grads, devices, lanes, other_way, me)
     grad_a = sums(one_way, halves)
-    grad_b = sums(one_way, halves_kv, late)
+    grad_b = sums(other_way, halves_kv, late)
     gain_sums = grad_b[:, 2 * width :]
 
     grad_kv = after(grad_kv, late[0])
     back = (((2,), (1,)), ((), ()))
     grad_images = lax.dot_general(grad_kv[0], w_kv[:, :width], back, preferred_element_type=f32)
     grad_images += lax.dot_general(grad_kv[1], w_kv[:, width:], back, preferred_element_type=f32)
+    grad_images = grad_images.astype(bf16)
     output = product_rows(order, output).astype(bf16)
     grad_inputs = product_rows(order, grad_inputs).astype(bf16)
     return (
         output[None],
         grad_inputs[None],
-        grad_images.astype(bf16),
+        grad_images,
         gain_sums[:, 0],
         grad_a[:, width:],
         grad_b[:, :width],

time: 576 us -> 559 us (0.970)
  Pallas kernels: 354 us -> 337 us
  starting transfers between devices: 23.9 us -> 32.5 us
  waiting for transfers between devices: 131 us -> 123 us
    ppermute x26, waiting for transfers between devices: 131 us -> 118 us  [swap(): return lax.ppermute(values, AXES, [(i, i ^ bit) for i in range(devices)])]
    pallas_call x1, Pallas kernels: 30.5 us -> 19.3 us  [cross_forward(): pl.pallas_call(cross_forward_kernel, grid_spec=pltpu.PrefetchScalarGridSp...]
    ppermute x26, starting transfers between devices: 23.8 us -> 32.5 us  [swap(): return lax.ppermute(values, AXES, [(i, i ^ bit) for i in range(devices)])]
    pallas_call x1, Pallas kernels: 35.6 us -> 29 us  [cross_backward(): pl.pallas_call(cross_backward_kernel, grid_spec=pltpu.PrefetchScalarGridS...]
  transfers between devices with their start and end apart: 27 -> 27, of which waited for: 12 -> 12; matrix products, arithmetic and copies ran while one was open for 7% -> 7% of each run, Pallas kernels for 37% -> 36%
where the time goes in v4:
time: 559 us; the launch traced here: 551 us
  Pallas kernels  337 us (60%)
  waiting for transfers between devices  123 us (22%)
  starting transfers between devices  32.5 us (6%)
  matrix products  15.8 us (3%)
  between operations  14.9 us (3%)
  other arithmetic  14.4 us (3%)
  local copies, waits for them, and re-layouts  13.4 us (2%)
    ppermute x26, waiting for transfers between devices, swap(): return lax.ppermute(values, AXES, [(i, i ^ bit) for i in range(devices)])  118 us
    pallas_call x1, Pallas kernels, attend(): pl.pallas_call(functools.partial(attend_kernel, devices, lanes, tracks_of...  83.7 us
    pallas_call x6, Pallas kernels, weight_grad(): pl.pallas_call(functools.partial(weight_grad_kernel, devices, lanes, way,...  52.9 us
    pallas_call x1, Pallas kernels, feed(): pl.pallas_call(functools.partial(feed_kernel, devices, lanes, ways), grid...  49 us
    pallas_call x1, Pallas kernels, gather(): pl.pallas_call(functools.partial(gather_kernel, devices, lanes, tracks_of...  43.7 us
    ppermute x26, starting transfers between devices, swap(): return lax.ppermute(values, AXES, [(i, i ^ bit) for i in range(devices)])  32.5 us
    pallas_call x1, Pallas kernels, cross_backward(): pl.pallas_call(cross_backward_kernel, grid_spec=pltpu.PrefetchScalarGridS...  29 us
    pallas_call x2, Pallas kernels, norm_grad(): pl.pallas_call(norm_grad_kernel, grid=(width // wide,), in_specs=[whole((...  21.3 us
  transfers between devices with their start and end apart: 27, of which 12 were waited for; matrix products, arithmetic and copies ran while one was open for 7% of the time, Pallas kernels for 36%

profile of v4, /device:TPU:0, one launch (start us, length us, event | category | flops | bytes accessed | tf_op | source)
XLA Modules:
  0.0 550.8 jit_solution(11949177787950559689)
XLA Ops:
  8.0 1.6 fusion.12.x_ref
  9.6 43.7 %gather.18 = bf16[32,32,3200]{2,1,0:T(8,128)(2,1)} custom-call(bf16[32,3200]{1,0:T(8,128)(2,1)} %fusion.12.x_ref), custom_call_target="tpu_custom_call" | custom-call | flops 60000002048 | tf_op jit(solution)/shard_map/gather/pallas_call | solution.py:894
  54.2 1.0 copy.75
  55.1 0.9 copy.72.page_column
  56.0 2.2 copy.73.images.refs_0_
  59.0 6.5 %arrange.1 = (s32[1]{0:T(128)}, bf16[512,512]{1,0:T(8,128)(2,1)}, s32[512,1]{1,0:T(8,128)}, s32[1,512]{1,0:T(1,128)}, f32[512,1024]{1,0:T(8,128)}, /*index=5*/bf...) custom-call(s32[4]{0:T(128)} %bitcast.84, ...), custom_call_target="tpu_custom_call" | custom-call | flops 6000000000 | tf_op jit(solution)/shard_map/arrange/pallas_call | solution.py:127
  65.5 83.7 %attend.1 = (bf16[32,32,5120]{2,1,0:T(8,128)(2,1)}, bf16[512,1024]{1,0:T(8,128)(2,1)}, bf16[512,1024]{1,0:T(8,128)(2,1)}, bf16[512,1024]{1,0:T(8,128)(2,1)}, bf1...) custom-call(bf16[32,5120]{1,0:T(8,128)(2,1)} %copy-done.14, s32[512,1]{1,0:T(8,128)} %get-tuple-element.79.page_column, ...), custom_call_target="tpu_custom_call" | custom-call | flops 60000002048 | tf_op jit(solution)/shard_map/attend/pallas_call | solution.py:944
  149.2 9.2 %image_keys.1.k.v = bf16[2,588,2048]{2,1,0:T(8,128)(2,1)} custom-call(bf16[2,588,1024]{2,1,0:T(8,128)(2,1)} %copy.73.images.refs_0_, bf16[1024,5120]{1,0:T(8,128)(2,1)} %bitcast.63), custom_call_target="tpu_custom_call" | custom-call | flops 8000000000 | tf_op jit(solution)/shard_map/image_keys/pallas_call | solution.py:985
  158.3 7.2 %between.1 = (f32[512,1024]{1,0:T(8,128)}, bf16[512,1024]{1,0:T(8,128)(2,1)}, f32[512,1024]{1,0:T(8,128)}, f32[512,1]{1,0:T(8,128)}, bf16[512,1024]{1,0:T(8,128)(2,1)}) custom-call(f32[512,1024]{1,0:T(8,128)} %get-tuple-element.78.x_ref, bf16[512,1024]{1,0:T(8,128)(2,1)} %get-tuple-element.82.mixed, bf16[1024,5120]{1,0:T(8,128)(2,1)} %bitcast.64, ...), custom_call_target="tpu_custom_call" | custom-call | flops 8000000000 | tf_op jit(solution)/shard_map/between/pallas_call | solution.py:159
  165.6 19.3 %cross_forward.1 = (bf16[512,1024]{1,0:T(8,128)(2,1)}, f32[4,4,512]{2,1,0:T(4,128)}) custom-call(s32[1]{0:T(128)} %get-tuple-element.86.count_ref, bf16[512,1024]{1,0:T(8,128)(2,1)} %get-tuple-element.87.q, bf16[2,588,2048]{2,1,0:T(8,128)(2,1)} %image_keys.1.k.v, bf16[2,588,2048]{2,1,0:T(8,128)(2,1)} %image_keys.1.k.v), custom_call_target="tpu_custom_call" | custom-call | flops 24000000000 | tf_op jit(solution)/shard_map/cross_forward/pallas_call | solution.py:312
  184.9 5.1 all-gather.3.cloned.1.call-done
  190.0 49.0 %feed.1 = (bf16[512,1024]{1,0:T(8,128)(2,1)}, f32[512,1024]{1,0:T(8,128)}, bf16[512,1024]{1,0:T(8,128)(2,1)}, bf16[512,1024]{1,0:T(8,128)(2,1)}, f32[1,1024]{1,0...) custom-call(f32[512,1024]{1,0:T(8,128)} %get-tuple-element.85.x_ref,, ...), custom_call_target="tpu_custom_call" | custom-call | flops 40000000000 | tf_op jit(solution)/shard_map/feed/pallas_call | solution.py:728
  239.0 29.0 %cross_backward.1 = (bf16[512,1024]{1,0:T(8,128)(2,1)}, bf16[2,2,588,1024]{3,2,1,0:T(8,128)(2,1)}) custom-call(s32[1]{0:T(128)} %get-tuple-element.86.count_ref, bf16[512,1024]{1,0:T(8,128)(2,1)} %get-tuple-element.87.q, bf16[2,588,2048]{2,1,0:T(8,128)(2,1)} %image_keys.1.k.v, bf16[2,588,2048]{2,1,0:T(8,128)(2,1)} %image_keys.1.k.v, ...), custom_call_target="tpu_custom_call" | custom-call | flops 28000000000 | tf_op jit(solution)/shard_map/cross_backward/pallas_call | solution.py:383
  268.1 7.3 %weight_grad.6 = (bf16[8,32,2048]{2,1,0:T(8,128)(2,1)}, bf16[8,32,2048]{2,1,0:T(8,128)(2,1)}) custom-call(bf16[1,512,1024]{2,1,0:T(8,128)(2,1)} %bitcast.96, bf16[1,1,512,1024]{3,2,1,0:T(8,128)(2,1)} %bitcast.97), custom_call_target="tpu_custom_call" | custom-call | flops 3000000000 | tf_op jit(solution)/shard_map/weight_grad/pallas_call | solution.py:524
  275.4 7.2 %weight_grad.7 = (bf16[8,32,2048]{2,1,0:T(8,128)(2,1)}, bf16[8,32,2048]{2,1,0:T(8,128)(2,1)}) custom-call(bf16[1,512,1024]{2,1,0:T(8,128)(2,1)} %bitcast.95, bf16[1,1,512,1024]{3,2,1,0:T(8,128)(2,1)} %bitcast.71, bf16[8,32,2048]{2,1,0:T(8,128)(2,1)} %get-tuple-element.103.refs_2_, ...), custom_call_target="tpu_custom_call", output_to_operand_aliasing={{0}: (2, {}), {1}: (3, {})} | custom-call | flops 3000000000 | tf_op jit(solution)/shard_map/weight_grad/pallas_call | solution.py:524
  282.6 1.0 collective-permute-start.10
  283.6 14.3 %weight_grad.8 = (bf16[8,32,2048]{2,1,0:T(8,128)(2,1)}, bf16[8,32,2048]{2,1,0:T(8,128)(2,1)}) custom-call(bf16[2,588,1024]{2,1,0:T(8,128)(2,1)} %copy.73.images.refs_0_, bf16[2,2,588,1024]{3,2,1,0:T(8,128)(2,1)} %get-tuple-element.129.refs_1_), custom_call_target="tpu_custom_call" | custom-call | flops 12000000000 | tf_op jit(solution)/shard_map/weight_grad/pallas_call | solution.py:524
  298.6 10.2 %norm_grad.2 = (f32[512,1024]{1,0:T(8,128)}, bf16[512,1024]{1,0:T(8,128)(2,1)}, f32[1,1024]{1,0:T(1,128)}, bf16[512,1024]{1,0:T(8,128)(2,1)}) custom-call(bf16[1,512,1024]{2,1,0:T(8,128)(2,1)} %bitcast.72, bf16[1024,5120]{1,0:T(8,128)(2,1)} %bitcast.67, f32[512,1024]{1,0:T(8,128)} %get-tuple-element.109.unit, f32[512,1]{1,0:T(8,128)} %get-tuple-element.110.inverse, ...), custom_call_target="tpu_custom_call" | custom-call | flops 4000000000 | tf_op jit(solution)/shard_map/norm_grad/pallas_call | solution.py:584
  308.8 14.9 %self_backward.1.d_ref = bf16[3,512,1024]{2,1,0:T(8,128)(2,1)} custom-call(s32[512,1]{1,0:T(8,128)} %get-tuple-element.79.page_column, s32[1,512]{1,0:T(1,128)} %get-tuple-element.80.page_row, bf16[512,1024]{1,0:T(8,128)(2,1)} %get-tuple-element.93.q, bf16[512,1024]{1,0:T(8,128)(2,1)} %get-tuple-element.94.k, bf16[512,1024]{1,0:T(8,128)(2,1)} %get-tuple-element.95.v, ...), custom_call_target="tpu_custom_call" | custom-call | flops 15000000512 | tf_op jit(solution)/shard_map/self_backward/pallas_call | solution.py:240
  323.6 9.8 %weight_grad.9 = (bf16[8,32,2048]{2,1,0:T(8,128)(2,1)}, bf16[8,32,2048]{2,1,0:T(8,128)(2,1)}) custom-call(bf16[1,512,1024]{2,1,0:T(8,128)(2,1)} %bitcast.92, bf16[3,1,512,1024]{3,2,1,0:T(8,128)(2,1)} %bitcast.90), custom_call_target="tpu_custom_call" | custom-call | flops 6000000000 | tf_op jit(solution)/shard_map/weight_grad/pallas_call | solution.py:524
  333.4 7.0 %weight_grad.10 = (bf16[8,32,2048]{2,1,0:T(8,128)(2,1)}, bf16[8,32,2048]{2,1,0:T(8,128)(2,1)}) custom-call(bf16[1,512,1024]{2,1,0:T(8,128)(2,1)} %bitcast.94, bf16[1,1,512,1024]{3,2,1,0:T(8,128)(2,1)} %bitcast.83), custom_call_target="tpu_custom_call" | custom-call | flops 3000000000 | tf_op jit(solution)/shard_map/weight_grad/pallas_call | solution.py:524
  340.4 7.4 %weight_grad.11 = (bf16[8,32,2048]{2,1,0:T(8,128)(2,1)}, bf16[8,32,2048]{2,1,0:T(8,128)(2,1)}) custom-call(bf16[1,512,1024]{2,1,0:T(8,128)(2,1)} %bitcast.93, bf16[3,1,512,1024]{3,2,1,0:T(8,128)(2,1)} %bitcast.91, bf16[8,32,2048]{2,1,0:T(8,128)(2,1)} %get-tuple-element.117.refs_2_, ...), custom_call_target="tpu_custom_call", output_to_operand_aliasing={{0}: (2, {}), {1}: (3, {})} | custom-call | flops 3000000000 | tf_op jit(solution)/shard_map/weight_grad/pallas_call | solution.py:524
  347.8 2.0 collective-permute-start.6
  350.4 11.1 %norm_grad.3 = (f32[512,1024]{1,0:T(8,128)}, bf16[512,1024]{1,0:T(8,128)(2,1)}, f32[1,1024]{1,0:T(1,128)}) custom-call(bf16[3,512,1024]{2,1,0:T(8,128)(2,1)} %self_backward.1.d_ref, bf16[1024,3200]{1,0:T(8,128)(2,1)} %bitcast.89, f32[512,1024]{1,0:T(8,128)} %get-tuple-element.121.unit, f32[512,1]{1,0:T(8,128)} %get-tuple-element.122.inverse, ...), custom_call_target="tpu_custom_call" | custom-call | flops 12000000000 | tf_op jit(solution)/shard_map/norm_grad/pallas_call | solution.py:584
  362.4 0.7 gather_fusion
  363.5 2.9 fusion.9
  366.5 2.9 fusion.8
  369.5 1.4 collective-permute-start.2
  370.9 5.0 fusion
  376.0 4.9 add_convert_fusion
  380.9 3.9 copy.79
  384.8 1.1 collective-permute-start.22
  386.5 1.6 add_convert_fusion.10
  388.1 1.6 collective-permute-start.15
  390.1 1.1 collective-permute-start.11
  391.2 1.6 add_convert_fusion.14
  392.8 1.1 collective-permute-start.7
  393.8 1.6 add_convert_fusion.16
  395.5 49.1 %collective-permute-done.15 = bf16[4,32,2048]{2,1,0:T(8,128)(2,1)S(1)} collective-permute-done((bf16[4,32,2048]{2,1,0:T(8,128)(2,1)S(1)}, bf16[4,32,2048]{2,1,0:T(8,128)(2,1)S(1)}, u32[]{:S(2)}, u32[]{:S(2)}) %collective-permute-start.15) | collective-permute-done | bytes 524320 | tf_op jit(solution)/shard_map/ppermute | solution.py:1001
  444.5 0.9 collective-permute-start.3
  445.6 2.9 collective-permute-start.16
  448.5 6.8 %collective-permute-done.7 = bf16[4,32,2048]{2,1,0:T(8,128)(2,1)S(1)} collective-permute-done((bf16[4,32,2048]{2,1,0:T(8,128)(2,1)S(1)}, bf16[4,32,2048]{2,1,0:T(8,128)(2,1)S(1)}, u32[]{:S(2)}, u32[]{:S(2)}) %collective-permute-start.7) | collective-permute-done | bytes 524320 | tf_op jit(solution)/shard_map/ppermute | solution.py:1001
  455.3 3.1 collective-permute-start.12
  458.6 2.5 collective-permute-start.8
  461.3 4.2 collective-permute-done.12
  465.6 2.1 collective-permute-start.17
  467.7 7.7 %collective-permute-done.8 = bf16[2,32,2048]{2,1,0:T(8,128)(2,1)S(1)} collective-permute-done((bf16[2,32,2048]{2,1,0:T(8,128)(2,1)S(1)}, bf16[2,32,2048]{2,1,0:T(8,128)(2,1)S(1)}, u32[]{:S(2)}, u32[]{:S(2)}) %collective-permute-start.8) | collective-permute-done | bytes 262176 | tf_op jit(solution)/shard_map/ppermute | solution.py:1001
  475.5 4.7 collective-permute-done.4
  480.4 2.8 collective-permute-start.5
  484.0 7.5 %collective-permute-done.13 = bf16[1,32,2048]{2,1,0:T(8,128)(2,1)S(1)} collective-permute-done((bf16[1,32,2048]{2,1,0:T(8,128)(2,1)S(1)}, bf16[1,32,2048]{2,1,0:T(8,128)(2,1)S(1)}, u32[]{:S(2)}, u32[]{:S(2)}) %collective-permute-start.13) | collective-permute-done | bytes 131104 | tf_op jit(solution)/shard_map/ppermute | solution.py:1001
  491.5 1.0 add_convert_fusion.2
  493.1 0.8 add_convert_fusion.4
  493.9 1.5 collective-permute-start.19
  496.9 11.5 %collective-permute-done.23 = bf16[4,128,1024]{2,1,0:T(8,128)(2,1)S(1)} collective-permute-done((bf16[4,128,1024]{2,1,0:T(8,128)(2,1)S(1)}, bf16[4,128,1024]{2,1,0:T(8,128)(2,1)S(1)}, u32[]{:S(2)}, u32[]{:S(2)}) %collective-permute-start.23) | collective-permute-done | bytes 1048608 | tf_op jit(solution)/shard_map/ppermute | solution.py:1001
  509.2 1.3 collective-permute-done.19
  511.3 0.7 fusion.13
  512.0 9.5 %collective-permute-done.24 = bf16[2,128,1024]{2,1,0:T(8,128)(2,1)S(1)} collective-permute-done((bf16[2,128,1024]{2,1,0:T(8,128)(2,1)S(1)}, bf16[2,128,1024]{2,1,0:T(8,128)(2,1)S(1)}, u32[]{:S(2)}, u32[]{:S(2)}) %collective-permute-start.24) | collective-permute-done | bytes 524320 | tf_op jit(solution)/shard_map/ppermute | solution.py:1001
  521.6 2.8 collective-permute-start.25
  524.5 8.2 %collective-permute-done.20 = bf16[2,32,4096]{2,1,0:T(8,128)(2,1)S(1)} collective-permute-done((bf16[2,32,4096]{2,1,0:T(8,128)(2,1)S(1)}, bf16[2,32,4096]{2,1,0:T(8,128)(2,1)S(1)}, u32[]{:S(2)}, u32[]{:S(2)}) %collective-permute-start.20) | collective-permute-done | bytes 524320 | tf_op jit(solution)/shard_map/ppermute | solution.py:1001
  532.8 1.2 collective-permute-start.21
  534.0 0.7 slice_reduce_fusion
  534.7 0.9 add_bitcast_fusion
  535.6 7.3 %collective-permute-done.21 = bf16[1,32,4096]{2,1,0:T(8,128)(2,1)S(1)} collective-permute-done((bf16[1,32,4096]{2,1,0:T(8,128)(2,1)S(1)}, bf16[1,32,4096]{2,1,0:T(8,128)(2,1)S(1)}, u32[]{:S(2)}, u32[]{:S(2)}) %collective-permute-start.21) | collective-permute-done | bytes 262176 | tf_op jit(solution)/shard_map/ppermute | solution.py:1001
  542.9 0.9 add_bitcast_fusion.1
  (120 shorter events, 11.5 us)
Async XLA Ops:
  7.2 182.9 %all-gather.3.cloned.1.call-start = ((), (), s32[]{:S(2)}) async-start(), calls=%async_computation | async-start | bytes 17301504 | tf_op jit(solution)/shard_map/all_gather | solution.py:1060
  9.6 43.7 %copy-start.7 = (bf16[32,4096]{1,0:T(8,128)(2,1)S(1)}, bf16[32,4096]{1,0:T(8,128)(2,1)}, u32[]{:S(2)}) copy-start(bf16[32,4096]{1,0:T(8,128)(2,1)} %param.35) | copy-start | bytes 786436
  9.6 43.9 %copy-start.8 = (bf16[128,1024]{1,0:T(8,128)(2,1)S(1)}, bf16[128,1024]{1,0:T(8,128)(2,1)}, u32[]{:S(2)}) copy-start(bf16[128,1024]{1,0:T(8,128)(2,1)} %param.36) | copy-start | bytes 786436
  53.3 1.8 copy-start.17
  53.4 2.6 copy-start
  56.0 2.2 copy-start.20
  56.0 2.8 copy-start.9
  56.0 2.9 copy-start.10
  56.0 2.9 copy-start.11
  56.0 2.9 copy-start.12
  56.0 2.9 copy-start.13
  59.0 6.6 %copy-start.14 = (bf16[32,5120]{1,0:T(8,128)(2,1)}, bf16[32,5120]{1,0:T(8,128)(2,1)S(1)}, u32[]{:S(2)}) copy-start(bf16[32,5120]{1,0:T(8,128)(2,1)S(1)} %constant_dynamic-update-slice_fusion.x_ref) | copy-start | bytes 983044
  282.6 105.5 %collective-permute-start.10 = (bf16[8,32,2048]{2,1,0:T(8,128)(2,1)}, bf16[8,32,2048]{2,1,0:T(8,128)(2,1)S(1)}, u32[]{:S(2)}, u32[]{:S(2)}) collective-permute-start(bf16[8,32,2048]{2,1,0:T(8,128)(2,1)} %get-tuple-element.105), channel_id=1, source_target_pairs={{0,1},{1,0},{2,3},{3,2},{4,5},{5,4},{6,7},{7,6},{8,9},{9,8},{10,11... | collective-permute-start | bytes 3145736 | tf_op jit(solution)/shard_map/ppermute | solution.py:1001
  297.9 88.0 %collective-permute-start.14 = (bf16[8,32,2048]{2,1,0:T(8,128)(2,1)}, bf16[8,32,2048]{2,1,0:T(8,128)(2,1)}, u32[]{:S(2)}, u32[]{:S(2)}) collective-permute-start(bf16[8,32,2048]{2,1,0:T(8,128)(2,1)} %get-tuple-element.107), channel_id=1, source_target_pairs={{0,2},{1,3},{2,0},{3,1},{4,6},{5,7},{6,4},{7,5},{8,10},{9,11},{10,... | collective-permute-start | bytes 3145736 | tf_op jit(solution)/shard_map/ppermute | solution.py:1001
  347.8 42.3 %collective-permute-start.6 = (bf16[8,32,2048]{2,1,0:T(8,128)(2,1)}, bf16[8,32,2048]{2,1,0:T(8,128)(2,1)}, u32[]{:S(2)}, u32[]{:S(2)}) collective-permute-start(bf16[8,32,2048]{2,1,0:T(8,128)(2,1)} %get-tuple-element.119), channel_id=1, source_target_pairs={{0,1},{1,0},{2,3},{3,2},{4,5},{5,4},{6,7},{7,6},{8,9},{9,8},{10,11... | collective-permute-start | bytes 3145736 | tf_op jit(solution)/shard_map/ppermute | solution.py:1001
  349.7 43.0 %collective-permute-start.1 = (bf16[8,32,2048]{2,1,0:T(8,128)(2,1)}, bf16[8,32,2048]{2,1,0:T(8,128)(2,1)}, u32[]{:S(2)}, u32[]{:S(2)}) collective-permute-start(bf16[8,32,2048]{2,1,0:T(8,128)(2,1)} %get-tuple-element.115), channel_id=1, source_target_pairs={{0,2},{1,3},{2,0},{3,1},{4,6},{5,7},{6,4},{7,5},{8,10},{9,11},{10,... | collective-permute-start | bytes 3145736 | tf_op jit(solution)/shard_map/ppermute | solution.py:1001
  350.4 11.8 %copy-start.16 = (f32[1,1024]{1,0:T(1,128)S(1)}, f32[1,1024]{1,0:T(1,128)}, u32[]{:S(2)}) copy-start(f32[1,1024]{1,0:T(1,128)} %get-tuple-element.127) | copy-start | bytes 12292
  350.4 11.8 %copy-start.15 = (f32[1,1024]{1,0:T(1,128)S(1)}, f32[1,1024]{1,0:T(1,128)}, u32[]{:S(2)}) copy-start(f32[1,1024]{1,0:T(1,128)} %get-tuple-element.128) | copy-start | bytes 12292
  350.4 13.1 %copy-start.21 = (bf16[512,512]{1,0:T(8,128)(2,1)S(1)}, bf16[512,512]{1,0:T(8,128)(2,1)}, u32[]{:S(2)}) copy-start(bf16[512,512]{1,0:T(8,128)(2,1)} %get-tuple-element.77) | copy-start | bytes 1572868
  363.4 5.9 %collective-permute-start = (bf16[16,32,128]{2,1,0:T(8,128)(2,1)S(1)}, bf16[16,32,128]{2,1,0:T(8,128)(2,1)S(1)}, u32[]{:S(2)}, u32[]{:S(2)}) collective-permute-start(bf16[16,32,128]{2,1,0:T(8,128)(2,1)S(1)} %pad_slice_fusion.2), channel_id=1, source_target_pairs={{0,4},{1,5},{2,6},{3,7},{4,0},{5,1},{6,2},{7,3},{8,12},{9,13},{10,... | collective-permute-start | bytes 393224 | tf_op jit(solution)/shard_map/ppermute | solution.py:1001
  369.4 6.5 %slice-start = ((s8[4849664]{0:T(1024)(128)(4,1)}), s8[4194304]{0:T(1024)(128)(4,1)S(1)}, s32[]{:S(2)}) async-start(s8[4849664]{0:T(1024)(128)(4,1)} %bitcast.98), calls=%async_computation.1 | async-start | bytes 8388608
  369.5 6.5 %slice-start.1 = ((s8[4849664]{0:T(1024)(128)(4,1)}), s8[655360]{0:T(1024)(128)(4,1)S(1)}, s32[]{:S(2)}) async-start(s8[4849664]{0:T(1024)(128)(4,1)} %bitcast.98), calls=%async_computation.2 | async-start | bytes 1310720
  369.5 15.3 %collective-permute-start.2 = (bf16[8,32,128]{2,1,0:T(8,128)(2,1)S(1)}, bf16[8,32,128]{2,1,0:T(8,128)(2,1)S(1)}, u32[]{:S(2)}, u32[]{:S(2)}) collective-permute-start(bf16[8,32,128]{2,1,0:T(8,128)(2,1)S(1)} %slice.388), channel_id=1, source_target_pairs={{0,2},{1,3},{2,0},{3,1},{4,6},{5,7},{6,4},{7,5},{8,10},{9,11},{10,... | collective-permute-start | bytes 196616 | tf_op jit(solution)/shard_map/ppermute | solution.py:1001
  376.0 8.8 %copy-start.19 = (bf16[8,128,1024]{2,1,0:T(8,128)(2,1)S(1)}, bf16[8,128,1024]{2,1,0:T(8,128)(2,1)}, u32[]{:S(2)}) copy-start(bf16[8,128,1024]{2,1,0:T(8,128)(2,1)} %get-tuple-element.137) | copy-start | bytes 6291460
  380.9 5.0 copy-start.18
  380.9 5.6 %copy-start.4 = (bf16[8,32,2048]{2,1,0:T(8,128)(2,1)S(1)}, bf16[8,32,2048]{2,1,0:T(8,128)(2,1)}, u32[]{:S(2)}) copy-start(bf16[8,32,2048]{2,1,0:T(8,128)(2,1)} %get-tuple-element.133) | copy-start | bytes 3145732
  384.8 4.9 copy-start.5
  384.8 106.7 %collective-permute-start.22 = (bf16[8,128,1024]{2,1,0:T(8,128)(2,1)S(1)}, bf16[8,128,1024]{2,1,0:T(8,128)(2,1)S(1)}, u32[]{:S(2)}, u32[]{:S(2)}) collective-permute-start(bf16[8,128,1024]{2,1,0:T(8,128)(2,1)S(1)} %copy-done.19), channel_id=1, source_target_pairs={{0,2},{1,3},{2,0},{3,1},{4,6},{5,7},{6,4},{7,5},{8,10},{9,11},{10,... | collective-permute-start | bytes 6291464 | tf_op jit(solution)/shard_map/ppermute | solution.py:1001
  385.9 107.1 %collective-permute-start.18 = (bf16[8,32,4096]{2,1,0:T(8,128)(2,1)S(1)}, bf16[8,32,4096]{2,1,0:T(8,128)(2,1)S(1)}, u32[]{:S(2)}, u32[]{:S(2)}) collective-permute-start(bf16[8,32,4096]{2,1,0:T(8,128)(2,1)S(1)} %copy-done.18), channel_id=1, source_target_pairs={{0,1},{1,0},{2,3},{3,2},{4,5},{5,4},{6,7},{7,6},{8,9},{9,8},{10,11... | collective-permute-start | bytes 6291464 | tf_op jit(solution)/shard_map/ppermute | solution.py:1001
  388.1 3.1 copy-start.6
  388.1 56.4 %collective-permute-start.15 = (bf16[4,32,2048]{2,1,0:T(8,128)(2,1)S(1)}, bf16[4,32,2048]{2,1,0:T(8,128)(2,1)S(1)}, u32[]{:S(2)}, u32[]{:S(2)}) collective-permute-start(bf16[4,32,2048]{2,1,0:T(8,128)(2,1)S(1)} %get-tuple-element.230), channel_id=1, source_target_pairs={{0,1},{1,0},{2,3},{3,2},{4,5},{5,4},{6,7},{7,6},{8,9},{9,8},{10,11... | collective-permute-start | bytes 1572872 | tf_op jit(solution)/shard_map/ppermute | solution.py:1001
  390.1 3.7 copy-start.3
  390.1 55.4 %collective-permute-start.11 = (bf16[4,32,2048]{2,1,0:T(8,128)(2,1)S(1)}, bf16[4,32,2048]{2,1,0:T(8,128)(2,1)S(1)}, u32[]{:S(2)}, u32[]{:S(2)}) collective-permute-start(bf16[4,32,2048]{2,1,0:T(8,128)(2,1)S(1)} %get-tuple-element.232), channel_id=1, source_target_pairs={{0,2},{1,3},{2,0},{3,1},{4,6},{5,7},{6,4},{7,5},{8,10},{9,11},{10,... | collective-permute-start | bytes 1572872 | tf_op jit(solution)/shard_map/ppermute | solution.py:1001
  392.8 62.6 %collective-permute-start.7 = (bf16[4,32,2048]{2,1,0:T(8,128)(2,1)S(1)}, bf16[4,32,2048]{2,1,0:T(8,128)(2,1)S(1)}, u32[]{:S(2)}, u32[]{:S(2)}) collective-permute-start(bf16[4,32,2048]{2,1,0:T(8,128)(2,1)S(1)} %get-tuple-element.234), channel_id=1, source_target_pairs={{0,2},{1,3},{2,0},{3,1},{4,6},{5,7},{6,4},{7,5},{8,10},{9,11},{10,... | collective-permute-start | bytes 1572872 | tf_op jit(solution)/shard_map/ppermute | solution.py:1001
  444.5 14.0 %collective-permute-start.3 = (bf16[4,32,2176]{2,1,0:T(8,128)(2,1)S(1)}, bf16[4,32,2176]{2,1,0:T(8,128)(2,1)S(1)}, u32[]{:S(2)}, u32[]{:S(2)}) collective-permute-start(bf16[4,32,2176]{2,1,0:T(8,128)(2,1)S(1)} %pad_maximum_fusion), channel_id=1, source_target_pairs={{0,1},{1,0},{2,3},{3,2},{4,5},{5,4},{6,7},{7,6},{8,9},{9,8},{10,11... | collective-permute-start | bytes 1671176 | tf_op jit(solution)/shard_map/ppermute | solution.py:1001
  445.6 15.7 %collective-permute-start.16 = (bf16[2,32,2048]{2,1,0:T(8,128)(2,1)S(1)}, bf16[2,32,2048]{2,1,0:T(8,128)(2,1)S(1)}, u32[]{:S(2)}, u32[]{:S(2)}) collective-permute-start(bf16[2,32,2048]{2,1,0:T(8,128)(2,1)S(1)} %get-tuple-element.240), channel_id=1, source_target_pairs={{0,8},{1,9},{2,10},{3,11},{4,12},{5,13},{6,14},{7,15},{8,0},{9,1},... | collective-permute-start | bytes 786440 | tf_op jit(solution)/shard_map/ppermute | solution.py:1001
  455.3 10.2 %collective-permute-start.12 = (bf16[2,32,2048]{2,1,0:T(8,128)(2,1)S(1)}, bf16[2,32,2048]{2,1,0:T(8,128)(2,1)S(1)}, u32[]{:S(2)}, u32[]{:S(2)}) collective-permute-start(bf16[2,32,2048]{2,1,0:T(8,128)(2,1)S(1)} %get-tuple-element.242), channel_id=1, source_target_pairs={{0,8},{1,9},{2,10},{3,11},{4,12},{5,13},{6,14},{7,15},{8,0},{9,1},... | collective-permute-start | bytes 786440 | tf_op jit(solution)/shard_map/ppermute | solution.py:1001
  458.6 16.8 %collective-permute-start.8 = (bf16[2,32,2048]{2,1,0:T(8,128)(2,1)S(1)}, bf16[2,32,2048]{2,1,0:T(8,128)(2,1)S(1)}, u32[]{:S(2)}, u32[]{:S(2)}) collective-permute-start(bf16[2,32,2048]{2,1,0:T(8,128)(2,1)S(1)} %get-tuple-element.244), channel_id=1, source_target_pairs={{0,8},{1,9},{2,10},{3,11},{4,12},{5,13},{6,14},{7,15},{8,0},{9,1},... | collective-permute-start | bytes 786440 | tf_op jit(solution)/shard_map/ppermute | solution.py:1001
  461.2 30.3 %copy-start.2 = (bf16[8,128,1024]{2,1,0:T(8,128)(2,1)S(1)}, bf16[8,128,1024]{2,1,0:T(8,128)(2,1)}, u32[]{:S(2)}) copy-start(bf16[8,128,1024]{2,1,0:T(8,128)(2,1)} %get-tuple-element.136) | copy-start | bytes 6291460
  461.2 18.9 %collective-permute-start.4 = (bf16[2,32,2176]{2,1,0:T(8,128)(2,1)S(1)}, bf16[2,32,2176]{2,1,0:T(8,128)(2,1)S(1)}, u32[]{:S(2)}, u32[]{:S(2)}) collective-permute-start(bf16[2,32,2176]{2,1,0:T(8,128)(2,1)S(1)} %get-tuple-element.238), channel_id=1, source_target_pairs={{0,8},{1,9},{2,10},{3,11},{4,12},{5,13},{6,14},{7,15},{8,0},{9,1},... | collective-permute-start | bytes 835592 | tf_op jit(solution)/shard_map/ppermute | solution.py:1001
  465.6 14.8 %collective-permute-start.17 = (bf16[1,32,2048]{2,1,0:T(8,128)(2,1)S(1)}, bf16[1,32,2048]{2,1,0:T(8,128)(2,1)S(1)}, u32[]{:S(2)}, u32[]{:S(2)}) collective-permute-start(bf16[1,32,2048]{2,1,0:T(8,128)(2,1)S(1)} %add_convert_fusion.31), channel_id=1, source_target_pairs={{0,16},{1,17},{2,18},{3,19},{4,20},{5,21},{6,22},{7,23},{8,24},{9,... | collective-permute-start | bytes 393224 | tf_op jit(solution)/shard_map/ppermute | solution.py:1001
  475.4 16.0 %collective-permute-start.13 = (bf16[1,32,2048]{2,1,0:T(8,128)(2,1)S(1)}, bf16[1,32,2048]{2,1,0:T(8,128)(2,1)S(1)}, u32[]{:S(2)}, u32[]{:S(2)}) collective-permute-start(bf16[1,32,2048]{2,1,0:T(8,128)(2,1)S(1)} %add_convert_fusion.33), channel_id=1, source_target_pairs={{0,16},{1,17},{2,18},{3,19},{4,20},{5,21},{6,22},{7,23},{8,24},{9,... | collective-permute-start | bytes 393224 | tf_op jit(solution)/shard_map/ppermute | solution.py:1001
  480.1 16.0 %collective-permute-start.9 = (bf16[1,32,2048]{2,1,0:T(8,128)(2,1)S(1)}, bf16[1,32,2048]{2,1,0:T(8,128)(2,1)S(1)}, u32[]{:S(2)}, u32[]{:S(2)}) collective-permute-start(bf16[1,32,2048]{2,1,0:T(8,128)(2,1)S(1)} %add_convert_fusion.35), channel_id=1, source_target_pairs={{0,16},{1,17},{2,18},{3,19},{4,20},{5,21},{6,22},{7,23},{8,24},{9,... | collective-permute-start | bytes 393224 | tf_op jit(solution)/shard_map/ppermute | solution.py:1001
  480.4 30.8 %collective-permute-start.5 = (bf16[1,32,2176]{2,1,0:T(8,128)(2,1)S(1)}, bf16[1,32,2176]{2,1,0:T(8,128)(2,1)S(1)}, u32[]{:S(2)}, u32[]{:S(2)}) collective-permute-start(bf16[1,32,2176]{2,1,0:T(8,128)(2,1)S(1)} %add_convert_fusion.29), channel_id=1, source_target_pairs={{0,16},{1,17},{2,18},{3,19},{4,20},{5,21},{6,22},{7,23},{8,24},{9,... | collective-permute-start | bytes 417800 | tf_op jit(solution)/shard_map/ppermute | solution.py:1001
  491.5 1.6 copy-start.1
  492.5 15.9 %collective-permute-start.23 = (bf16[4,128,1024]{2,1,0:T(8,128)(2,1)S(1)}, bf16[4,128,1024]{2,1,0:T(8,128)(2,1)S(1)}, u32[]{:S(2)}, u32[]{:S(2)}) collective-permute-start(bf16[4,128,1024]{2,1,0:T(8,128)(2,1)S(1)} %get-tuple-element.222), channel_id=1, source_target_pairs={{0,1},{1,0},{2,3},{3,2},{4,5},{5,4},{6,7},{7,6},{8,9},{9,8},{10,11... | collective-permute-start | bytes 3145736 | tf_op jit(solution)/shard_map/ppermute | solution.py:1001
  493.9 16.6 %collective-permute-start.19 = (bf16[4,32,4096]{2,1,0:T(8,128)(2,1)S(1)}, bf16[4,32,4096]{2,1,0:T(8,128)(2,1)S(1)}, u32[]{:S(2)}, u32[]{:S(2)}) collective-permute-start(bf16[4,32,4096]{2,1,0:T(8,128)(2,1)S(1)} %get-tuple-element.224), channel_id=1, source_target_pairs={{0,2},{1,3},{2,0},{3,1},{4,6},{5,7},{6,4},{7,5},{8,10},{9,11},{10,... | collective-permute-start | bytes 3145736 | tf_op jit(solution)/shard_map/ppermute | solution.py:1001
  508.8 12.7 %collective-permute-start.24 = (bf16[2,128,1024]{2,1,0:T(8,128)(2,1)S(1)}, bf16[2,128,1024]{2,1,0:T(8,128)(2,1)S(1)}, u32[]{:S(2)}, u32[]{:S(2)}) collective-permute-start(bf16[2,128,1024]{2,1,0:T(8,128)(2,1)S(1)} %get-tuple-element.226), channel_id=1, source_target_pairs={{0,8},{1,9},{2,10},{3,11},{4,12},{5,13},{6,14},{7,15},{8,0},{9,1},... | collective-permute-start | bytes 1572872 | tf_op jit(solution)/shard_map/ppermute | solution.py:1001
  510.7 22.0 %collective-permute-start.20 = (bf16[2,32,4096]{2,1,0:T(8,128)(2,1)S(1)}, bf16[2,32,4096]{2,1,0:T(8,128)(2,1)S(1)}, u32[]{:S(2)}, u32[]{:S(2)}) collective-permute-start(bf16[2,32,4096]{2,1,0:T(8,128)(2,1)S(1)} %get-tuple-element.228), channel_id=1, source_target_pairs={{0,8},{1,9},{2,10},{3,11},{4,12},{5,13},{6,14},{7,15},{8,0},{9,1},... | collective-permute-start | bytes 1572872 | tf_op jit(solution)/shard_map/ppermute | solution.py:1001
  521.6 13.1 %collective-permute-start.25 = (bf16[1,128,1024]{2,1,0:T(8,128)(2,1)S(1)}, bf16[1,128,1024]{2,1,0:T(8,128)(2,1)S(1)}, u32[]{:S(2)}, u32[]{:S(2)}) collective-permute-start(bf16[1,128,1024]{2,1,0:T(8,128)(2,1)S(1)} %add_convert_fusion.19), channel_id=1, source_target_pairs={{0,16},{1,17},{2,18},{3,19},{4,20},{5,21},{6,22},{7,23},{8,24},{9,... | collective-permute-start | bytes 786440 | tf_op jit(solution)/shard_map/ppermute | solution.py:1001
  532.8 10.1 %collective-permute-start.21 = (bf16[1,32,4096]{2,1,0:T(8,128)(2,1)S(1)}, bf16[1,32,4096]{2,1,0:T(8,128)(2,1)S(1)}, u32[]{:S(2)}, u32[]{:S(2)}) collective-permute-start(bf16[1,32,4096]{2,1,0:T(8,128)(2,1)S(1)} %add_convert_fusion.21), channel_id=1, source_target_pairs={{0,16},{1,17},{2,18},{3,19},{4,20},{5,21},{6,22},{7,23},{8,24},{9,... | collective-permute-start | bytes 786440 | tf_op jit(solution)/shard_map/ppermute | solution.py:1001
Sparse Core Ops, SparseCore 0:
  55.3 134.7 all-gather.2
